TPU v7x, 512 devices: a whole 4x8x8 slice. The times are simulated.
512 devices in a mesh: gx: 8 (over y), gy: 8 (over z), gz: 8 (over x, core).
Axes of the slice: x: 4, y: 8, z: 8, core: 2. Of those that a mesh axis runs over, the one named last changes fastest.
Arguments:
- source: float32 [2, 32, 64, 1024], P(None, 'gx', 'gy', 'gz'), may hold values from -6 to 6
- sigma_intra: float32 [3, 32, 64, 1024], P(None, 'gx', 'gy', 'gz'), may hold values from 0.3 to 3
- sigma_extra: float32 [3, 32, 64, 1024], P(None, 'gx', 'gy', 'gz'), may hold values from 0.5 to 3
- membrane: float32 [32, 64, 1024], P('gx', 'gy', 'gz'), may hold values from 0.5 to 5
Outputs:
- solution: float32 [2, 32, 64, 1024], P(None, 'gx', 'gy', 'gz')
- residual: float32 [2, 32, 64, 1024], P(None, 'gx', 'gy', 'gz')
All inputs are finite; a program needn't handle non-finite values.
Results may differ from a plain program's by a relative error of at most 0.0009.
Values sent between devices are 32-bit elements; how exact they have to be, the bound alone decides.
No kernel may reach another device: no remote copies, remote signals or barrier semaphores. Data moves between devices by JAX's collectives and lax.ppermute only.
A program may use at most 64 MiB of HBM per device.

v0:
```python
import jax
import jax.numpy as jnp
from jax import lax
from jax.sharding import Mesh
from jax.sharding import PartitionSpec as P

KRYLOV = 10
GZ = ("gz_0", "gz_1")


highest = lax.Precision.HIGHEST


def with_halo(x, sides, width):
    edges = {}
    for axis, dim in sides:
        size, length = (lax.axis_size(axis), x.shape[dim])
        up = [(i, (i + 1) % size) for i in range(size - 1)]
        last = lax.slice_in_dim(x, length - width, length, axis=dim)
        initial = lax.slice_in_dim(x, 0, width, axis=dim)
        edges[dim] = (
            lax.ppermute(last, axis, up),
            lax.ppermute(initial, axis, [(b, a) for a, b in up]),
        )
    done = []
    for _, dim in sides:
        low, high = edges[dim]
        around = [(width, width) if d in done else (0, 0) for d in range(x.ndim)]
        x = jnp.concatenate([jnp.pad(low, around), x, jnp.pad(high, around)], axis=dim)
        done.append(dim)
    return x


def copy_for_each(x, axis):
    copies = jnp.broadcast_to(x, (lax.axis_size(axis), *x.shape))
    return lax.all_to_all(copies, axis, split_axis=0, concat_axis=0, tiled=True)


def of_everyone(x, axis):
    return copy_for_each(x, axis).sum(axis=0)


def by_axis(x, axes):
    far, near = axes
    return of_everyone(of_everyone(x, near), far)


def packed_total(arrays, axis):
    ravelled, at, done = (jnp.concatenate([a.reshape(-1) for a in arrays]), 0, [])
    so_far = by_axis(ravelled, axis)
    for a in arrays:
        done.append(so_far[at : at + a.size].reshape(a.shape))
        at += a.size
    return tuple(done)


def shifted(padded_grid, spatial, offset):
    pieces = [slice(1, -1), slice(1, -1), slice(1, -1)]
    if offset > 0:
        pieces[spatial] = slice(2, None)
    else:
        pieces[spatial] = slice(None, -2)
    return padded_grid[tuple(pieces)]


def face_terms(padded_sigma):
    upper_faces = []
    lower_faces = []
    for spatial in range(3):
        component = padded_sigma[spatial]
        middle = component[1:-1, 1:-1, 1:-1]
        upper_faces.append(0.5 * (middle + shifted(component, spatial, 1)))
        lower_faces.append(0.5 * (middle + shifted(component, spatial, -1)))
    diagonal = upper_faces[0] + lower_faces[0]
    for spatial in range(1, 3):
        diagonal = diagonal + upper_faces[spatial] + lower_faces[spatial]
    return (upper_faces, lower_faces, diagonal)


def apply_laplace(faces, padded_field):
    upper_faces, lower_faces, diagonal = faces
    result = diagonal * padded_field[1:-1, 1:-1, 1:-1]
    for spatial in range(3):
        result = result - upper_faces[spatial] * shifted(padded_field, spatial, 1)
        result = result - lower_faces[spatial] * shifted(padded_field, spatial, -1)
    return result


def operate(intra_faces, extra_faces, membrane, padded_pair):
    joined = padded_pair[0] + padded_pair[1]
    shared = apply_laplace(intra_faces, joined)
    leading = membrane * padded_pair[0, 1:-1, 1:-1, 1:-1] + shared
    second = shared + apply_laplace(extra_faces, padded_pair[1])
    return jnp.stack([leading, second])


def inverse_blocks(intra_faces, extra_faces, membrane):
    intra_sum = intra_faces[2]
    extra_sum = extra_faces[2]
    determinant = membrane * intra_sum + membrane * extra_sum + intra_sum * extra_sum
    return jnp.stack(
        [
            (intra_sum + extra_sum) / determinant,
            -intra_sum / determinant,
            (membrane + intra_sum) / determinant,
        ]
    )


def precondition(inverse, pair):
    leading = inverse[0] * pair[0] + inverse[1] * pair[1]
    second = inverse[1] * pair[0] + inverse[2] * pair[1]
    return jnp.stack([leading, second])


def least_squares(hessenberg, start_norm):
    krylov = hessenberg.shape[1]
    rotated = hessenberg
    target = jnp.zeros((krylov + 1,), jnp.float32).at[0].set(start_norm)
    for column in range(krylov):
        pivot = rotated[column, column]
        lower_entry = rotated[column + 1, column]
        radius = jnp.sqrt(pivot * pivot + lower_entry * lower_entry)
        cosine = pivot / radius
        sine_value = lower_entry / radius
        row_top = cosine * rotated[column] + sine_value * rotated[column + 1]
        row_below = -sine_value * rotated[column] + cosine * rotated[column + 1]
        rotated = rotated.at[column].set(row_top).at[column + 1].set(row_below)
        leading = cosine * target[column] + sine_value * target[column + 1]
        second = -sine_value * target[column] + cosine * target[column + 1]
        target = target.at[column].set(leading).at[column + 1].set(second)
    coeffs = jnp.zeros((krylov,), jnp.float32)
    for column in range(krylov - 1, -1, -1):
        partial_sum = jnp.sum(rotated[column, column + 1 :] * coeffs[column + 1 :])
        coeffs = coeffs.at[column].set((target[column] - partial_sum) / rotated[column, column])
    return coeffs


def body(source, sigma_intra, sigma_extra, membrane):
    stacked = jnp.concatenate([sigma_intra, sigma_extra], 0)
    padded_sigma = with_halo(stacked, (("gx", 1), ("gy", 2), (GZ, 3)), 1)
    intra_faces = face_terms(padded_sigma[:3])
    extra_faces = face_terms(padded_sigma[3:])
    inverse = inverse_blocks(intra_faces, extra_faces, membrane)
    padded_inverse = with_halo(inverse, (("gx", 1), ("gy", 2), (GZ, 3)), 1)
    start_norm = jnp.sqrt(by_axis(jnp.sum(source * source), (("gx", "gy"), ("gz_0", "gz_1"))))
    basis = jnp.zeros((KRYLOV + 1,) + source.shape, jnp.float32).at[0].set(source / start_norm)
    hessenberg = jnp.zeros((KRYLOV + 1, KRYLOV), jnp.float32)
    for column in range(KRYLOV):
        padded_vector = with_halo(basis[column], (("gx", 1), ("gy", 2), (GZ, 3)), 1)
        padded_solved = precondition(padded_inverse, padded_vector)
        applied = operate(intra_faces, extra_faces, membrane, padded_solved)
        flat_basis = basis[: column + 1].reshape(column + 1, -1)
        local_project = jnp.dot(flat_basis, applied.reshape(-1), precision=highest)
        project, total = packed_total(
            (local_project, jnp.sum(applied * applied)), (("gx", "gy"), ("gz_0", "gz_1"))
        )
        applied = applied - jnp.dot(project, flat_basis, precision=highest).reshape(applied.shape)
        norm_sq = total - jnp.sum(project * project)
        new_norm = jnp.sqrt(norm_sq)
        basis = basis.at[column + 1].set(applied / new_norm)
        hessenberg = (
            hessenberg.at[: column + 1, column].set(project).at[column + 1, column].set(new_norm)
        )
    coeffs = least_squares(hessenberg, start_norm)
    combined = jnp.dot(coeffs, basis[:KRYLOV].reshape(KRYLOV, -1), precision=highest).reshape(
        source.shape
    )
    solution = precondition(inverse, combined)
    remainder = jnp.zeros((KRYLOV + 1,), jnp.float32).at[0].set(start_norm) - jnp.dot(
        hessenberg, coeffs, precision=highest
    )
    residual = jnp.dot(remainder, basis.reshape(KRYLOV + 1, -1), precision=highest).reshape(
        source.shape
    )
    return (solution, residual)


def solution(mesh):
    torus = Mesh(
        mesh.devices.reshape(mesh.shape["gx"], mesh.shape["gy"], 4, 2), ("gx", "gy", "gz_0", "gz_1")
    )
    return jax.shard_map(
        body,
        mesh=torus,
        in_specs=(
            P(None, "gx", "gy", GZ),
            P(None, "gx", "gy", GZ),
            P(None, "gx", "gy", GZ),
            P("gx", "gy", GZ),
        ),
        out_specs=(P(None, "gx", "gy", GZ), P(None, "gx", "gy", GZ)),
        check_vma=False,
    )
```

profile of v0, /device:TPU:1, one launch (start us, length us, event | category | flops | bytes accessed | tf_op | source)
XLA Modules:
  0.0 710.9 jit_solution(4066487713449410849)
XLA Ops:
  30.7 17.8 %all-to-all-start.1 = ((f32[64,1,1]{2,1,0:T(1,128)}), f32[64,1,1]{2,1,0:T(1,128)S(1)}, u32[]{:S(2)}, u32[]{:S(2)}) async-start(f32[64,1,1]{2,1,0:T(1,128)} %broadcast_in_dim.69), calls=%async_computation.1 | async-start | bytes 65536 | tf_op jit(solution)/shard_map/all_to_all | solution.py:36
  49.3 10.1 %all-to-all-done.1 = f32[64,1,1]{2,1,0:T(1,128)S(1)} async-done(((f32[64,1,1]{2,1,0:T(1,128)}), f32[64,1,1]{2,1,0:T(1,128)S(1)}, u32[]{:S(2)}, u32[]{:S(2)}) %all-to-all-start.1) | async-done | bytes 288 | tf_op jit(solution)/shard_map/all_to_all | solution.py:36
  114.1 9.1 %all-to-all-start.3 = ((f32[64,1,2]{2,1,0:T(1,128)}), f32[64,1,2]{2,1,0:T(1,128)S(1)}, u32[]{:S(2)}, u32[]{:S(2)}) async-start(f32[64,1,2]{2,1,0:T(1,128)} %broadcast_in_dim.71), calls=%async_computation.3 | async-start | bytes 65536 | tf_op jit(solution)/shard_map/all_to_all | solution.py:36
  123.3 10.7 %all-to-all-done.3 = f32[64,1,2]{2,1,0:T(1,128)S(1)} async-done(((f32[64,1,2]{2,1,0:T(1,128)}), f32[64,1,2]{2,1,0:T(1,128)S(1)}, u32[]{:S(2)}, u32[]{:S(2)}) %all-to-all-start.3) | async-done | bytes 544 | tf_op jit(solution)/shard_map/all_to_all | solution.py:36
  167.6 7.2 %all-to-all-start.5 = ((f32[64,1,3]{2,1,0:T(1,128)}), f32[64,1,3]{2,1,0:T(1,128)S(1)}, u32[]{:S(2)}, u32[]{:S(2)}) async-start(f32[64,1,3]{2,1,0:T(1,128)} %broadcast_in_dim.73), calls=%async_computation.5 | async-start | bytes 65536 | tf_op jit(solution)/shard_map/all_to_all | solution.py:36
  175.0 10.7 %all-to-all-done.5 = f32[64,1,3]{2,1,0:T(1,128)S(1)} async-done(((f32[64,1,3]{2,1,0:T(1,128)}), f32[64,1,3]{2,1,0:T(1,128)S(1)}, u32[]{:S(2)}, u32[]{:S(2)}) %all-to-all-start.5) | async-done | bytes 800 | tf_op jit(solution)/shard_map/all_to_all | solution.py:36
  208.1 5.7 all-to-all-start.6
  219.0 7.2 %all-to-all-start.7 = ((f32[64,1,4]{2,1,0:T(1,128)}), f32[64,1,4]{2,1,0:T(1,128)S(1)}, u32[]{:S(2)}, u32[]{:S(2)}) async-start(f32[64,1,4]{2,1,0:T(1,128)} %broadcast_in_dim.75), calls=%async_computation.7 | async-start | bytes 65536 | tf_op jit(solution)/shard_map/all_to_all | solution.py:36
  227.0 10.1 %all-to-all-done.7 = f32[64,1,4]{2,1,0:T(1,128)S(1)} async-done(((f32[64,1,4]{2,1,0:T(1,128)}), f32[64,1,4]{2,1,0:T(1,128)S(1)}, u32[]{:S(2)}, u32[]{:S(2)}) %all-to-all-start.7) | async-done | bytes 1056 | tf_op jit(solution)/shard_map/all_to_all | solution.py:36
  270.5 7.2 %all-to-all-start.9 = ((f32[64,1,5]{2,1,0:T(1,128)}), f32[64,1,5]{2,1,0:T(1,128)S(1)}, u32[]{:S(2)}, u32[]{:S(2)}) async-start(f32[64,1,5]{2,1,0:T(1,128)} %broadcast_in_dim.77), calls=%async_computation.9 | async-start | bytes 65536 | tf_op jit(solution)/shard_map/all_to_all | solution.py:36
  277.8 10.7 %all-to-all-done.9 = f32[64,1,5]{2,1,0:T(1,128)S(1)} async-done(((f32[64,1,5]{2,1,0:T(1,128)}), f32[64,1,5]{2,1,0:T(1,128)S(1)}, u32[]{:S(2)}, u32[]{:S(2)}) %all-to-all-start.9) | async-done | bytes 1312 | tf_op jit(solution)/shard_map/all_to_all | solution.py:36
  321.9 7.2 %all-to-all-start.11 = ((f32[64,1,6]{2,1,0:T(1,128)}), f32[64,1,6]{2,1,0:T(1,128)S(1)}, u32[]{:S(2)}, u32[]{:S(2)}) async-start(f32[64,1,6]{2,1,0:T(1,128)} %broadcast_in_dim.79), calls=%async_computation.11 | async-start | bytes 65536 | tf_op jit(solution)/shard_map/all_to_all | solution.py:36
  329.9 10.0 %all-to-all-done.11 = f32[64,1,6]{2,1,0:T(1,128)S(1)} async-done(((f32[64,1,6]{2,1,0:T(1,128)}), f32[64,1,6]{2,1,0:T(1,128)S(1)}, u32[]{:S(2)}, u32[]{:S(2)}) %all-to-all-start.11) | async-done | bytes 1568 | tf_op jit(solution)/shard_map/all_to_all | solution.py:36
  362.3 5.7 all-to-all-start.12
  373.2 7.2 %all-to-all-start.13 = ((f32[64,1,7]{2,1,0:T(1,128)}), f32[64,1,7]{2,1,0:T(1,128)S(1)}, u32[]{:S(2)}, u32[]{:S(2)}) async-start(f32[64,1,7]{2,1,0:T(1,128)} %broadcast_in_dim.81), calls=%async_computation.13 | async-start | bytes 65536 | tf_op jit(solution)/shard_map/all_to_all | solution.py:36
  380.6 10.7 %all-to-all-done.13 = f32[64,1,7]{2,1,0:T(1,128)S(1)} async-done(((f32[64,1,7]{2,1,0:T(1,128)}), f32[64,1,7]{2,1,0:T(1,128)S(1)}, u32[]{:S(2)}, u32[]{:S(2)}) %all-to-all-start.13) | async-done | bytes 1824 | tf_op jit(solution)/shard_map/all_to_all | solution.py:36
  424.0 8.8 %all-to-all-start.15 = ((f32[64,1,8]{2,1,0:T(1,128)}), f32[64,1,8]{2,1,0:T(1,128)S(1)}, u32[]{:S(2)}, u32[]{:S(2)}) async-start(f32[64,1,8]{2,1,0:T(1,128)} %broadcast_in_dim.83), calls=%async_computation.15 | async-start | bytes 65536 | tf_op jit(solution)/shard_map/all_to_all | solution.py:36
  436.5 7.1 all-to-all-done.15
  478.4 10.2 %all-to-all-start.17 = ((f32[64,1,9]{2,1,0:T(1,128)}), f32[64,1,9]{2,1,0:T(1,128)S(1)}, u32[]{:S(2)}, u32[]{:S(2)}) async-start(f32[64,1,9]{2,1,0:T(1,128)} %broadcast_in_dim.85), calls=%async_computation.17 | async-start | bytes 65536 | tf_op jit(solution)/shard_map/all_to_all | solution.py:36
  492.2 7.1 all-to-all-done.17
  534.5 10.1 %all-to-all-start.19 = ((f32[64,1,10]{2,1,0:T(1,128)}), f32[64,1,10]{2,1,0:T(1,128)S(1)}, u32[]{:S(2)}, u32[]{:S(2)}) async-start(f32[64,1,10]{2,1,0:T(1,128)} %broadcast_in_dim.87), calls=%async_computation.19 | async-start | bytes 65536 | tf_op jit(solution)/shard_map/all_to_all | solution.py:36
  544.6 10.8 %all-to-all-done.19 = f32[64,1,10]{2,1,0:T(1,128)S(1)} async-done(((f32[64,1,10]{2,1,0:T(1,128)}), f32[64,1,10]{2,1,0:T(1,128)S(1)}, u32[]{:S(2)}, u32[]{:S(2)}) %all-to-all-start.19) | async-done | bytes 2592 | tf_op jit(solution)/shard_map/all_to_all | solution.py:36
  591.0 8.8 %all-to-all-start.21 = ((f32[64,1,11]{2,1,0:T(1,128)}), f32[64,1,11]{2,1,0:T(1,128)S(1)}, u32[]{:S(2)}, u32[]{:S(2)}) async-start(f32[64,1,11]{2,1,0:T(1,128)} %broadcast_in_dim.89), calls=%async_computation.21 | async-start | bytes 65536 | tf_op jit(solution)/shard_map/all_to_all | solution.py:36
  603.4 7.1 all-to-all-done.21
  (557 shorter events, 410.5 us)
Async XLA Ops:
  1.6 59.2 %collective-permute-start = (f32[6,4,8,1]{3,2,1,0:T(8,128)S(1)}, f32[6,4,8,1]{3,2,1,0:T(8,128)S(1)}, u32[]{:S(2)}, u32[]{:S(2)}) collective-permute-start(f32[6,4,8,1]{3,2,1,0:T(8,128)S(1)} %get-tuple-element.1087), channel_id=1, source_target_pairs={{0,1},{1,2},{2,3},{3,4},{4,5},{5,6},{6,7},{8,9},{9,10},{10,11},{11... | collective-permute-start | bytes 2312 | tf_op jit(solution)/shard_map/ppermute | solution.py:22
  6.1 56.1 %collective-permute-start.5 = (f32[6,4,8,1]{3,2,1,0:T(8,128)S(1)}, f32[6,4,8,1]{3,2,1,0:T(8,128)S(1)}, u32[]{:S(2)}, u32[]{:S(2)}) collective-permute-start(f32[6,4,8,1]{3,2,1,0:T(8,128)S(1)} %get-tuple-element.1088), channel_id=1, source_target_pairs={{1,0},{2,1},{3,2},{4,3},{5,4},{6,5},{7,6},{9,8},{10,9},{11,10},{12... | collective-permute-start | bytes 2312 | tf_op jit(solution)/shard_map/ppermute | solution.py:23
  11.6 59.7 %collective-permute-start.2 = (f32[6,1,8,128]{3,2,1,0:T(8,128)S(1)}, f32[6,1,8,128]{3,2,1,0:T(8,128)S(1)}, u32[]{:S(2)}, u32[]{:S(2)}) collective-permute-start(f32[6,1,8,128]{3,2,1,0:T(8,128)S(1)} %get-tuple-element.1085), channel_id=1, source_target_pairs={{0,64},{64,128},{128,192},{192,256},{256,320},{320,384},{384,448},... | collective-permute-start | bytes 73736 | tf_op jit(solution)/shard_map/ppermute | solution.py:22
  12.9 59.7 %collective-permute-start.3 = (f32[6,1,8,128]{3,2,1,0:T(8,128)S(1)}, f32[6,1,8,128]{3,2,1,0:T(8,128)S(1)}, u32[]{:S(2)}, u32[]{:S(2)}) collective-permute-start(f32[6,1,8,128]{3,2,1,0:T(8,128)S(1)} %get-tuple-element.1086), channel_id=1, source_target_pairs={{64,0},{128,64},{192,128},{256,192},{320,256},{384,320},{448,384},... | collective-permute-start | bytes 73736 | tf_op jit(solution)/shard_map/ppermute | solution.py:23
  14.3 52.8 %collective-permute-start.1 = (f32[6,4,1,128]{3,2,1,0:T(1,128)S(1)}, f32[6,4,1,128]{3,2,1,0:T(1,128)S(1)}, u32[]{:S(2)}, u32[]{:S(2)}) collective-permute-start(f32[6,4,1,128]{3,2,1,0:T(1,128)S(1)} %get-tuple-element.1089), channel_id=1, source_target_pairs={{0,8},{8,16},{16,24},{24,32},{32,40},{40,48},{48,56},{1,9},{9,17},... | collective-permute-start | bytes 36872 | tf_op jit(solution)/shard_map/ppermute | solution.py:22
  30.7 28.6 %all-to-all-start.1 = ((f32[64,1,1]{2,1,0:T(1,128)}), f32[64,1,1]{2,1,0:T(1,128)S(1)}, u32[]{:S(2)}, u32[]{:S(2)}) async-start(f32[64,1,1]{2,1,0:T(1,128)} %broadcast_in_dim.69), calls=%async_computation.1 | async-start | bytes 65536 | tf_op jit(solution)/shard_map/all_to_all | solution.py:36
  62.1 16.1 %collective-permute-start.12 = (f32[2,4,8,1]{3,2,1,0:T(8,128)S(1)}, f32[2,4,8,1]{3,2,1,0:T(8,128)S(1)}, u32[]{:S(2)}, u32[]{:S(2)}) collective-permute-start(f32[2,4,8,1]{3,2,1,0:T(8,128)S(1)} %get-tuple-element.1173), channel_id=1, source_target_pairs={{0,1},{1,2},{2,3},{3,4},{4,5},{5,6},{6,7},{8,9},{9,10},{10,11},{11... | collective-permute-start | bytes 776 | tf_op jit(solution)/shard_map/ppermute | solution.py:22
  69.0 18.5 %collective-permute-start.14 = (f32[2,1,8,128]{3,2,1,0:T(8,128)S(1)}, f32[2,1,8,128]{3,2,1,0:T(8,128)S(1)}, u32[]{:S(2)}, u32[]{:S(2)}) collective-permute-start(f32[2,1,8,128]{3,2,1,0:T(8,128)S(1)} %get-tuple-element.1171), channel_id=1, source_target_pairs={{0,64},{64,128},{128,192},{192,256},{256,320},{320,384},{384,448},... | collective-permute-start | bytes 24584 | tf_op jit(solution)/shard_map/ppermute | solution.py:22
  71.3 21.0 %collective-permute-start.15 = (f32[2,1,8,128]{3,2,1,0:T(8,128)S(1)}, f32[2,1,8,128]{3,2,1,0:T(8,128)S(1)}, u32[]{:S(2)}, u32[]{:S(2)}) collective-permute-start(f32[2,1,8,128]{3,2,1,0:T(8,128)S(1)} %get-tuple-element.1172), channel_id=1, source_target_pairs={{64,0},{128,64},{192,128},{256,192},{320,256},{384,320},{448,384},... | collective-permute-start | bytes 24584 | tf_op jit(solution)/shard_map/ppermute | solution.py:23
  79.6 18.4 %collective-permute-start.10 = (f32[3,4,1,128]{3,2,1,0:T(1,128)S(1)}, f32[3,4,1,128]{3,2,1,0:T(1,128)S(1)}, u32[]{:S(2)}, u32[]{:S(2)}) collective-permute-start(f32[3,4,1,128]{3,2,1,0:T(1,128)S(1)} %get-tuple-element.1098), channel_id=1, source_target_pairs={{8,0},{16,8},{24,16},{32,24},{40,32},{48,40},{56,48},{9,1},{17,9},... | collective-permute-start | bytes 18440 | tf_op jit(solution)/shard_map/ppermute | solution.py:23
  80.9 15.6 %collective-permute-start.11 = (f32[3,4,8,1]{3,2,1,0:T(8,128)S(1)}, f32[3,4,8,1]{3,2,1,0:T(8,128)S(1)}, u32[]{:S(2)}, u32[]{:S(2)}) collective-permute-start(f32[3,4,8,1]{3,2,1,0:T(8,128)S(1)} %get-tuple-element.1096), channel_id=1, source_target_pairs={{1,0},{2,1},{3,2},{4,3},{5,4},{6,5},{7,6},{9,8},{10,9},{11,10},{12... | collective-permute-start | bytes 1160 | tf_op jit(solution)/shard_map/ppermute | solution.py:23
  114.1 19.9 %all-to-all-start.3 = ((f32[64,1,2]{2,1,0:T(1,128)}), f32[64,1,2]{2,1,0:T(1,128)S(1)}, u32[]{:S(2)}, u32[]{:S(2)}) async-start(f32[64,1,2]{2,1,0:T(1,128)} %broadcast_in_dim.71), calls=%async_computation.3 | async-start | bytes 65536 | tf_op jit(solution)/shard_map/all_to_all | solution.py:36
  167.6 18.1 %all-to-all-start.5 = ((f32[64,1,3]{2,1,0:T(1,128)}), f32[64,1,3]{2,1,0:T(1,128)S(1)}, u32[]{:S(2)}, u32[]{:S(2)}) async-start(f32[64,1,3]{2,1,0:T(1,128)} %broadcast_in_dim.73), calls=%async_computation.5 | async-start | bytes 65536 | tf_op jit(solution)/shard_map/all_to_all | solution.py:36
  219.0 18.1 %all-to-all-start.7 = ((f32[64,1,4]{2,1,0:T(1,128)}), f32[64,1,4]{2,1,0:T(1,128)S(1)}, u32[]{:S(2)}, u32[]{:S(2)}) async-start(f32[64,1,4]{2,1,0:T(1,128)} %broadcast_in_dim.75), calls=%async_computation.7 | async-start | bytes 65536 | tf_op jit(solution)/shard_map/all_to_all | solution.py:36
  270.5 18.1 %all-to-all-start.9 = ((f32[64,1,5]{2,1,0:T(1,128)}), f32[64,1,5]{2,1,0:T(1,128)S(1)}, u32[]{:S(2)}, u32[]{:S(2)}) async-start(f32[64,1,5]{2,1,0:T(1,128)} %broadcast_in_dim.77), calls=%async_computation.9 | async-start | bytes 65536 | tf_op jit(solution)/shard_map/all_to_all | solution.py:36
  321.9 18.1 %all-to-all-start.11 = ((f32[64,1,6]{2,1,0:T(1,128)}), f32[64,1,6]{2,1,0:T(1,128)S(1)}, u32[]{:S(2)}, u32[]{:S(2)}) async-start(f32[64,1,6]{2,1,0:T(1,128)} %broadcast_in_dim.79), calls=%async_computation.11 | async-start | bytes 65536 | tf_op jit(solution)/shard_map/all_to_all | solution.py:36
  373.2 18.1 %all-to-all-start.13 = ((f32[64,1,7]{2,1,0:T(1,128)}), f32[64,1,7]{2,1,0:T(1,128)S(1)}, u32[]{:S(2)}, u32[]{:S(2)}) async-start(f32[64,1,7]{2,1,0:T(1,128)} %broadcast_in_dim.81), calls=%async_computation.13 | async-start | bytes 65536 | tf_op jit(solution)/shard_map/all_to_all | solution.py:36
  424.0 19.6 %all-to-all-start.15 = ((f32[64,1,8]{2,1,0:T(1,128)}), f32[64,1,8]{2,1,0:T(1,128)S(1)}, u32[]{:S(2)}, u32[]{:S(2)}) async-start(f32[64,1,8]{2,1,0:T(1,128)} %broadcast_in_dim.83), calls=%async_computation.15 | async-start | bytes 65536 | tf_op jit(solution)/shard_map/all_to_all | solution.py:36
  451.1 15.6 %collective-permute-start.56 = (f32[2,1,8,128]{3,2,1,0:T(8,128)S(1)}, f32[2,1,8,128]{3,2,1,0:T(8,128)S(1)}, u32[]{:S(2)}, u32[]{:S(2)}) collective-permute-start(f32[2,1,8,128]{3,2,1,0:T(8,128)S(1)} %get-tuple-element.1117), channel_id=1, source_target_pairs={{0,64},{64,128},{128,192},{192,256},{256,320},{320,384},{384,448},... | collective-permute-start | bytes 24584 | tf_op jit(solution)/shard_map/ppermute | solution.py:22
  478.4 21.0 %all-to-all-start.17 = ((f32[64,1,9]{2,1,0:T(1,128)}), f32[64,1,9]{2,1,0:T(1,128)S(1)}, u32[]{:S(2)}, u32[]{:S(2)}) async-start(f32[64,1,9]{2,1,0:T(1,128)} %broadcast_in_dim.85), calls=%async_computation.17 | async-start | bytes 65536 | tf_op jit(solution)/shard_map/all_to_all | solution.py:36
  506.6 15.7 %collective-permute-start.62 = (f32[2,1,8,128]{3,2,1,0:T(8,128)S(1)}, f32[2,1,8,128]{3,2,1,0:T(8,128)S(1)}, u32[]{:S(2)}, u32[]{:S(2)}) collective-permute-start(f32[2,1,8,128]{3,2,1,0:T(8,128)S(1)} %get-tuple-element.1109), channel_id=1, source_target_pairs={{0,64},{64,128},{128,192},{192,256},{256,320},{320,384},{384,448},... | collective-permute-start | bytes 24584 | tf_op jit(solution)/shard_map/ppermute | solution.py:22
  534.5 20.9 %all-to-all-start.19 = ((f32[64,1,10]{2,1,0:T(1,128)}), f32[64,1,10]{2,1,0:T(1,128)S(1)}, u32[]{:S(2)}, u32[]{:S(2)}) async-start(f32[64,1,10]{2,1,0:T(1,128)} %broadcast_in_dim.87), calls=%async_computation.19 | async-start | bytes 65536 | tf_op jit(solution)/shard_map/all_to_all | solution.py:36
  563.0 15.8 %collective-permute-start.68 = (f32[2,1,8,128]{3,2,1,0:T(8,128)S(1)}, f32[2,1,8,128]{3,2,1,0:T(8,128)S(1)}, u32[]{:S(2)}, u32[]{:S(2)}) collective-permute-start(f32[2,1,8,128]{3,2,1,0:T(8,128)S(1)} %get-tuple-element.1101), channel_id=1, source_target_pairs={{0,64},{64,128},{128,192},{192,256},{256,320},{320,384},{384,448},... | collective-permute-start | bytes 24584 | tf_op jit(solution)/shard_map/ppermute | solution.py:22
  591.0 19.6 %all-to-all-start.21 = ((f32[64,1,11]{2,1,0:T(1,128)}), f32[64,1,11]{2,1,0:T(1,128)S(1)}, u32[]{:S(2)}, u32[]{:S(2)}) async-start(f32[64,1,11]{2,1,0:T(1,128)} %broadcast_in_dim.89), calls=%async_computation.21 | async-start | bytes 65536 | tf_op jit(solution)/shard_map/all_to_all | solution.py:36
  (81 other events, 671.7 us)
where the time goes:
time: 724 us; the launch traced here: 711 us
  starting transfers between devices  324 us (45%)
  waiting for transfers between devices  169 us (23%)
  between operations  83 us (11%)
  local copies, waits for them, and re-layouts  64 us (9%)
  other arithmetic  59.3 us (8%)
  matrix products  11.6 us (2%)
    all_to_all x22, starting transfers between devices, copy_for_each(): return lax.all_to_all(copies, axis, split_axis=0, concat_axis=0, tiled=True)  154 us
    all_to_all x22, waiting for transfers between devices, copy_for_each(): return lax.all_to_all(copies, axis, split_axis=0, concat_axis=0, tiled=True)  141 us
    ppermute x36, starting transfers between devices, with_halo(): lax.ppermute(last, axis, up)  111 us
    ppermute x36, starting transfers between devices, with_halo(): lax.ppermute(initial, axis, [(b, a) for a, b in up])  57.8 us
    ppermute x36, waiting for transfers between devices, with_halo(): lax.ppermute(initial, axis, [(b, a) for a, b in up])  28.6 us
    another operation x26, other arithmetic  23.6 us
    scatter x20, local copies, waits for them, and re-layouts, body(): hessenberg.at[:column + 1, column].set(project).at[column + 1, column]  15.1 us
    broadcast_in_dim x22, local copies, waits for them, and re-layouts, copy_for_each(): copies = jnp.broadcast_to(x, (lax.axis_size(axis), *x.shape))  14.9 us
  transfers between devices with their start and end apart: 94, of which 31 were waited for; matrix products, arithmetic and copies ran while one was open for 7% of the time, Pallas kernels for 0%

commit v1 on v0

v1 whole, which is shorter than its diff:
```python
import jax
import jax.numpy as jnp
from jax import lax
from jax.experimental import pallas as pl
from jax.experimental.pallas import tpu as pltpu
from jax.sharding import PartitionSpec as P

KRYLOV = 10
DEPTH = KRYLOV + 1
FINE = 16
EXT = FINE + 2 * DEPTH
FIELDS = 9
SLOT = KRYLOV + 2
ROWS = 40
f32 = jnp.float32


def lanes():
    return lax.broadcasted_iota(jnp.int32, (8, 128), 1)


def sublanes(rows=8):
    return lax.broadcasted_iota(jnp.int32, (rows, 128), 0)


def turn(v, by):
    return pltpu.roll(v, by % 128, 1)


def sink(v, by):
    return pltpu.roll(v, by % 8, 0)


def two_sum(a, b):
    s = a + b
    z = s - a
    return s, (a - (s - z)) + (b - z)


def quick_sum(a, b):
    s = a + b
    return s, b - (s - a)


def split(a):
    c = a * 4097.0
    high = c - (c - a)
    return high, a - high


def two_prod(a, b):
    p = a * b
    ah, al = split(a)
    bh, bl = split(b)
    return p, ((ah * bh - p) + ah * bl + al * bh) + al * bl


def dd_add(a, b):
    s, e = two_sum(a[0], b[0])
    t, g = two_sum(a[1], b[1])
    s, e = quick_sum(s, e + t)
    return quick_sum(s, e + g)


def dd_mul(a, b):
    p, e = two_prod(a[0], b[0])
    return quick_sum(p, e + (a[0] * b[1] + a[1] * b[0]))


def dd_neg(a):
    return (-a[0], -a[1])


def dd_inverse(a):
    x = 1.0 / a[0]
    for _ in range(2):
        p = dd_mul(a, (x, jnp.zeros_like(x))) if not isinstance(x, tuple) else dd_mul(a, x)
        r = dd_add((jnp.ones_like(p[0]), jnp.zeros_like(p[0])), dd_neg(p))
        full = x if isinstance(x, tuple) else (x, jnp.zeros_like(x))
        x = dd_add(full, dd_mul(full, r))
    return x


def dd_fold(a):
    for by in (4, 2, 1):
        a = dd_add(a, (sink(a[0], by), sink(a[1], by)))
    return a


def dd_total(pairs):
    pairs = list(pairs)
    while len(pairs) > 1:
        pairs = [
            dd_add(pairs[i], pairs[i + 1]) if i + 1 < len(pairs) else pairs[i]
            for i in range(0, len(pairs), 2)
        ]
    return pairs[0]


def swap_blocks(v, width):
    v = list(v)
    block = lanes() // width
    d = len(v) // 2
    while d >= 1:
        low = (block & d) == 0
        for k in range(len(v)):
            if k & d == 0:
                a, b = v[k], v[k + d]
                v[k] = jnp.where(low, a, turn(b, width * d))
                v[k + d] = jnp.where(low, turn(a, -width * d), b)
        d //= 2
    return v


def pack_kernel(source, intra, extra, membrane, out, rows):
    pieces = [(intra, i) for i in range(3)] + [(extra, i) for i in range(3)]
    pieces += [(source, i) for i in range(2)]
    for f, (ref, i) in enumerate(pieces):
        for x in range(4):
            rows[pl.ds(f * 32 + x, 8, stride=4), :] = ref[i, x]
    for x in range(4):
        rows[pl.ds(256 + x, 8, stride=4), :] = membrane[x]
    rows[pl.ds(288, 96), :] = jnp.zeros((96, 128), f32)
    halves = []
    for half in (0, 16):
        halves.append(
            jnp.concatenate([rows[pl.ds(f * 32 + half, 16), :] for f in range(8)], 0).T
        )
    last = rows[pl.ds(256, 128), :].T
    near = lanes() < 32
    for j in range(8):
        at = j * ROWS
        out[pl.ds(at, 16), :] = halves[0][16 * j : 16 * j + 16]
        out[pl.ds(at + 16, 8), :] = jnp.where(
            near, last[16 * j : 16 * j + 8], turn(last[16 * j + 8 : 16 * j + 16], 32)
        )
        out[pl.ds(at + 24, 16), :] = halves[1][16 * j : 16 * j + 16]


def plane_kernel(main, above, below, above2, below2, out, first, final):
    lane = lanes()
    quarter = lane // 32
    early = (lane % 32) < 16

    def take(ref, row, height):
        return ref[pl.ds(row, 8, stride=height), :]

    for z in range(FINE):
        v = [
            take(main, z, ROWS),
            take(main, 24 + z, ROWS),
            take(above, z, ROWS),
            take(above, 24 + z, ROWS),
            take(above2, z, 24),
            take(below2, 8 + z, 24),
            take(below, z, ROWS),
            take(below, 24 + z, ROWS),
        ]
        v = swap_blocks(v, 16)
        r, shift = z % 8, 32 * (z // 8)
        outer = jnp.where(early, take(above2, 16 + r, 24), take(below2, r, 24))
        m = turn(take(below, 16 + r, ROWS), 96 - shift)
        m = jnp.where(quarter == 2, turn(outer, 64 - shift), m)
        m = jnp.where(quarter == 1, turn(take(above, 16 + r, ROWS), 32 - shift), m)
        m = jnp.where(quarter == 0, turn(take(main, 16 + r, ROWS), -shift), m)
        for f, value in enumerate(v + [m]):
            out[f, z] = value
            if z < DEPTH:
                first[f, z] = value
            if z >= FINE - DEPTH:
                final[f, z - (FINE - DEPTH)] = value


def x_up(v):
    return jnp.where(lanes() % 4 < 3, turn(v, -1), turn(sink(v, -1), 3))


def x_down(v):
    return jnp.where(lanes() % 4 > 0, turn(v, 1), turn(sink(v, 1), -3))


def y_up(v):
    return turn(v, -4)


def y_down(v):
    return turn(v, 4)


def cycle_kernel(
    main, low, high, sums, fields, images, ext, face, inv, ta, tb, tc, qp, cbuf, gram, parts, acc
):
    for f in range(FIELDS):
        ext[f, pl.ds(0, DEPTH)] = low[f]
        ext[f, pl.ds(DEPTH, FINE)] = main[f]
        ext[f, pl.ds(DEPTH + FINE, DEPTH)] = high[f]

    lane = lanes()
    ix = sublanes() * 4 + lane % 4
    last_x, first_x = ix == 31, ix == 0

    def faces_z(i, _):
        for s in range(2):
            face[s * 3 + 2, i] = 0.5 * (ext[s * 3 + 2, i] + ext[s * 3 + 2, i + 1])
        return _

    lax.fori_loop(0, EXT - 1, faces_z, 0)

    def coefficients(i, _):
        diagonals = []
        for s in range(2):
            sx, sy = ext[s * 3, i], ext[s * 3 + 1, i]
            up_x = 0.5 * (sx + jnp.where(last_x, 0.0, x_up(sx)))
            low_x = 0.5 * (sx + jnp.where(first_x, 0.0, x_down(sx)))
            up_y = 0.5 * (sy + y_up(sy))
            low_y = 0.5 * (sy + y_down(sy))
            up_z, low_z = face[s * 3 + 2, i], face[s * 3 + 2, i - 1]
            face[s * 3, i] = jnp.where(last_x, 0.0, up_x)
            face[s * 3 + 1, i] = up_y
            diagonals.append(up_x + low_x + up_y + low_y + up_z + low_z)
        di, de = diagonals
        m = ext[8, i]
        det = m * di + m * de + di * de
        inside = m > 0.0
        scale = jnp.where(inside, 1.0 / jnp.where(inside, det, 1.0), 0.0)
        inv[0, i] = de * scale
        inv[1, i] = m * scale
        inv[2, i] = -di * scale
        inv[3, i] = (m + di) * scale
        ta[0, i] = ext[6, i]
        ta[1, i] = ext[7, i]
        return _

    lax.fori_loop(1, EXT - 1, coefficients, 0, unroll=2)

    block = lane // 32

    def compact(read):
        got = []
        for g in range(FINE // 4):
            value = turn(read(4 * g + 3), 96)
            for j in (2, 1):
                value = jnp.where(block == j, turn(read(4 * g + j), 32 * j), value)
            got.append(jnp.where(block == 0, read(4 * g), value))
        return got

    def remember(r, part, values):
        for g, value in enumerate(values):
            at = part * 4 + g
            images[r, at] = value
            high_part, low_part = split(value)
            gram[0, r, at] = high_part
            gram[1, r, at] = low_part

    for part in range(2):
        remember(0, part, compact(lambda z: main[6 + part, z]))

    buffers = (ta, tb, tc)
    for k in range(KRYLOV):
        now, then, new = buffers[k % 3], buffers[(k - 1) % 3], buffers[(k + 1) % 3]

        def blocks(i, _):
            v, p = now[0, i], now[1, i]
            qp[0, i] = inv[0, i] * v + inv[1, i] * p
            qp[1, i] = inv[2, i] * v + inv[3, i] * p
            return _

        lax.fori_loop(1 + k, EXT - 1 - k, blocks, 0, unroll=2)

        def spread(s, i):
            u = qp[s, i]
            fx, fy = face[s * 3, i], face[s * 3 + 1, i]
            total = fx * x_up(u) + x_down(fx * u)
            total = total + (fy * y_up(u) + y_down(fy * u))
            return total + (
                face[s * 3 + 2, i] * qp[s, i + 1] + face[s * 3 + 2, i - 1] * qp[s, i - 1]
            )

        def apply(i, main_planes):
            shared = spread(0, i)
            bv, bp = -shared, -(shared + spread(1, i))
            if main_planes:
                cbuf[0, i - DEPTH] = now[0, i] + bv
                cbuf[1, i - DEPTH] = now[1, i] + bp
            if k + 1 < KRYLOV:
                if k == 0:
                    new[0, i] = bv
                    new[1, i] = bp
                else:
                    new[0, i] = 2.0 * bv - then[0, i]
                    new[1, i] = 2.0 * bp - then[1, i]

        def outer(i, _):
            apply(i, False)
            return _

        def inner(i, _):
            apply(i, True)
            return _

        if k + 1 < KRYLOV:
            lax.fori_loop(2 + k, DEPTH, outer, 0)
            lax.fori_loop(DEPTH + FINE, EXT - 2 - k, outer, 0)
        lax.fori_loop(DEPTH, DEPTH + FINE, inner, 0, unroll=2)
        for part in range(2):
            values = compact(lambda z: qp[part, DEPTH + z])
            for g, value in enumerate(values):
                fields[k, part * 4 + g] = value
            remember(k + 1, part, compact(lambda z: cbuf[part, z]))

    parts[...] = jnp.zeros((2048, 128), f32)
    for r in range(1, KRYLOV + 1):

        def product(s, _):
            total, error = None, None
            for at in range(8):
                a, b = images[r, at], images[s, at]
                ah, al, bh, bl = gram[0, r, at], gram[1, r, at], gram[0, s, at], gram[1, s, at]
                p = a * b
                e = ((ah * bh - p) + ah * bl + al * bh) + al * bl
                if total is None:
                    total, error = p, e
                else:
                    total, e2 = two_sum(total, p)
                    error = error + (e + e2)
            column = jnp.where(s == 0, KRYLOV, s - 1)
            slot = ((r - 1) * SLOT + column) * 8
            mirror = jnp.where(s == 0, slot, ((s - 1) * SLOT + r - 1) * 8)
            for at in (slot, mirror):
                at = pl.multiple_of(at, 8)
                parts[pl.ds(at, 8), :] = total
                parts[pl.ds(1024 + at, 8), :] = error
            return _

        lax.fori_loop(0, r + 1, product, 0)

    for group in range(16):
        total = dd_total(
            (
                parts[pl.ds(group * 64 + i, 8, stride=8), :],
                parts[pl.ds(1024 + group * 64 + i, 8, stride=8), :],
            )
            for i in range(8)
        )
        acc[0, pl.ds(group * 8, 8), :] = total[0]
        acc[1, pl.ds(group * 8, 8), :] = total[1]
    turned = acc[0].T, acc[1].T
    total = dd_total(
        (turned[0][8 * i : 8 * i + 8], turned[1][8 * i : 8 * i + 8]) for i in range(16)
    )
    share(dd_fold(total), sums)


def share(total, out):
    rows = jnp.where(sublanes() % 2 == 0, total[0], total[1])
    for i in range(out.shape[0] // 8):
        out[pl.ds(8 * i, 8), :] = rows


def gathered(ref):
    count = ref.shape[0] // 2
    total = dd_total(
        (ref[pl.ds(16 * i, 8, stride=2), :], ref[pl.ds(16 * i + 1, 8, stride=2), :])
        for i in range(count // 8)
    )
    return dd_fold(total)


def sum_kernel(received, out):
    share(gathered(received), out)


def solve_kernel(received, fields, images, out):
    total = gathered(received)
    row = sublanes(16)
    matrix = []
    for part in total:
        part = jnp.concatenate([part, part], 0)
        value = jnp.zeros((16, 128), f32)
        for r in range(KRYLOV):
            value = jnp.where(row == r, turn(part, -r * SLOT), value)
        matrix.append(value)
    for j in range(KRYLOV):
        pivot_row = tuple(
            jnp.broadcast_to(part[j : j + 1, :], (8, 128)) for part in matrix
        )
        pivot = tuple(jnp.broadcast_to(part[:, j : j + 1], (8, 128)) for part in pivot_row)
        scaled = dd_mul(pivot_row, dd_inverse(pivot))
        scaled = tuple(jnp.concatenate([part, part], 0) for part in scaled)
        column = tuple(jnp.broadcast_to(part[:, j : j + 1], (16, 128)) for part in matrix)
        rest = dd_add(tuple(matrix), dd_neg(dd_mul(column, scaled)))
        matrix = [jnp.where(row == j, a, b) for a, b in zip(scaled, rest)]
    coeffs = [
        jnp.broadcast_to(matrix[0][k : k + 1, KRYLOV : KRYLOV + 1], (8, 128))
        for k in range(KRYLOV)
    ]
    for g in range(FINE // 4):
        v = []
        for part in range(2):
            value = coeffs[0] * fields[0, part * 4 + g]
            for k in range(1, KRYLOV):
                value = value + coeffs[k] * fields[k, part * 4 + g]
            v.append(value)
        v[0] = v[0] - v[1]
        for part in range(2):
            value = coeffs[0] * images[1, part * 4 + g]
            for k in range(1, KRYLOV):
                value = value + coeffs[k] * images[k + 1, part * 4 + g]
            v.append(images[0, part * 4 + g] - value)
        for j, value in enumerate(swap_blocks(v, 32)):
            out[pl.ds(4 * g + j, 8, stride=FINE), :] = value


def unpack_kernel(received, solution, residual, rows):
    rows[...] = received[...].T
    for f in range(4):
        ref = solution if f < 2 else residual
        for x in range(4):
            ref[f % 2, x] = rows[pl.ds(f * 32 + x, 8, stride=4), :]


def shape(*dims):
    return jax.ShapeDtypeStruct(dims, f32)


def scratch(*dims):
    return pltpu.VMEM(dims, f32)


def body(source, sigma_intra, sigma_extra, membrane):
    nx, ny, nz = (lax.axis_size(a) for a in ("gx", "gy", "gz"))
    packed = pl.pallas_call(
        pack_kernel, out_shape=shape(8 * ROWS, 128), scratch_shapes=[scratch(384, 128)]
    )(source, sigma_intra, sigma_extra, membrane)
    own = lax.all_to_all(packed.reshape(8, ROWS, 128), "gx", 0, 0, tiled=True)

    def from_y(value, by):
        pairs = [(i, i - by) for i in range(ny) if 0 <= i - by < ny]
        got = lax.ppermute(value, "gy", pairs)
        return got.reshape(-1, 128)

    halo = (from_y(own, 1), from_y(own, -1), from_y(own[:, :24], 2), from_y(own[:, 16:], -2))
    planes, first, final = pl.pallas_call(
        plane_kernel,
        out_shape=(
            shape(FIELDS, FINE, 8, 128),
            shape(FIELDS, DEPTH, 8, 128),
            shape(FIELDS, DEPTH, 8, 128),
        ),
    )(own.reshape(-1, 128), *halo)

    def place(c):
        return (c % nx) * nz + c // nx

    up = [(place(c), place(c + 1)) for c in range(nx * nz - 1)]
    low = lax.ppermute(final, ("gx", "gz"), up)
    high = lax.ppermute(first, ("gx", "gz"), [(b, a) for a, b in up])

    sums, fields, images = pl.pallas_call(
        cycle_kernel,
        out_shape=(
            shape(2 * nx * ny, 128),
            shape(KRYLOV, 8, 8, 128),
            shape(KRYLOV + 1, 8, 8, 128),
        ),
        scratch_shapes=[
            scratch(FIELDS, EXT, 8, 128),
            scratch(6, EXT, 8, 128),
            scratch(4, EXT, 8, 128),
            scratch(2, EXT, 8, 128),
            scratch(2, EXT, 8, 128),
            scratch(2, EXT, 8, 128),
            scratch(2, EXT, 8, 128),
            scratch(2, FINE, 8, 128),
            scratch(2, KRYLOV + 1, 8, 8, 128),
            scratch(2048, 128),
            scratch(2, 128, 128),
        ],
    )(planes, low, high)

    got = lax.all_to_all(sums.reshape(nx * ny, 2, 128), ("gx", "gy"), 0, 0, tiled=True)
    sums = pl.pallas_call(sum_kernel, out_shape=shape(2 * nz, 128))(got.reshape(-1, 128))
    got = lax.all_to_all(sums.reshape(nz, 2, 128), "gz", 0, 0, tiled=True)
    result = pl.pallas_call(solve_kernel, out_shape=shape(8 * FINE, 128))(
        got.reshape(-1, 128), fields, images
    )
    result = lax.all_to_all(result.reshape(8, FINE, 128), "gx", 0, 0, tiled=True)
    return pl.pallas_call(
        unpack_kernel,
        out_shape=(shape(2, 4, 8, 128), shape(2, 4, 8, 128)),
        scratch_shapes=[scratch(128, 128)],
    )(result.reshape(-1, 128))


def solution(mesh):
    spread = P(None, "gx", "gy", "gz")
    return jax.shard_map(
        body,
        mesh=mesh,
        in_specs=(spread, spread, spread, P("gx", "gy", "gz")),
        out_specs=(spread, spread),
        check_vma=False,
    )
```

time: 724 us -> 137 us (0.19); the launches traced: 711 us -> 136 us
  starting transfers between devices: 324 us -> 19.8 us
  waiting for transfers between devices: 169 us -> 14.2 us
  between operations: 83 us -> 0.73 us
  local copies, waits for them, and re-layouts: 64 us -> 1.53 us
  blocking collectives: 0 us -> 62.3 us
  other arithmetic: 59.3 us -> 0 us
  Pallas kernels: 0 us -> 37.4 us
  matrix products: 11.6 us -> 0 us
    all_to_all x22 -> x0, starting transfers between devices: 154 us -> none  [copy_for_each(): return lax.all_to_all(copies, axis, split_axis=0, concat_axis=0, tiled=True)]
    ppermute x72 -> x6, starting transfers between devices: 169 us -> 19.8 us  [the longest x4 12.9 us: from_y(): got = lax.ppermute(value, 'gy', pairs)]
    all_to_all x22 -> x0, waiting for transfers between devices: 141 us -> none  [copy_for_each(): return lax.all_to_all(copies, axis, split_axis=0, concat_axis=0, tiled=True)]
    all_to_all x0 -> x4, blocking collectives: none -> 62.3 us  [the longest x1 26.3 us: body(): lax.all_to_all(sums.reshape(nx * ny, 2, 128), ('gx', 'gy'), 0, 0, tiled=T...]
    pallas_call x0 -> x6, Pallas kernels: none -> 37.4 us  [the longest x1 24.3 us: body(): pl.pallas_call(cycle_kernel, out_shape=(shape(2 * nx * ny, 128), shape(KR...]
    another operation x58 -> x0, other arithmetic: 31.7 us -> none
    slice x90 -> x1, local copies, waits for them, and re-layouts: 24.2 us -> 0.02 us  [body(): own[:, 16:]]
    scatter x58 -> x0, local copies, waits for them, and re-layouts: 16.6 us -> none  [the longest x20 15.1 us: body(): hessenberg.at[:column + 1, column].set(project).at[column + 1, column]]
  transfers between devices with their start and end apart: 94 -> 6, of which waited for: 31 -> 4; matrix products, arithmetic and copies ran while one was open for 7% -> 0% of each run, Pallas kernels for 0% -> 0%
where the time goes in v1:
time: 137 us; the launch traced here: 136 us
  blocking collectives  62.3 us (45%)
  Pallas kernels  37.4 us (27%)
  starting transfers between devices  19.8 us (14%)
  waiting for transfers between devices  14.2 us (10%)
  local copies, waits for them, and re-layouts  1.53 us (1%)
    all_to_all x1, blocking collectives, body(): lax.all_to_all(sums.reshape(nx * ny, 2, 128), ('gx', 'gy'), 0, 0, tiled=T...  26.3 us
    pallas_call x1, Pallas kernels, body(): pl.pallas_call(cycle_kernel, out_shape=(shape(2 * nx * ny, 128), shape(KR...  24.3 us
    all_to_all x1, blocking collectives, body(): own = lax.all_to_all(packed.reshape(8, ROWS, 128), 'gx', 0, 0, tiled=True)  16 us
    ppermute x4, starting transfers between devices, from_y(): got = lax.ppermute(value, 'gy', pairs)  12.9 us
    all_to_all x1, blocking collectives, body(): lax.all_to_all(result.reshape(8, FINE, 128), 'gx', 0, 0, tiled=True)  11.2 us
    ppermute x4, waiting for transfers between devices, from_y(): got = lax.ppermute(value, 'gy', pairs)  9.04 us
    all_to_all x1, blocking collectives, body(): got = lax.all_to_all(sums.reshape(nz, 2, 128), 'gz', 0, 0, tiled=True)  8.84 us
    pallas_call x1, Pallas kernels, body(): pl.pallas_call(solve_kernel, out_shape=shape(8 * FINE, 128))  4.54 us
  transfers between devices with their start and end apart: 6, of which 4 were waited for; matrix products, arithmetic and copies ran while one was open for 0% of the time, Pallas kernels for 0%

profile of v1, /device:TPU:1, one launch (start us, length us, event | category | flops | bytes accessed | tf_op | source)
XLA Modules:
  0.0 136.0 jit_solution(9227923798645033185)
XLA Ops:
  0.6 1.7 %shard_map.59 = f32[320,128]{1,0:T(8,128)} custom-call(f32[2,4,8,128]{3,2,1,0:T(8,128)} %source.1, f32[3,4,8,128]{3,2,1,0:T(8,128)} %intra.1, f32[3,4,8,128]{3,2,1,0:T(8,128)} %extra.1, f32[4,8,128]{2,1,0:T(8,128)} %membrane.1), custom_call_target="tpu_custom_call" | custom-call | tf_op jit(solution)/shard_map/pallas_call | solution.py:432
  2.4 16.0 %all_to_all.20 = f32[8,40,128]{2,1,0:T(8,128)S(1)} all-to-all(f32[8,40,128]{2,1,0:T(8,128)} %bitcast.13), channel_id=1, replica_groups=mesh['gx'=8,'gy'=8,'gz'=8] {'gx'}, dimensions={0} | all-to-all | bytes 327680 | tf_op jit(solution)/shard_map/all_to_all | solution.py:435
  18.4 3.8 %collective-permute-start.1 = (f32[8,40,128]{2,1,0:T(8,128)S(1)}, f32[8,40,128]{2,1,0:T(8,128)S(1)}, u32[]{:S(2)}, u32[]{:S(2)}) collective-permute-start(f32[8,40,128]{2,1,0:T(8,128)S(1)} %all_to_all.20), channel_id=1, source_target_pairs={{0,8},{8,16},{16,24},{24,32},{32,40},{40,48},{48,56},{1,9},{9,17},... | collective-permute-start | bytes 491528 | tf_op jit(solution)/shard_map/ppermute | solution.py:439
  22.2 1.3 collective-permute-start
  23.6 6.4 %collective-permute-start.3 = (f32[8,24,128]{2,1,0:T(8,128)S(1)}, f32[8,24,128]{2,1,0:T(8,128)S(1)}, u32[]{:S(2)}, u32[]{:S(2)}) collective-permute-start(f32[8,24,128]{2,1,0:T(8,128)S(1)} %get-tuple-element.14), channel_id=1, source_target_pairs={{0,16},{8,24},{16,32},{24,40},{32,48},{40,56},{1,17},{9,25},{17,33... | collective-permute-start | bytes 294920 | tf_op jit(solution)/shard_map/ppermute | solution.py:439
  30.0 1.3 collective-permute-start.2
  31.3 0.3 collective-permute-done.3
  31.6 8.7 %collective-permute-done.2 = f32[8,24,128]{2,1,0:T(8,128)S(1)} collective-permute-done((f32[8,24,128]{2,1,0:T(8,128)S(1)}, f32[8,24,128]{2,1,0:T(8,128)S(1)}, u32[]{:S(2)}, u32[]{:S(2)}) %collective-permute-start.2) | collective-permute-done | bytes 98336 | tf_op jit(solution)/shard_map/ppermute | solution.py:439
  40.4 0.6 copy-done.6
  41.0 0.1 copy-done.3
  41.0 0.1 copy-done.4
  41.1 3.8 %shard_map.60 = (f32[9,16,8,128]{3,2,1,0:T(8,128)}, f32[9,11,8,128]{3,2,1,0:T(8,128)}, f32[9,11,8,128]{3,2,1,0:T(8,128)}) custom-call(f32[320,128]{1,0:T(8,128)} %bitcast.12, f32[320,128]{1,0:T(8,128)} %bitcast.18, f32[320,128]{1,0:T(8,128)} %bitcast.17, f32[192,128]{1,0:T(8,128)} %bitcast.20, f32[192,128]{1,0:T(8,128)} %bitcast.19), custom_call_target="tpu_custom_call" | custom-call | tf_op jit(solution)/shard_map/pallas_call | solution.py:443
  44.9 2.4 %collective-permute-start.4 = (f32[9,11,8,128]{3,2,1,0:T(8,128)}, f32[9,11,8,128]{3,2,1,0:T(8,128)S(1)}, u32[]{:S(2)}, u32[]{:S(2)}) collective-permute-start(f32[9,11,8,128]{3,2,1,0:T(8,128)} %get-tuple-element.9), channel_id=1, source_target_pairs={{0,64},{64,128},{128,192},{192,256},{256,320},{320,384},{384,448},... | collective-permute-start | bytes 1216520 | tf_op jit(solution)/shard_map/ppermute | solution.py:456
  47.3 4.5 %collective-permute-start.5 = (f32[9,11,8,128]{3,2,1,0:T(8,128)}, f32[9,11,8,128]{3,2,1,0:T(8,128)S(1)}, u32[]{:S(2)}, u32[]{:S(2)}) collective-permute-start(f32[9,11,8,128]{3,2,1,0:T(8,128)} %get-tuple-element.10), channel_id=1, source_target_pairs={{64,0},{128,64},{192,128},{256,192},{320,256},{384,320},{448,384},... | collective-permute-start | bytes 1216520 | tf_op jit(solution)/shard_map/ppermute | solution.py:457
  51.9 3.9 %collective-permute-done.4.low = f32[9,11,8,128]{3,2,1,0:T(8,128)S(1)} collective-permute-done((f32[9,11,8,128]{3,2,1,0:T(8,128)}, f32[9,11,8,128]{3,2,1,0:T(8,128)S(1)}, u32[]{:S(2)}, u32[]{:S(2)}) %collective-permute-start.4) | collective-permute-done | bytes 405536 | tf_op jit(solution)/shard_map/ppermute | solution.py:456
  55.7 1.3 collective-permute-done.5.high
  57.0 0.8 copy-done.2
  57.8 24.3 %shard_map.61 = (f32[128,128]{1,0:T(8,128)}, f32[10,8,8,128]{3,2,1,0:T(8,128)}, f32[11,8,8,128]{3,2,1,0:T(8,128)}) custom-call(f32[9,16,8,128]{3,2,1,0:T(8,128)} %get-tuple-element.8.main, f32[9,11,8,128]{3,2,1,0:T(8,128)} %copy-done.1, f32[9,11,8,128]{3,2,1,0:T(8,128)} %copy-done.2), custom_call_target="tpu_custom_call" | custom-call | tf_op jit(solution)/shard_map/pallas_call | solution.py:459
  82.1 26.3 %all_to_all.21 = f32[64,2,128]{2,1,0:T(2,128)} all-to-all(f32[64,2,128]{2,1,0:T(2,128)} %bitcast.21), channel_id=1, replica_groups=mesh['gx'=8,'gy'=8,'gz'=8] {'gx','gy'}, dimensions={0} | all-to-all | bytes 131072 | tf_op jit(solution)/shard_map/all_to_all | solution.py:481
  108.4 1.5 %shard_map.62 = f32[16,128]{1,0:T(8,128)} custom-call(f32[128,128]{1,0:T(8,128)} %bitcast.16), custom_call_target="tpu_custom_call" | custom-call | tf_op jit(solution)/shard_map/pallas_call | solution.py:482
  109.9 8.8 %all_to_all.22 = f32[8,2,128]{2,1,0:T(2,128)} all-to-all(f32[8,2,128]{2,1,0:T(2,128)} %bitcast.23), channel_id=1, replica_groups=mesh['gx'=8,'gy'=8,'gz'=8] {'gz'}, dimensions={0} | all-to-all | bytes 16384 | tf_op jit(solution)/shard_map/all_to_all | solution.py:483
  118.7 4.5 %shard_map.63 = f32[128,128]{1,0:T(8,128)} custom-call(f32[16,128]{1,0:T(8,128)} %bitcast.22, f32[10,8,8,128]{3,2,1,0:T(8,128)} %get-tuple-element.12.fields, f32[11,8,8,128]{3,2,1,0:T(8,128)} %get-tuple-element.13.images), custom_call_target="tpu_custom_call" | custom-call | tf_op jit(solution)/shard_map/pallas_call | solution.py:484
  123.3 11.2 %all_to_all.23 = f32[8,16,128]{2,1,0:T(8,128)} all-to-all(f32[8,16,128]{2,1,0:T(8,128)} %bitcast.14), channel_id=1, replica_groups=mesh['gx'=8,'gy'=8,'gz'=8] {'gx'}, dimensions={0} | all-to-all | bytes 131072 | tf_op jit(solution)/shard_map/all_to_all | solution.py:487
  134.5 1.6 %shard_map.64 = (f32[2,4,8,128]{3,2,1,0:T(8,128)}, f32[2,4,8,128]{3,2,1,0:T(8,128)}) custom-call(f32[128,128]{1,0:T(8,128)} %bitcast.15), custom_call_target="tpu_custom_call" | custom-call | tf_op jit(solution)/shard_map/pallas_call | solution.py:488
  (13 shorter events, 0.0 us)
Async XLA Ops:
  18.4 5.2 %copy-start = (f32[8,40,128]{2,1,0:T(8,128)}, f32[8,40,128]{2,1,0:T(8,128)S(1)}, u32[]{:S(2)}) copy-start(f32[8,40,128]{2,1,0:T(8,128)S(1)} %all_to_all.20) | copy-start | bytes 491524
  18.4 22.0 %collective-permute-start.1 = (f32[8,40,128]{2,1,0:T(8,128)S(1)}, f32[8,40,128]{2,1,0:T(8,128)S(1)}, u32[]{:S(2)}, u32[]{:S(2)}) collective-permute-start(f32[8,40,128]{2,1,0:T(8,128)S(1)} %all_to_all.20), channel_id=1, source_target_pairs={{0,8},{8,16},{16,24},{24,32},{32,40},{40,48},{48,56},{1,9},{9,17},... | collective-permute-start | bytes 491528 | tf_op jit(solution)/shard_map/ppermute | solution.py:439
  22.2 18.1 %collective-permute-start = (f32[8,40,128]{2,1,0:T(8,128)S(1)}, f32[8,40,128]{2,1,0:T(8,128)S(1)}, u32[]{:S(2)}, u32[]{:S(2)}) collective-permute-start(f32[8,40,128]{2,1,0:T(8,128)S(1)} %all_to_all.20), channel_id=1, source_target_pairs={{8,0},{16,8},{24,16},{32,24},{40,32},{48,40},{56,48},{9,1},{17,9},... | collective-permute-start | bytes 491528 | tf_op jit(solution)/shard_map/ppermute | solution.py:439
  23.6 8.1 %collective-permute-start.3 = (f32[8,24,128]{2,1,0:T(8,128)S(1)}, f32[8,24,128]{2,1,0:T(8,128)S(1)}, u32[]{:S(2)}, u32[]{:S(2)}) collective-permute-start(f32[8,24,128]{2,1,0:T(8,128)S(1)} %get-tuple-element.14), channel_id=1, source_target_pairs={{0,16},{8,24},{16,32},{24,40},{32,48},{40,56},{1,17},{9,25},{17,33... | collective-permute-start | bytes 294920 | tf_op jit(solution)/shard_map/ppermute | solution.py:439
  30.0 10.3 %collective-permute-start.2 = (f32[8,24,128]{2,1,0:T(8,128)S(1)}, f32[8,24,128]{2,1,0:T(8,128)S(1)}, u32[]{:S(2)}, u32[]{:S(2)}) collective-permute-start(f32[8,24,128]{2,1,0:T(8,128)S(1)} %get-tuple-element.15), channel_id=1, source_target_pairs={{16,0},{24,8},{32,16},{40,24},{48,32},{56,40},{17,1},{25,9},{33,17... | collective-permute-start | bytes 294920 | tf_op jit(solution)/shard_map/ppermute | solution.py:439
  31.6 8.8 %copy-start.5 = (f32[8,24,128]{2,1,0:T(8,128)}, f32[8,24,128]{2,1,0:T(8,128)S(1)}, u32[]{:S(2)}) copy-start(f32[8,24,128]{2,1,0:T(8,128)S(1)} %collective-permute-done.3) | copy-start | bytes 294916
  40.3 0.6 copy-start.6
  40.3 0.7 copy-start.3
  40.4 0.7 copy-start.4
  44.9 10.9 %collective-permute-start.4 = (f32[9,11,8,128]{3,2,1,0:T(8,128)}, f32[9,11,8,128]{3,2,1,0:T(8,128)S(1)}, u32[]{:S(2)}, u32[]{:S(2)}) collective-permute-start(f32[9,11,8,128]{3,2,1,0:T(8,128)} %get-tuple-element.9), channel_id=1, source_target_pairs={{0,64},{64,128},{128,192},{192,256},{256,320},{320,384},{384,448},... | collective-permute-start | bytes 1216520 | tf_op jit(solution)/shard_map/ppermute | solution.py:456
  47.3 9.7 %collective-permute-start.5 = (f32[9,11,8,128]{3,2,1,0:T(8,128)}, f32[9,11,8,128]{3,2,1,0:T(8,128)S(1)}, u32[]{:S(2)}, u32[]{:S(2)}) collective-permute-start(f32[9,11,8,128]{3,2,1,0:T(8,128)} %get-tuple-element.10), channel_id=1, source_target_pairs={{64,0},{128,64},{192,128},{256,192},{320,256},{384,320},{448,384},... | collective-permute-start | bytes 1216520 | tf_op jit(solution)/shard_map/ppermute | solution.py:457
  55.7 1.3 copy-start.1
  57.0 0.8 copy-start.2

commit v2 on v1

v2 whole, which is shorter than its diff:
```python
import jax
import jax.numpy as jnp
from jax import lax
from jax.experimental import pallas as pl
from jax.experimental.pallas import tpu as pltpu
from jax.sharding import PartitionSpec as P

KRYLOV = 10
DEPTH = KRYLOV + 1
FINE = 16
EXT = FINE + 2 * DEPTH
SENT = 7
FIELDS = 9
ROWS = 40
UNIQUE = KRYLOV * (KRYLOV + 1) // 2
f32 = jnp.float32


def lanes(rows=8):
    return lax.broadcasted_iota(jnp.int32, (rows, 128), 1)


def sublanes(rows=8):
    return lax.broadcasted_iota(jnp.int32, (rows, 128), 0)


def turn(v, by):
    return v if by % 128 == 0 else pltpu.roll(v, by % 128, 1)


def sink(v, by):
    return pltpu.roll(v, by % 8, 0)


def two_sum(a, b):
    s = a + b
    z = s - a
    return s, (a - (s - z)) + (b - z)


def quick_sum(a, b):
    s = a + b
    return s, b - (s - a)


def split(a):
    c = a * 4097.0
    high = c - (c - a)
    return high, a - high


def two_prod(a, b):
    p = a * b
    ah, al = split(a)
    bh, bl = split(b)
    return p, ((ah * bh - p) + ah * bl + al * bh) + al * bl


def dd_add(a, b):
    s, e = two_sum(a[0], b[0])
    return quick_sum(s, e + (a[1] + b[1]))


def dd_mul(a, b):
    p, e = two_prod(a[0], b[0])
    return quick_sum(p, e + (a[0] * b[1] + a[1] * b[0]))


def dd_inverse(a):
    x = 1.0 / a[0]
    p, e = two_prod(a[0], x)
    return quick_sum(x, x * (((1.0 - p) - e) - a[1] * x))


def add_pairs(a, b):
    s, e = two_sum(a[0], b[0])
    return s, e + (a[1] + b[1])


def total_of(pairs):
    pairs = list(pairs)
    while len(pairs) > 1:
        pairs = [
            add_pairs(pairs[i], pairs[i + 1]) if i + 1 < len(pairs) else pairs[i]
            for i in range(0, len(pairs), 2)
        ]
    return pairs[0]


def fold_sublanes(a):
    for by in (4, 2, 1):
        a = add_pairs(a, (sink(a[0], by), sink(a[1], by)))
    return quick_sum(*a)


def swap_blocks(v, width):
    v = list(v)
    block = lanes() // width
    d = len(v) // 2
    while d >= 1:
        low = (block & d) == 0
        for k in range(len(v)):
            if k & d == 0:
                a, b = v[k], v[k + d]
                v[k] = jnp.where(low, a, turn(b, width * d))
                v[k + d] = jnp.where(low, turn(a, -width * d), b)
        d //= 2
    return v


def pack_kernel(source, intra, extra, membrane, out):
    refs = [(intra, 0), (intra, 1), (intra, 2), (extra, 0), (extra, 1), (extra, 2), (source, 0), (source, 1)]
    top = sublanes() < 4
    lower, upper = [], []
    for x in range(4):
        for f in range(0, 8, 2):
            a, b = refs[f][0][refs[f][1], x], refs[f + 1][0][refs[f + 1][1], x]
            lower.append(jnp.where(top, a, sink(b, 4)))
            upper.append(jnp.where(top, sink(a, 4), b))
    empty = jnp.zeros((24, 128), f32)
    last = []
    for x in range(4):
        last += [membrane[x], empty]
    lower, upper, last = (jnp.concatenate(part, 0).T for part in (lower, upper, last))
    near = (lanes() % 32) < 8
    for j in range(8):
        at = j * ROWS
        out[pl.ds(at, 16), :] = lower[16 * j : 16 * j + 16]
        out[pl.ds(at + 16, 8), :] = jnp.where(
            near, last[16 * j : 16 * j + 8], turn(last[16 * j + 8 : 16 * j + 16], 8)
        )
        out[pl.ds(at + 24, 16), :] = upper[16 * j : 16 * j + 16]


def plane_kernel(main, above, below, above2, below2, out, first, final):
    y = lanes() % 32

    def take(ref, row, height):
        return ref[pl.ds(row, 8, stride=height), :]

    def plane(z):
        v = [
            take(below2, 8 + z, 24),
            take(below, z, ROWS),
            take(below, 24 + z, ROWS),
            take(main, z, ROWS),
            take(main, 24 + z, ROWS),
            take(above, z, ROWS),
            take(above, 24 + z, ROWS),
            take(above2, z, 24),
        ]
        v = swap_blocks(v, 4)
        r, shift = z % 8, 8 * (z // 8)
        m = turn(take(above2, 16 + r, 24), 28 - shift)
        m = jnp.where(y < 28, turn(take(above, 16 + r, ROWS), 20 - shift), m)
        m = jnp.where(y < 20, turn(take(main, 16 + r, ROWS), 12 - shift), m)
        m = jnp.where(y < 12, turn(take(below, 16 + r, ROWS), 4 - shift), m)
        m = jnp.where(y < 4, turn(take(below2, r, 24), -4 - shift), m)
        return v + [m]

    for z in range(FINE):
        for f, value in enumerate(plane(z)):
            out[f, z] = value
    for ref, at in ((first, lambda d: d - 1), (final, lambda d: FINE - d)):
        for d in range(1, SENT + 1):
            near = (y > d) & (y < 31 - d)
            for f in range(FIELDS):
                value = out[f, at(d)]
                if 2 < d < SENT:
                    value = jnp.where(near, value, turn(out[f, at(14 - d)], 16))
                ref[f, d - 1] = value


def x_up(v):
    v = turn(v, -32)
    return jnp.where(lanes() < 96, v, sink(v, -1))


def x_down(v):
    v = turn(v, 32)
    return jnp.where(lanes() >= 32, v, sink(v, 1))


def y_up(v):
    return turn(v, -1)


def y_down(v):
    return turn(v, 1)


def slot_of(r, s):
    if s < 0:
        return UNIQUE + r if r < KRYLOV - 1 else 64 + UNIQUE
    return r * (r + 1) // 2 + s


def cycle_kernel(main, low, high, sums, fields, images, face, inv, ta, tb, halves, parts, acc):
    lane = lanes()
    ix = sublanes() * 4 + lane // 32
    last_x, first_x = ix == 31, ix == 0

    def far(ref, f, d):
        return ref[f, d - 1] if d <= SENT else turn(ref[f, 13 - d], -16)

    def field(f, i):
        if i < DEPTH:
            return far(low, f, DEPTH - i)
        if i < DEPTH + FINE:
            return main[f, i - DEPTH]
        return far(high, f, i - DEPTH - FINE + 1)

    sz = [field(2, 0), field(5, 0)]
    low_z = [None, None]
    for i in range(EXT - 1):
        diagonals = []
        for s in range(2):
            above = field(s * 3 + 2, i + 1)
            up_z = 0.5 * (sz[s] + above)
            face[s * 3 + 2, i] = up_z
            if i > 0:
                sx, sy = field(s * 3, i), field(s * 3 + 1, i)
                up_x = 0.5 * (sx + jnp.where(last_x, 0.0, x_up(sx)))
                low_x = 0.5 * (sx + jnp.where(first_x, 0.0, x_down(sx)))
                up_y = 0.5 * (sy + y_up(sy))
                low_y = 0.5 * (sy + y_down(sy))
                face[s * 3, i] = jnp.where(last_x, 0.0, up_x)
                face[s * 3 + 1, i] = up_y
                diagonals.append(up_x + low_x + up_y + low_y + up_z + low_z[s])
            sz[s], low_z[s] = above, up_z
        if i > 0:
            di, de = diagonals
            m = field(8, i)
            det = m * di + m * de + di * de
            inside = m > 0.0
            scale = jnp.where(inside, 1.0 / jnp.where(inside, det, 1.0), 0.0)
            inv[0, i] = de * scale
            inv[1, i] = m * scale
            inv[2, i] = -di * scale
            inv[3, i] = (m + di) * scale

    block = (lane % 32) // 8

    def compact(planes):
        value = turn(planes[3], 12)
        for j in (2, 1, 0):
            value = jnp.where(block == j, turn(planes[j], 8 * j - 12), value)
        return value

    def remember(r, at, value):
        images[r, at] = value
        halves[0, r, at], halves[1, r, at] = split(value)

    for part in range(2):
        for g in range(FINE // 4):
            remember(0, part * 4 + g, compact([main[6 + part, 4 * g + j] for j in range(4)]))

    buffers = (ta, tb)

    def vector(k, part, i):
        return field(6 + part, i) if k == 0 else buffers[k % 2][part, i]

    for k in range(KRYLOV):

        def blocks(i):
            v, p = vector(k, 0, i), vector(k, 1, i)
            return (inv[0, i] * v + inv[1, i] * p, inv[2, i] * v + inv[3, i] * p), (v, p)

        def spread(s, i, u):
            fx, fy = face[s * 3, i], face[s * 3 + 1, i]
            across = fx * x_up(u[1][s]) + x_down(fx * u[1][s])
            along = fy * y_up(u[1][s]) + y_down(fy * u[1][s])
            deep = face[s * 3 + 2, i] * u[2][s] + face[s * 3 + 2, i - 1] * u[0][s]
            return across + along + deep

        start, end = 2 + k, EXT - 2 - k
        (before, _), (here, t_here) = blocks(start - 1), blocks(start)
        kept = ([], [], [], [])
        for i in range(start, end):
            after, t_after = blocks(i + 1)
            shared = spread(0, i, (before, here, after))
            b = (-shared, -(shared + spread(1, i, (before, here, after))))
            if DEPTH <= i < DEPTH + FINE:
                for part in range(2):
                    kept[part].append(here[part])
                    kept[2 + part].append(t_here[part] + b[part])
                if len(kept[0]) == 4:
                    g = (i - DEPTH) // 4
                    for part in range(2):
                        fields[k, part * 4 + g] = compact(kept[part])
                        remember(k + 1, part * 4 + g, compact(kept[2 + part]))
                    kept = ([], [], [], [])
            if k + 1 < KRYLOV:
                for part in range(2):
                    value = b[part]
                    if k > 0:
                        value = 2.0 * value - vector(k - 1, part, i)
                    buffers[(k + 1) % 2][part, i] = value
            before, here, t_here = here, after, t_after

    parts[...] = jnp.zeros((2048, 128), f32)
    for r in range(1, KRYLOV + 1):
        for s in range(r + 1):
            terms = []
            for at in range(8):
                a, b = images[r, at], images[s, at]
                ah, al, bh, bl = halves[0, r, at], halves[1, r, at], halves[0, s, at], halves[1, s, at]
                p = a * b
                terms.append((p, ((ah * bh - p) + ah * bl + al * bh) + al * bl))
            value = total_of(terms)
            slot = slot_of(r - 1, s - 1) * 8
            parts[pl.ds(slot, 8), :] = value[0]
            parts[pl.ds(1024 + slot, 8), :] = value[1]

    for group in range(16):
        value = total_of(
            (
                parts[pl.ds(group * 64 + i, 8, stride=8), :],
                parts[pl.ds(1024 + group * 64 + i, 8, stride=8), :],
            )
            for i in range(8)
        )
        acc[0, pl.ds(group * 8, 8), :] = value[0]
        acc[1, pl.ds(group * 8, 8), :] = value[1]
    turned = acc[0].T, acc[1].T
    value = fold_sublanes(
        total_of((turned[0][8 * i : 8 * i + 8], turned[1][8 * i : 8 * i + 8]) for i in range(16))
    )
    whole = (lane < 64) | (lane == 64 + UNIQUE)
    row = jnp.where(whole, value[0], turn(value[1], 64))
    for i in range(sums.shape[0] // 8):
        sums[pl.ds(8 * i, 8), :] = row


def solve_kernel(received, fields, images, out):
    chunk = 8
    groups = received.shape[0] // 8
    value = total_of(
        total_of(
            (received[pl.ds(8 * i, 8), :], jnp.zeros((8, 128), f32))
            for i in range(at, min(at + chunk, groups))
        )
        for at in range(0, groups, chunk)
    )
    high, error = fold_sublanes(value)
    error = error + jnp.where(lanes() < UNIQUE, turn(high, 64), 0.0)
    row, lane = sublanes(16), lanes(16)
    matrix = []
    for n, part in enumerate((high, error)):
        part = jnp.concatenate([part, part], 0)
        value = jnp.zeros((16, 128), f32)
        for r in range(KRYLOV):
            value = jnp.where(row == r, turn(part, -slot_of(r, 0)), value)
        value = jnp.where(lane <= row, value, 0.0)
        flipped = jnp.concatenate([value, jnp.zeros((112, 128), f32)], 0).T[:16]
        value = jnp.where(lane <= row, value, flipped)
        right = jnp.zeros((16, 128), f32)
        for r in range(KRYLOV):
            right = jnp.where(row == r, turn(part, KRYLOV - slot_of(r, -1)), right)
        matrix.append(jnp.where(lane == KRYLOV, right, value))
    matrix = quick_sum(*matrix)
    for j in range(KRYLOV):
        pivot_row = tuple(jnp.broadcast_to(part[j : j + 1, :], (8, 128)) for part in matrix)
        pivot = tuple(jnp.broadcast_to(part[j : j + 1, j : j + 1], (8, 128)) for part in matrix)
        scaled = dd_mul(pivot_row, dd_inverse(pivot))
        scaled = tuple(jnp.concatenate([part, part], 0) for part in scaled)
        column = tuple(-jnp.broadcast_to(part[:, j : j + 1], (16, 128)) for part in matrix)
        rest = dd_add(matrix, dd_mul(column, scaled))
        matrix = tuple(jnp.where(row == j, a, b) for a, b in zip(scaled, rest))
    coeffs = [
        jnp.broadcast_to(matrix[0][k : k + 1, KRYLOV : KRYLOV + 1], (8, 128))
        for k in range(KRYLOV)
    ]
    for g in range(FINE // 4):
        v = []
        for part in range(2):
            v.append(sum(coeffs[k] * fields[k, part * 4 + g] for k in range(KRYLOV)))
        v[0] = v[0] - v[1]
        for part in range(2):
            value = sum(coeffs[k] * images[k + 1, part * 4 + g] for k in range(KRYLOV))
            v.append(images[0, part * 4 + g] - value)
        for j, value in enumerate(swap_blocks(v, 8)):
            out[pl.ds(4 * g + j, 8, stride=FINE), :] = value


def unpack_kernel(received, solution, residual):
    rows = received[...].T
    for f in range(4):
        ref = solution if f < 2 else residual
        for x in range(4):
            ref[f % 2, x] = rows[x * 32 + f * 8 : x * 32 + f * 8 + 8]


def shape(*dims):
    return jax.ShapeDtypeStruct(dims, f32)


def scratch(*dims):
    return pltpu.VMEM(dims, f32)


def body(source, sigma_intra, sigma_extra, membrane):
    nx, ny, nz = (lax.axis_size(a) for a in ("gx", "gy", "gz"))
    packed = pl.pallas_call(pack_kernel, out_shape=shape(8 * ROWS, 128))(
        source, sigma_intra, sigma_extra, membrane
    )
    own = lax.all_to_all(packed.reshape(8, ROWS, 128), "gx", 0, 0, tiled=True)

    def from_y(value, by):
        pairs = [(i, i - by) for i in range(ny) if 0 <= i - by < ny]
        got = lax.ppermute(value, "gy", pairs)
        return got.reshape(-1, 128)

    halo = (from_y(own, 1), from_y(own, -1), from_y(own[:, :24], 2), from_y(own[:, 16:], -2))
    planes, first, final = pl.pallas_call(
        plane_kernel,
        out_shape=(
            shape(FIELDS, FINE, 8, 128),
            shape(FIELDS, SENT, 8, 128),
            shape(FIELDS, SENT, 8, 128),
        ),
    )(own.reshape(-1, 128), *halo)

    def place(c):
        return (c % nx) * nz + c // nx

    up = [(place(c), place(c + 1)) for c in range(nx * nz - 1)]
    low = lax.ppermute(final, ("gx", "gz"), up)
    high = lax.ppermute(first, ("gx", "gz"), [(b, a) for a, b in up])

    sums, fields, images = pl.pallas_call(
        cycle_kernel,
        out_shape=(
            shape(nx * ny * nz, 128),
            shape(KRYLOV, 8, 8, 128),
            shape(KRYLOV + 1, 8, 8, 128),
        ),
        scratch_shapes=[
            scratch(6, EXT, 8, 128),
            scratch(4, EXT, 8, 128),
            scratch(2, EXT, 8, 128),
            scratch(2, EXT, 8, 128),
            scratch(2, KRYLOV + 1, 8, 8, 128),
            scratch(2048, 128),
            scratch(2, 128, 128),
        ],
    )(planes, low, high)

    everyone = ("gx", "gy", "gz")
    got = lax.all_to_all(sums.reshape(-1, 1, 128), everyone, 0, 0, tiled=True)
    result = pl.pallas_call(solve_kernel, out_shape=shape(8 * FINE, 128))(
        got.reshape(-1, 128), fields, images
    )
    result = lax.all_to_all(result.reshape(8, FINE, 128), "gx", 0, 0, tiled=True)
    return pl.pallas_call(
        unpack_kernel,
        out_shape=(shape(2, 4, 8, 128), shape(2, 4, 8, 128)),
    )(result.reshape(-1, 128))


def solution(mesh):
    spread = P(None, "gx", "gy", "gz")
    return jax.shard_map(
        body,
        mesh=mesh,
        in_specs=(spread, spread, spread, P("gx", "gy", "gz")),
        out_specs=(spread, spread),
        check_vma=False,
    )
```

time: 137 us -> 121 us (0.88)
  Pallas kernels: 37.4 us -> 20.4 us
  blocking collectives: 62.3 us -> 65.5 us
  waiting for transfers between devices: 14.2 us -> 12.6 us
    pallas_call x3 -> x2, Pallas kernels: 27.5 us -> 10.7 us  [the longest x1 9 us: body(): pl.pallas_call(cycle_kernel, out_shape=(shape(nx * ny * nz, 128), shape(K...]
    all_to_all x2 -> x1, blocking collectives: 35.1 us -> 37.3 us  [body(): got = lax.all_to_all(sums.reshape(-1, 1, 128), everyone, 0, 0, tiled=True)]
    ppermute x1, waiting for transfers between devices: 3.86 us -> 2.28 us  [body(): low = lax.ppermute(final, ('gx', 'gz'), up)]
where the time goes in v2:
time: 121 us
  blocking collectives  65.5 us (54%)
  Pallas kernels  20.4 us (17%)
  starting transfers between devices  19.8 us (16%)
  waiting for transfers between devices  12.6 us (10%)
  local copies, waits for them, and re-layouts  1.48 us (1%)
    all_to_all x1, blocking collectives, body(): got = lax.all_to_all(sums.reshape(-1, 1, 128), everyone, 0, 0, tiled=True)  37.3 us
    all_to_all x1, blocking collectives, body(): own = lax.all_to_all(packed.reshape(8, ROWS, 128), 'gx', 0, 0, tiled=True)  16 us
    ppermute x4, starting transfers between devices, from_y(): got = lax.ppermute(value, 'gy', pairs)  12.9 us
    all_to_all x1, blocking collectives, body(): lax.all_to_all(result.reshape(8, FINE, 128), 'gx', 0, 0, tiled=True)  12.1 us
    ppermute x4, waiting for transfers between devices, from_y(): got = lax.ppermute(value, 'gy', pairs)  9.04 us
    pallas_call x1, Pallas kernels, body(): pl.pallas_call(cycle_kernel, out_shape=(shape(nx * ny * nz, 128), shape(K...  9 us
    ppermute x1, starting transfers between devices, body(): high = lax.ppermute(first, ('gx', 'gz'), [(b, a) for a, b in up])  4.53 us
    pallas_call x1, Pallas kernels, body(): pl.pallas_call(plane_kernel, out_shape=(shape(FIELDS, FINE, 8, 128), shap...  4.26 us
  transfers between devices with their start and end apart: 6, of which 4 were waited for; matrix products, arithmetic and copies ran while one was open for 0% of the time, Pallas kernels for 0%

profile of v2, /device:TPU:1, one launch (start us, length us, event | category | flops | bytes accessed | tf_op | source)
XLA Modules:
  0.0 120.5 jit_solution(8377556981194409446)
XLA Ops:
  0.6 1.7 %shard_map.59 = f32[320,128]{1,0:T(8,128)} custom-call(f32[2,4,8,128]{3,2,1,0:T(8,128)} %source.1, f32[3,4,8,128]{3,2,1,0:T(8,128)} %intra.1, f32[3,4,8,128]{3,2,1,0:T(8,128)} %extra.1, f32[4,8,128]{2,1,0:T(8,128)} %membrane.1), custom_call_target="tpu_custom_call" | custom-call | tf_op jit(solution)/shard_map/pallas_call | solution.py:404
  2.3 16.0 %all_to_all.15 = f32[8,40,128]{2,1,0:T(8,128)S(1)} all-to-all(f32[8,40,128]{2,1,0:T(8,128)} %bitcast.14), channel_id=1, replica_groups=mesh['gx'=8,'gy'=8,'gz'=8] {'gx'}, dimensions={0} | all-to-all | bytes 327680 | tf_op jit(solution)/shard_map/all_to_all | solution.py:407
  18.3 3.8 %collective-permute-start.1 = (f32[8,40,128]{2,1,0:T(8,128)S(1)}, f32[8,40,128]{2,1,0:T(8,128)S(1)}, u32[]{:S(2)}, u32[]{:S(2)}) collective-permute-start(f32[8,40,128]{2,1,0:T(8,128)S(1)} %all_to_all.15), channel_id=1, source_target_pairs={{0,8},{8,16},{16,24},{24,32},{32,40},{40,48},{48,56},{1,9},{9,17},... | collective-permute-start | bytes 491528 | tf_op jit(solution)/shard_map/ppermute | solution.py:411
  22.2 1.3 %collective-permute-start = (f32[8,40,128]{2,1,0:T(8,128)S(1)}, f32[8,40,128]{2,1,0:T(8,128)S(1)}, u32[]{:S(2)}, u32[]{:S(2)}) collective-permute-start(f32[8,40,128]{2,1,0:T(8,128)S(1)} %all_to_all.15), channel_id=1, source_target_pairs={{8,0},{16,8},{24,16},{32,24},{40,32},{48,40},{56,48},{9,1},{17,9},... | collective-permute-start | bytes 491528 | tf_op jit(solution)/shard_map/ppermute | solution.py:411
  23.5 6.4 %collective-permute-start.3 = (f32[8,24,128]{2,1,0:T(8,128)S(1)}, f32[8,24,128]{2,1,0:T(8,128)S(1)}, u32[]{:S(2)}, u32[]{:S(2)}) collective-permute-start(f32[8,24,128]{2,1,0:T(8,128)S(1)} %get-tuple-element.14), channel_id=1, source_target_pairs={{0,16},{8,24},{16,32},{24,40},{32,48},{40,56},{1,17},{9,25},{17,33... | collective-permute-start | bytes 294920 | tf_op jit(solution)/shard_map/ppermute | solution.py:411
  29.9 1.3 %collective-permute-start.2 = (f32[8,24,128]{2,1,0:T(8,128)S(1)}, f32[8,24,128]{2,1,0:T(8,128)S(1)}, u32[]{:S(2)}, u32[]{:S(2)}) collective-permute-start(f32[8,24,128]{2,1,0:T(8,128)S(1)} %get-tuple-element.15), channel_id=1, source_target_pairs={{16,0},{24,8},{32,16},{40,24},{48,32},{56,40},{17,1},{25,9},{33,17... | collective-permute-start | bytes 294920 | tf_op jit(solution)/shard_map/ppermute | solution.py:411
  31.2 0.3 collective-permute-done.3
  31.6 8.7 %collective-permute-done.2 = f32[8,24,128]{2,1,0:T(8,128)S(1)} collective-permute-done((f32[8,24,128]{2,1,0:T(8,128)S(1)}, f32[8,24,128]{2,1,0:T(8,128)S(1)}, u32[]{:S(2)}, u32[]{:S(2)}) %collective-permute-start.2) | collective-permute-done | bytes 98336 | tf_op jit(solution)/shard_map/ppermute | solution.py:411
  40.3 0.0 collective-permute-done.1
  40.3 0.0 collective-permute-done
  40.3 0.6 copy-done.6
  40.9 0.1 copy-done.3
  41.0 0.1 copy-done.4
  41.0 4.3 %shard_map.60 = (f32[9,16,8,128]{3,2,1,0:T(8,128)}, f32[9,7,8,128]{3,2,1,0:T(8,128)}, f32[9,7,8,128]{3,2,1,0:T(8,128)}) custom-call(f32[320,128]{1,0:T(8,128)} %bitcast.12, f32[320,128]{1,0:T(8,128)} %bitcast.19, f32[320,128]{1,0:T(8,128)} %bitcast.18, f32[192,128]{1,0:T(8,128)} %bitcast.21, f32[192,128]{1,0:T(8,128)} %bitcast.20), custom_call_target="tpu_custom_call" | custom-call | tf_op jit(solution)/shard_map/pallas_call | solution.py:415
  45.3 2.4 %collective-permute-start.4 = (f32[9,7,8,128]{3,2,1,0:T(8,128)}, f32[9,7,8,128]{3,2,1,0:T(8,128)S(1)}, u32[]{:S(2)}, u32[]{:S(2)}) collective-permute-start(f32[9,7,8,128]{3,2,1,0:T(8,128)} %get-tuple-element.9), channel_id=1, source_target_pairs={{0,64},{64,128},{128,192},{192,256},{256,320},{320,384},{384,448},... | collective-permute-start | bytes 774152 | tf_op jit(solution)/shard_map/ppermute | solution.py:428
  47.8 4.5 %collective-permute-start.5 = (f32[9,7,8,128]{3,2,1,0:T(8,128)}, f32[9,7,8,128]{3,2,1,0:T(8,128)S(1)}, u32[]{:S(2)}, u32[]{:S(2)}) collective-permute-start(f32[9,7,8,128]{3,2,1,0:T(8,128)} %get-tuple-element.10), channel_id=1, source_target_pairs={{64,0},{128,64},{192,128},{256,192},{320,256},{384,320},{448,384},... | collective-permute-start | bytes 774152 | tf_op jit(solution)/shard_map/ppermute | solution.py:429
  52.3 2.3 %collective-permute-done.4.low = f32[9,7,8,128]{3,2,1,0:T(8,128)S(1)} collective-permute-done((f32[9,7,8,128]{3,2,1,0:T(8,128)}, f32[9,7,8,128]{3,2,1,0:T(8,128)S(1)}, u32[]{:S(2)}, u32[]{:S(2)}) %collective-permute-start.4) | collective-permute-done | bytes 258080 | tf_op jit(solution)/shard_map/ppermute | solution.py:428
  54.6 1.3 %collective-permute-done.5.high = f32[9,7,8,128]{3,2,1,0:T(8,128)S(1)} collective-permute-done((f32[9,7,8,128]{3,2,1,0:T(8,128)}, f32[9,7,8,128]{3,2,1,0:T(8,128)S(1)}, u32[]{:S(2)}, u32[]{:S(2)}) %collective-permute-start.5) | collective-permute-done | bytes 258080 | tf_op jit(solution)/shard_map/ppermute | solution.py:429
  55.9 0.7 copy-done.2
  56.6 9.0 %shard_map.61 = (f32[512,128]{1,0:T(8,128)}, f32[10,8,8,128]{3,2,1,0:T(8,128)}, f32[11,8,8,128]{3,2,1,0:T(8,128)}) custom-call(f32[9,16,8,128]{3,2,1,0:T(8,128)} %get-tuple-element.8.main, f32[9,7,8,128]{3,2,1,0:T(8,128)} %copy-done.1, f32[9,7,8,128]{3,2,1,0:T(8,128)} %copy-done.2), custom_call_target="tpu_custom_call" | custom-call | tf_op jit(solution)/shard_map/pallas_call | solution.py:431
  65.6 37.3 %all_to_all.16 = f32[512,1,128]{2,1,0:T(1,128)} all-to-all(f32[512,1,128]{2,1,0:T(1,128)} %bitcast.16), channel_id=1, replica_groups=mesh['gx'=8,'gy'=8,'gz'=8] {'gx','gy','gz'}, dimensions={0} | all-to-all | bytes 524288 | tf_op jit(solution)/shard_map/all_to_all | solution.py:450
  102.9 3.9 %shard_map.62 = f32[128,128]{1,0:T(8,128)} custom-call(f32[512,128]{1,0:T(8,128)} %bitcast.13, f32[10,8,8,128]{3,2,1,0:T(8,128)} %get-tuple-element.12.fields, f32[11,8,8,128]{3,2,1,0:T(8,128)} %get-tuple-element.13.images), custom_call_target="tpu_custom_call" | custom-call | tf_op jit(solution)/shard_map/pallas_call | solution.py:451
  106.8 12.1 %all_to_all.17 = f32[8,16,128]{2,1,0:T(8,128)} all-to-all(f32[8,16,128]{2,1,0:T(8,128)} %bitcast.15), channel_id=1, replica_groups=mesh['gx'=8,'gy'=8,'gz'=8] {'gx'}, dimensions={0} | all-to-all | bytes 131072 | tf_op jit(solution)/shard_map/all_to_all | solution.py:454
  119.0 1.6 %shard_map.63 = (f32[2,4,8,128]{3,2,1,0:T(8,128)}, f32[2,4,8,128]{3,2,1,0:T(8,128)}) custom-call(f32[128,128]{1,0:T(8,128)} %bitcast.17), custom_call_target="tpu_custom_call" | custom-call | tf_op jit(solution)/shard_map/pallas_call | solution.py:455
  (11 shorter events, 0.0 us)
Async XLA Ops:
  18.3 5.2 %copy-start = (f32[8,40,128]{2,1,0:T(8,128)}, f32[8,40,128]{2,1,0:T(8,128)S(1)}, u32[]{:S(2)}) copy-start(f32[8,40,128]{2,1,0:T(8,128)S(1)} %all_to_all.15) | copy-start | bytes 491524
  18.3 22.0 %collective-permute-start.1 = (f32[8,40,128]{2,1,0:T(8,128)S(1)}, f32[8,40,128]{2,1,0:T(8,128)S(1)}, u32[]{:S(2)}, u32[]{:S(2)}) collective-permute-start(f32[8,40,128]{2,1,0:T(8,128)S(1)} %all_to_all.15), channel_id=1, source_target_pairs={{0,8},{8,16},{16,24},{24,32},{32,40},{40,48},{48,56},{1,9},{9,17},... | collective-permute-start | bytes 491528 | tf_op jit(solution)/shard_map/ppermute | solution.py:411
  22.2 18.1 %collective-permute-start = (f32[8,40,128]{2,1,0:T(8,128)S(1)}, f32[8,40,128]{2,1,0:T(8,128)S(1)}, u32[]{:S(2)}, u32[]{:S(2)}) collective-permute-start(f32[8,40,128]{2,1,0:T(8,128)S(1)} %all_to_all.15), channel_id=1, source_target_pairs={{8,0},{16,8},{24,16},{32,24},{40,32},{48,40},{56,48},{9,1},{17,9},... | collective-permute-start | bytes 491528 | tf_op jit(solution)/shard_map/ppermute | solution.py:411
  23.5 8.1 %collective-permute-start.3 = (f32[8,24,128]{2,1,0:T(8,128)S(1)}, f32[8,24,128]{2,1,0:T(8,128)S(1)}, u32[]{:S(2)}, u32[]{:S(2)}) collective-permute-start(f32[8,24,128]{2,1,0:T(8,128)S(1)} %get-tuple-element.14), channel_id=1, source_target_pairs={{0,16},{8,24},{16,32},{24,40},{32,48},{40,56},{1,17},{9,25},{17,33... | collective-permute-start | bytes 294920 | tf_op jit(solution)/shard_map/ppermute | solution.py:411
  29.9 10.3 %collective-permute-start.2 = (f32[8,24,128]{2,1,0:T(8,128)S(1)}, f32[8,24,128]{2,1,0:T(8,128)S(1)}, u32[]{:S(2)}, u32[]{:S(2)}) collective-permute-start(f32[8,24,128]{2,1,0:T(8,128)S(1)} %get-tuple-element.15), channel_id=1, source_target_pairs={{16,0},{24,8},{32,16},{40,24},{48,32},{56,40},{17,1},{25,9},{33,17... | collective-permute-start | bytes 294920 | tf_op jit(solution)/shard_map/ppermute | solution.py:411
  31.6 8.8 %copy-start.5 = (f32[8,24,128]{2,1,0:T(8,128)}, f32[8,24,128]{2,1,0:T(8,128)S(1)}, u32[]{:S(2)}) copy-start(f32[8,24,128]{2,1,0:T(8,128)S(1)} %collective-permute-done.3) | copy-start | bytes 294916
  40.3 0.6 copy-start.6
  40.3 0.7 copy-start.3
  40.3 0.7 copy-start.4
  45.3 9.3 %collective-permute-start.4 = (f32[9,7,8,128]{3,2,1,0:T(8,128)}, f32[9,7,8,128]{3,2,1,0:T(8,128)S(1)}, u32[]{:S(2)}, u32[]{:S(2)}) collective-permute-start(f32[9,7,8,128]{3,2,1,0:T(8,128)} %get-tuple-element.9), channel_id=1, source_target_pairs={{0,64},{64,128},{128,192},{192,256},{256,320},{320,384},{384,448},... | collective-permute-start | bytes 774152 | tf_op jit(solution)/shard_map/ppermute | solution.py:428
  47.8 8.1 %collective-permute-start.5 = (f32[9,7,8,128]{3,2,1,0:T(8,128)}, f32[9,7,8,128]{3,2,1,0:T(8,128)S(1)}, u32[]{:S(2)}, u32[]{:S(2)}) collective-permute-start(f32[9,7,8,128]{3,2,1,0:T(8,128)} %get-tuple-element.10), channel_id=1, source_target_pairs={{64,0},{128,64},{192,128},{256,192},{320,256},{384,320},{448,384},... | collective-permute-start | bytes 774152 | tf_op jit(solution)/shard_map/ppermute | solution.py:429
  54.6 1.3 %copy-start.1 = (f32[9,7,8,128]{3,2,1,0:T(8,128)}, f32[9,7,8,128]{3,2,1,0:T(8,128)S(1)}, u32[]{:S(2)}) copy-start(f32[9,7,8,128]{3,2,1,0:T(8,128)S(1)} %collective-permute-done.4.low) | copy-start | bytes 774148
  55.9 0.7 copy-start.2

commit v3 on v2

--- a/solution.py
+++ b/solution.py
@@ -395,13 +395,21 @@
     return jax.ShapeDtypeStruct(dims, f32)
 
 
+def held(*dims):
+    return pltpu.VMEM(dims, f32)
+
+
+def near(*values):
+    return tuple(pltpu.with_memory_space_constraint(v, pltpu.VMEM) for v in values)
+
+
 def scratch(*dims):
     return pltpu.VMEM(dims, f32)
 
 
 def body(source, sigma_intra, sigma_extra, membrane):
     nx, ny, nz = (lax.axis_size(a) for a in ("gx", "gy", "gz"))
-    packed = pl.pallas_call(pack_kernel, out_shape=shape(8 * ROWS, 128))(
+    packed = pl.pallas_call(pack_kernel, out_shape=held(8 * ROWS, 128))(
         source, sigma_intra, sigma_extra, membrane
     )
     own = lax.all_to_all(packed.reshape(8, ROWS, 128), "gx", 0, 0, tiled=True)
@@ -415,11 +423,11 @@
     planes, first, final = pl.pallas_call(
         plane_kernel,
         out_shape=(
-            shape(FIELDS, FINE, 8, 128),
-            shape(FIELDS, SENT, 8, 128),
-            shape(FIELDS, SENT, 8, 128),
+            held(FIELDS, FINE, 8, 128),
+            held(FIELDS, SENT, 8, 128),
+            held(FIELDS, SENT, 8, 128),
         ),
-    )(own.reshape(-1, 128), *halo)
+    )(*near(own.reshape(-1, 128), *halo))
 
     def place(c):
         return (c % nx) * nz + c // nx
@@ -431,9 +439,9 @@
     sums, fields, images = pl.pallas_call(
         cycle_kernel,
         out_shape=(
-            shape(nx * ny * nz, 128),
-            shape(KRYLOV, 8, 8, 128),
-            shape(KRYLOV + 1, 8, 8, 128),
+            held(nx * ny * nz, 128),
+            held(KRYLOV, 8, 8, 128),
+            held(KRYLOV + 1, 8, 8, 128),
         ),
         scratch_shapes=[
             scratch(6, EXT, 8, 128),
@@ -444,18 +452,18 @@
             scratch(2048, 128),
             scratch(2, 128, 128),
         ],
-    )(planes, low, high)
+    )(*near(planes, low, high))
 
     everyone = ("gx", "gy", "gz")
     got = lax.all_to_all(sums.reshape(-1, 1, 128), everyone, 0, 0, tiled=True)
-    result = pl.pallas_call(solve_kernel, out_shape=shape(8 * FINE, 128))(
-        got.reshape(-1, 128), fields, images
+    result = pl.pallas_call(solve_kernel, out_shape=held(8 * FINE, 128))(
+        *near(got.reshape(-1, 128), fields, images)
     )
     result = lax.all_to_all(result.reshape(8, FINE, 128), "gx", 0, 0, tiled=True)
     return pl.pallas_call(
         unpack_kernel,
         out_shape=(shape(2, 4, 8, 128), shape(2, 4, 8, 128)),
-    )(result.reshape(-1, 128))
+    )(*near(result.reshape(-1, 128)))
 
 
 def solution(mesh):

time: 121 us -> 108 us (0.89)
  Pallas kernels: 20.4 us -> 12.9 us
  blocking collectives: 65.5 us -> 62 us
  local copies, waits for them, and re-layouts: 1.48 us -> 0.02 us
    pallas_call x4, Pallas kernels: 18.9 us -> 12.2 us  [the longest x1 6.92 us: body(): pl.pallas_call(cycle_kernel, out_shape=(held(nx * ny * nz, 128), held(KRY...]
    all_to_all x1, blocking collectives: 12.1 us -> 9.51 us  [body(): lax.all_to_all(result.reshape(8, FINE, 128), 'gx', 0, 0, tiled=True)]
    unnamed x14 -> x0, local copies, waits for them, and re-layouts: 1.46 us -> none
where the time goes in v3:
time: 108 us
  blocking collectives  62 us (57%)
  starting transfers between devices  19.9 us (18%)
  Pallas kernels  12.9 us (12%)
  waiting for transfers between devices  12.3 us (11%)
    all_to_all x1, blocking collectives, body(): got = lax.all_to_all(sums.reshape(-1, 1, 128), everyone, 0, 0, tiled=True)  36.7 us
    all_to_all x1, blocking collectives, body(): own = lax.all_to_all(packed.reshape(8, ROWS, 128), 'gx', 0, 0, tiled=True)  15.8 us
    ppermute x4, starting transfers between devices, from_y(): got = lax.ppermute(value, 'gy', pairs)  12.9 us
    all_to_all x1, blocking collectives, body(): lax.all_to_all(result.reshape(8, FINE, 128), 'gx', 0, 0, tiled=True)  9.51 us
    ppermute x4, waiting for transfers between devices, from_y(): got = lax.ppermute(value, 'gy', pairs)  9.05 us
    pallas_call x1, Pallas kernels, body(): pl.pallas_call(cycle_kernel, out_shape=(held(nx * ny * nz, 128), held(KRY...  6.92 us
    ppermute x1, starting transfers between devices, body(): high = lax.ppermute(first, ('gx', 'gz'), [(b, a) for a, b in up])  4.53 us
    ppermute x1, starting transfers between devices, body(): low = lax.ppermute(final, ('gx', 'gz'), up)  2.46 us
  transfers between devices with their start and end apart: 6, of which 4 were waited for; matrix products, arithmetic and copies ran while one was open for 0% of the time, Pallas kernels for 0%

profile of v3, /device:TPU:1, one launch (start us, length us, event | category | flops | bytes accessed | tf_op | source)
XLA Modules:
  0.0 107.8 jit_solution(58126951241247504)
XLA Ops:
  0.6 1.0 shard_map.59
  1.6 15.8 %all_to_all.15 = f32[8,40,128]{2,1,0:T(8,128)S(1)} all-to-all(f32[8,40,128]{2,1,0:T(8,128)S(1)} %bitcast.14), channel_id=1, replica_groups=mesh['gx'=8,'gy'=8,'gz'=8] {'gx'}, dimensions={0} | all-to-all | bytes 327680 | tf_op jit(solution)/shard_map/all_to_all | solution.py:415
  17.4 3.9 %collective-permute-start.1 = (f32[8,40,128]{2,1,0:T(8,128)S(1)}, f32[8,40,128]{2,1,0:T(8,128)S(1)}, u32[]{:S(2)}, u32[]{:S(2)}) collective-permute-start(f32[8,40,128]{2,1,0:T(8,128)S(1)} %all_to_all.15), channel_id=1, source_target_pairs={{0,8},{8,16},{16,24},{24,32},{32,40},{40,48},{48,56},{1,9},{9,17},... | collective-permute-start | bytes 491528 | tf_op jit(solution)/shard_map/ppermute | solution.py:419
  21.3 1.3 %collective-permute-start = (f32[8,40,128]{2,1,0:T(8,128)S(1)}, f32[8,40,128]{2,1,0:T(8,128)S(1)}, u32[]{:S(2)}, u32[]{:S(2)}) collective-permute-start(f32[8,40,128]{2,1,0:T(8,128)S(1)} %all_to_all.15), channel_id=1, source_target_pairs={{8,0},{16,8},{24,16},{32,24},{40,32},{48,40},{56,48},{9,1},{17,9},... | collective-permute-start | bytes 491528 | tf_op jit(solution)/shard_map/ppermute | solution.py:419
  22.6 6.4 %collective-permute-start.3 = (f32[8,24,128]{2,1,0:T(8,128)S(1)}, f32[8,24,128]{2,1,0:T(8,128)S(1)}, u32[]{:S(2)}, u32[]{:S(2)}) collective-permute-start(f32[8,24,128]{2,1,0:T(8,128)S(1)} %get-tuple-element.14), channel_id=1, source_target_pairs={{0,16},{8,24},{16,32},{24,40},{32,48},{40,56},{1,17},{9,25},{17,33... | collective-permute-start | bytes 294920 | tf_op jit(solution)/shard_map/ppermute | solution.py:419
  29.1 1.3 %collective-permute-start.2 = (f32[8,24,128]{2,1,0:T(8,128)S(1)}, f32[8,24,128]{2,1,0:T(8,128)S(1)}, u32[]{:S(2)}, u32[]{:S(2)}) collective-permute-start(f32[8,24,128]{2,1,0:T(8,128)S(1)} %get-tuple-element.15), channel_id=1, source_target_pairs={{16,0},{24,8},{32,16},{40,24},{48,32},{56,40},{17,1},{25,9},{33,17... | collective-permute-start | bytes 294920 | tf_op jit(solution)/shard_map/ppermute | solution.py:419
  30.4 0.3 collective-permute-done.3
  30.7 8.7 %collective-permute-done.2 = f32[8,24,128]{2,1,0:T(8,128)S(1)} collective-permute-done((f32[8,24,128]{2,1,0:T(8,128)S(1)}, f32[8,24,128]{2,1,0:T(8,128)S(1)}, u32[]{:S(2)}, u32[]{:S(2)}) %collective-permute-start.2) | collective-permute-done | bytes 98336 | tf_op jit(solution)/shard_map/ppermute | solution.py:419
  39.4 0.0 collective-permute-done.1
  39.4 0.0 collective-permute-done
  39.4 2.2 %shard_map.60 = (f32[9,16,8,128]{3,2,1,0:T(8,128)S(1)}, f32[9,7,8,128]{3,2,1,0:T(8,128)S(1)}, f32[9,7,8,128]{3,2,1,0:T(8,128)S(1)}) custom-call(f32[320,128]{1,0:T(8,128)S(1)} %bitcast.12, f32[320,128]{1,0:T(8,128)S(1)} %bitcast.19, f32[320,128]{1,0:T(8,128)S(1)} %bitcast.18, f32[192,128]{1,0:T(8,128)S(1)} %bitcast.21, f32[192,128]{1,0:T(8,128)S(1)} %bitcast.20), custom_call_target="tpu_custom_call" | custom-call | tf_op jit(solution)/shard_map/pallas_call | solution.py:423
  41.6 2.5 %collective-permute-start.4 = (f32[9,7,8,128]{3,2,1,0:T(8,128)S(1)}, f32[9,7,8,128]{3,2,1,0:T(8,128)S(1)}, u32[]{:S(2)}, u32[]{:S(2)}) collective-permute-start(f32[9,7,8,128]{3,2,1,0:T(8,128)S(1)} %get-tuple-element.9), channel_id=1, source_target_pairs={{0,64},{64,128},{128,192},{192,256},{256,320},{320,384},{384,448},... | collective-permute-start | bytes 774152 | tf_op jit(solution)/shard_map/ppermute | solution.py:436
  44.0 4.5 %collective-permute-start.5 = (f32[9,7,8,128]{3,2,1,0:T(8,128)S(1)}, f32[9,7,8,128]{3,2,1,0:T(8,128)S(1)}, u32[]{:S(2)}, u32[]{:S(2)}) collective-permute-start(f32[9,7,8,128]{3,2,1,0:T(8,128)S(1)} %get-tuple-element.10), channel_id=1, source_target_pairs={{64,0},{128,64},{192,128},{256,192},{320,256},{384,320},{448,384},... | collective-permute-start | bytes 774152 | tf_op jit(solution)/shard_map/ppermute | solution.py:437
  48.6 2.1 %collective-permute-done.4.low = f32[9,7,8,128]{3,2,1,0:T(8,128)S(1)} collective-permute-done((f32[9,7,8,128]{3,2,1,0:T(8,128)S(1)}, f32[9,7,8,128]{3,2,1,0:T(8,128)S(1)}, u32[]{:S(2)}, u32[]{:S(2)}) %collective-permute-start.4) | collective-permute-done | bytes 258080 | tf_op jit(solution)/shard_map/ppermute | solution.py:436
  50.7 1.2 %collective-permute-done.5.high = f32[9,7,8,128]{3,2,1,0:T(8,128)S(1)} collective-permute-done((f32[9,7,8,128]{3,2,1,0:T(8,128)S(1)}, f32[9,7,8,128]{3,2,1,0:T(8,128)S(1)}, u32[]{:S(2)}, u32[]{:S(2)}) %collective-permute-start.5) | collective-permute-done | bytes 258080 | tf_op jit(solution)/shard_map/ppermute | solution.py:437
  51.8 6.9 %shard_map.61 = (f32[512,128]{1,0:T(8,128)S(1)}, f32[10,8,8,128]{3,2,1,0:T(8,128)S(1)}, f32[11,8,8,128]{3,2,1,0:T(8,128)S(1)}) custom-call(f32[9,16,8,128]{3,2,1,0:T(8,128)S(1)} %get-tuple-element.8.main, f32[9,7,8,128]{3,2,1,0:T(8,128)S(1)} %collective-permute-done.4.low, f32[9,7,8,128]{3,2,1,0:T(8,128)S(1)} %collective-permute-done.5.high), custom_call_target="tpu_custom_call" | custom-call | tf_op jit(solution)/shard_map/pallas_call | solution.py:439
  58.8 36.7 %all_to_all.16 = f32[512,1,128]{2,1,0:T(1,128)S(1)} all-to-all(f32[512,1,128]{2,1,0:T(1,128)S(1)} %bitcast.16), channel_id=1, replica_groups=mesh['gx'=8,'gy'=8,'gz'=8] {'gx','gy','gz'}, dimensions={0} | all-to-all | bytes 524288 | tf_op jit(solution)/shard_map/all_to_all | solution.py:458
  95.5 2.1 %shard_map.62 = f32[128,128]{1,0:T(8,128)S(1)} custom-call(f32[512,128]{1,0:T(8,128)S(1)} %bitcast.13, f32[10,8,8,128]{3,2,1,0:T(8,128)S(1)} %get-tuple-element.12.fields, f32[11,8,8,128]{3,2,1,0:T(8,128)S(1)} %get-tuple-element.13.images), custom_call_target="tpu_custom_call" | custom-call | tf_op jit(solution)/shard_map/pallas_call | solution.py:459
  97.6 9.5 %all_to_all.17 = f32[8,16,128]{2,1,0:T(8,128)S(1)} all-to-all(f32[8,16,128]{2,1,0:T(8,128)S(1)} %bitcast.15), channel_id=1, replica_groups=mesh['gx'=8,'gy'=8,'gz'=8] {'gx'}, dimensions={0} | all-to-all | bytes 131072 | tf_op jit(solution)/shard_map/all_to_all | solution.py:462
  107.1 0.7 shard_map.63
  (1 shorter events, 0.0 us)
Async XLA Ops:
  17.4 22.0 %collective-permute-start.1 = (f32[8,40,128]{2,1,0:T(8,128)S(1)}, f32[8,40,128]{2,1,0:T(8,128)S(1)}, u32[]{:S(2)}, u32[]{:S(2)}) collective-permute-start(f32[8,40,128]{2,1,0:T(8,128)S(1)} %all_to_all.15), channel_id=1, source_target_pairs={{0,8},{8,16},{16,24},{24,32},{32,40},{40,48},{48,56},{1,9},{9,17},... | collective-permute-start | bytes 491528 | tf_op jit(solution)/shard_map/ppermute | solution.py:419
  21.3 18.1 %collective-permute-start = (f32[8,40,128]{2,1,0:T(8,128)S(1)}, f32[8,40,128]{2,1,0:T(8,128)S(1)}, u32[]{:S(2)}, u32[]{:S(2)}) collective-permute-start(f32[8,40,128]{2,1,0:T(8,128)S(1)} %all_to_all.15), channel_id=1, source_target_pairs={{8,0},{16,8},{24,16},{32,24},{40,32},{48,40},{56,48},{9,1},{17,9},... | collective-permute-start | bytes 491528 | tf_op jit(solution)/shard_map/ppermute | solution.py:419
  22.6 8.1 %collective-permute-start.3 = (f32[8,24,128]{2,1,0:T(8,128)S(1)}, f32[8,24,128]{2,1,0:T(8,128)S(1)}, u32[]{:S(2)}, u32[]{:S(2)}) collective-permute-start(f32[8,24,128]{2,1,0:T(8,128)S(1)} %get-tuple-element.14), channel_id=1, source_target_pairs={{0,16},{8,24},{16,32},{24,40},{32,48},{40,56},{1,17},{9,25},{17,33... | collective-permute-start | bytes 294920 | tf_op jit(solution)/shard_map/ppermute | solution.py:419
  29.1 10.3 %collective-permute-start.2 = (f32[8,24,128]{2,1,0:T(8,128)S(1)}, f32[8,24,128]{2,1,0:T(8,128)S(1)}, u32[]{:S(2)}, u32[]{:S(2)}) collective-permute-start(f32[8,24,128]{2,1,0:T(8,128)S(1)} %get-tuple-element.15), channel_id=1, source_target_pairs={{16,0},{24,8},{32,16},{40,24},{48,32},{56,40},{17,1},{25,9},{33,17... | collective-permute-start | bytes 294920 | tf_op jit(solution)/shard_map/ppermute | solution.py:419
  41.6 9.1 %collective-permute-start.4 = (f32[9,7,8,128]{3,2,1,0:T(8,128)S(1)}, f32[9,7,8,128]{3,2,1,0:T(8,128)S(1)}, u32[]{:S(2)}, u32[]{:S(2)}) collective-permute-start(f32[9,7,8,128]{3,2,1,0:T(8,128)S(1)} %get-tuple-element.9), channel_id=1, source_target_pairs={{0,64},{64,128},{128,192},{192,256},{256,320},{320,384},{384,448},... | collective-permute-start | bytes 774152 | tf_op jit(solution)/shard_map/ppermute | solution.py:436
  44.0 7.8 %collective-permute-start.5 = (f32[9,7,8,128]{3,2,1,0:T(8,128)S(1)}, f32[9,7,8,128]{3,2,1,0:T(8,128)S(1)}, u32[]{:S(2)}, u32[]{:S(2)}) collective-permute-start(f32[9,7,8,128]{3,2,1,0:T(8,128)S(1)} %get-tuple-element.10), channel_id=1, source_target_pairs={{64,0},{128,64},{192,128},{256,192},{320,256},{384,320},{448,384},... | collective-permute-start | bytes 774152 | tf_op jit(solution)/shard_map/ppermute | solution.py:437

commit v4 on v3

--- a/solution.py
+++ b/solution.py
@@ -12,6 +12,8 @@
 SENT = 7
 FIELDS = 9
 ROWS = 40
+BACK = 104
+SUMS = 4 * (2 * KRYLOV + 5)
 UNIQUE = KRYLOV * (KRYLOV + 1) // 2
 f32 = jnp.float32
 
@@ -195,7 +197,7 @@
     return r * (r + 1) // 2 + s
 
 
-def cycle_kernel(main, low, high, sums, fields, images, face, inv, ta, tb, halves, parts, acc):
+def cycle_kernel(main, low, high, sums, back, face, inv, ta, tb, images, halves, parts, acc):
     lane = lanes()
     ix = sublanes() * 4 + lane // 32
     last_x, first_x = ix == 31, ix == 0
@@ -210,6 +212,18 @@
             return main[f, i - DEPTH]
         return far(high, f, i - DEPTH - FINE + 1)
 
+    block = (lane % 32) // 8
+
+    def compact(planes):
+        value = turn(planes[3], 12)
+        for j in (2, 1, 0):
+            value = jnp.where(block == j, turn(planes[j], 8 * j - 12), value)
+        return value
+
+    def send_back(array, g, planes):
+        back[pl.ds(array * 4 + g, 8, stride=BACK), :] = compact(planes)
+
+    blocks_kept = ([], [], [])
     sz = [field(2, 0), field(5, 0)]
     low_z = [None, None]
     for i in range(EXT - 1):
@@ -238,14 +252,13 @@
             inv[1, i] = m * scale
             inv[2, i] = -di * scale
             inv[3, i] = (m + di) * scale
-
-    block = (lane % 32) // 8
-
-    def compact(planes):
-        value = turn(planes[3], 12)
-        for j in (2, 1, 0):
-            value = jnp.where(block == j, turn(planes[j], 8 * j - 12), value)
-        return value
+            if DEPTH <= i < DEPTH + FINE:
+                for n, value in enumerate(((di + de) * scale, -di * scale, (m + di) * scale)):
+                    blocks_kept[n].append(value)
+                if len(blocks_kept[0]) == 4:
+                    for n in range(3):
+                        send_back(2 * KRYLOV + 2 + n, (i - DEPTH) // 4, blocks_kept[n])
+                    blocks_kept = ([], [], [])
 
     def remember(r, at, value):
         images[r, at] = value
@@ -253,7 +266,9 @@
 
     for part in range(2):
         for g in range(FINE // 4):
-            remember(0, part * 4 + g, compact([main[6 + part, 4 * g + j] for j in range(4)]))
+            planes = [main[6 + part, 4 * g + j] for j in range(4)]
+            remember(0, part * 4 + g, compact(planes))
+            send_back(part, g, planes)
 
     buffers = (ta, tb)
 
@@ -282,20 +297,21 @@
             b = (-shared, -(shared + spread(1, i, (before, here, after))))
             if DEPTH <= i < DEPTH + FINE:
                 for part in range(2):
-                    kept[part].append(here[part])
-                    kept[2 + part].append(t_here[part] + b[part])
-                if len(kept[0]) == 4:
-                    g = (i - DEPTH) // 4
-                    for part in range(2):
-                        fields[k, part * 4 + g] = compact(kept[part])
-                        remember(k + 1, part * 4 + g, compact(kept[2 + part]))
-                    kept = ([], [], [], [])
-            if k + 1 < KRYLOV:
+                    kept[part].append(t_here[part] + b[part])
+            for part in range(2):
+                value = b[part]
+                if k > 0:
+                    value = 2.0 * value - vector(k - 1, part, i)
+                if k + 1 < KRYLOV:
+                    buffers[(k + 1) % 2][part, i] = value
+                if DEPTH <= i < DEPTH + FINE:
+                    kept[2 + part].append(value)
+            if len(kept[0]) == 4:
+                g = (i - DEPTH) // 4
                 for part in range(2):
-                    value = b[part]
-                    if k > 0:
-                        value = 2.0 * value - vector(k - 1, part, i)
-                    buffers[(k + 1) % 2][part, i] = value
+                    remember(k + 1, part * 4 + g, compact(kept[part]))
+                    send_back(2 * k + 2 + part, g, kept[2 + part])
+                kept = ([], [], [], [])
             before, here, t_here = here, after, t_after
 
     parts[...] = jnp.zeros((2048, 128), f32)
@@ -326,24 +342,34 @@
     value = fold_sublanes(
         total_of((turned[0][8 * i : 8 * i + 8], turned[1][8 * i : 8 * i + 8]) for i in range(16))
     )
-    whole = (lane < 64) | (lane == 64 + UNIQUE)
-    row = jnp.where(whole, value[0], turn(value[1], 64))
+    row = jnp.where(is_high(), value[0], turn(value[1], 64))
     for i in range(sums.shape[0] // 8):
         sums[pl.ds(8 * i, 8), :] = row
 
 
-def solve_kernel(received, fields, images, out):
-    chunk = 8
-    groups = received.shape[0] // 8
-    value = total_of(
-        total_of(
-            (received[pl.ds(8 * i, 8), :], jnp.zeros((8, 128), f32))
-            for i in range(at, min(at + chunk, groups))
-        )
-        for at in range(0, groups, chunk)
-    )
-    high, error = fold_sublanes(value)
-    error = error + jnp.where(lanes() < UNIQUE, turn(high, 64), 0.0)
+def is_high():
+    return (lanes() < 64) | (lanes() == 64 + UNIQUE)
+
+
+def low_words(error):
+    return turn(jnp.where(lanes() < UNIQUE, error, 0.0), 64)
+
+
+def sum_kernel(received, _, back):
+    zero = jnp.zeros((8, 128), f32)
+    groups = range(received.shape[0] // 8)
+    high, error = fold_sublanes(total_of((received[pl.ds(8 * i, 8), :], zero) for i in groups))
+    row = jnp.where(is_high(), high, high + low_words(error))
+    back[pl.ds(SUMS, 8, stride=BACK), :] = row
+
+
+def solve_kernel(received, solution, residual, rows):
+    def take(array, g):
+        return received[pl.ds(array * 4 + g, 8, stride=BACK), :]
+
+    zero = jnp.zeros((8, 128), f32)
+    high, error = fold_sublanes((received[pl.ds(SUMS, 8, stride=BACK), :], zero))
+    error = jnp.where(lanes() < UNIQUE, error + turn(high, 64), error)
     row, lane = sublanes(16), lanes(16)
     matrix = []
     for n, part in enumerate((high, error)):
@@ -371,24 +397,30 @@
         jnp.broadcast_to(matrix[0][k : k + 1, KRYLOV : KRYLOV + 1], (8, 128))
         for k in range(KRYLOV)
     ]
+    image = [y for y in coeffs] + [jnp.zeros((8, 128), f32)]
+    for k in range(KRYLOV):
+        image[k + 1] = image[k + 1] + (coeffs[k] if k == 0 else 0.5 * coeffs[k])
+        if k > 0:
+            image[k - 1] = image[k - 1] + 0.5 * coeffs[k]
+    image[0] = image[0] - 1.0
     for g in range(FINE // 4):
-        v = []
+        combined, left = [], []
         for part in range(2):
-            v.append(sum(coeffs[k] * fields[k, part * 4 + g] for k in range(KRYLOV)))
-        v[0] = v[0] - v[1]
-        for part in range(2):
-            value = sum(coeffs[k] * images[k + 1, part * 4 + g] for k in range(KRYLOV))
-            v.append(images[0, part * 4 + g] - value)
-        for j, value in enumerate(swap_blocks(v, 8)):
-            out[pl.ds(4 * g + j, 8, stride=FINE), :] = value
-
-
-def unpack_kernel(received, solution, residual):
-    rows = received[...].T
+            vectors = [take(2 * m + part, g) for m in range(KRYLOV + 1)]
+            combined.append(sum(coeffs[k] * vectors[k] for k in range(KRYLOV)))
+            left.append(-sum(image[m] * vectors[m] for m in range(KRYLOV + 1)))
+        b = [take(2 * KRYLOV + 2 + n, g) for n in range(3)]
+        v = [
+            b[0] * combined[0] + b[1] * combined[1],
+            b[1] * combined[0] + b[2] * combined[1],
+        ]
+        for j, value in enumerate(swap_blocks(v + left, 8)):
+            rows[pl.ds(4 * g + j, 8, stride=FINE), :] = value
+    turned = rows[...].T
     for f in range(4):
         ref = solution if f < 2 else residual
         for x in range(4):
-            ref[f % 2, x] = rows[x * 32 + f * 8 : x * 32 + f * 8 + 8]
+            ref[f % 2, x] = turned[x * 32 + f * 8 : x * 32 + f * 8 + 8]
 
 
 def shape(*dims):
@@ -436,34 +468,31 @@
     low = lax.ppermute(final, ("gx", "gz"), up)
     high = lax.ppermute(first, ("gx", "gz"), [(b, a) for a, b in up])
 
-    sums, fields, images = pl.pallas_call(
+    sums, back = pl.pallas_call(
         cycle_kernel,
-        out_shape=(
-            held(nx * ny * nz, 128),
-            held(KRYLOV, 8, 8, 128),
-            held(KRYLOV + 1, 8, 8, 128),
-        ),
+        out_shape=(held(ny * nz, 128), held(8 * BACK, 128)),
         scratch_shapes=[
             scratch(6, EXT, 8, 128),
             scratch(4, EXT, 8, 128),
             scratch(2, EXT, 8, 128),
             scratch(2, EXT, 8, 128),
+            scratch(KRYLOV + 1, 8, 8, 128),
             scratch(2, KRYLOV + 1, 8, 8, 128),
             scratch(2048, 128),
             scratch(2, 128, 128),
         ],
     )(*near(planes, low, high))
 
-    everyone = ("gx", "gy", "gz")
-    got = lax.all_to_all(sums.reshape(-1, 1, 128), everyone, 0, 0, tiled=True)
-    result = pl.pallas_call(solve_kernel, out_shape=held(8 * FINE, 128))(
-        *near(got.reshape(-1, 128), fields, images)
-    )
-    result = lax.all_to_all(result.reshape(8, FINE, 128), "gx", 0, 0, tiled=True)
+    got = lax.all_to_all(sums.reshape(-1, 1, 128), ("gy", "gz"), 0, 0, tiled=True)
+    back = pl.pallas_call(
+        sum_kernel, out_shape=held(8 * BACK, 128), input_output_aliases={1: 0}
+    )(*near(got.reshape(-1, 128), back))
+    got = lax.all_to_all(back.reshape(8, BACK, 128), "gx", 0, 0, tiled=True)
     return pl.pallas_call(
-        unpack_kernel,
+        solve_kernel,
         out_shape=(shape(2, 4, 8, 128), shape(2, 4, 8, 128)),
-    )(*near(result.reshape(-1, 128)))
+        scratch_shapes=[scratch(128, 128)],
+    )(*near(got.reshape(-1, 128)))
 
 
 def solution(mesh):

time: 108 us -> 104 us (0.963)
  blocking collectives: 62 us -> 57.5 us
    all_to_all x2, blocking collectives: 46.2 us -> 41.8 us  [the longest x1 23.4 us: body(): lax.all_to_all(sums.reshape(-1, 1, 128), ('gy', 'gz'), 0, 0, tiled=True)]
where the time goes in v4:
time: 104 us
  blocking collectives  57.5 us (55%)
  starting transfers between devices  19.9 us (19%)
  Pallas kernels  13.4 us (13%)
  waiting for transfers between devices  12.3 us (12%)
    all_to_all x1, blocking collectives, body(): lax.all_to_all(sums.reshape(-1, 1, 128), ('gy', 'gz'), 0, 0, tiled=True)  23.4 us
    all_to_all x1, blocking collectives, body(): got = lax.all_to_all(back.reshape(8, BACK, 128), 'gx', 0, 0, tiled=True)  18.4 us
    all_to_all x1, blocking collectives, body(): own = lax.all_to_all(packed.reshape(8, ROWS, 128), 'gx', 0, 0, tiled=True)  15.8 us
    ppermute x4, starting transfers between devices, from_y(): got = lax.ppermute(value, 'gy', pairs)  12.9 us
    ppermute x4, waiting for transfers between devices, from_y(): got = lax.ppermute(value, 'gy', pairs)  9.05 us
    pallas_call x1, Pallas kernels, body(): pl.pallas_call(cycle_kernel, out_shape=(held(ny * nz, 128), held(8 * BACK...  7.36 us
    ppermute x1, starting transfers between devices, body(): high = lax.ppermute(first, ('gx', 'gz'), [(b, a) for a, b in up])  4.53 us
    pallas_call x1, Pallas kernels, body(): pl.pallas_call(solve_kernel, out_shape=(shape(2, 4, 8, 128), shape(2, 4,...  2.83 us
  transfers between devices with their start and end apart: 6, of which 4 were waited for; matrix products, arithmetic and copies ran while one was open for 0% of the time, Pallas kernels for 0%

profile of v4, /device:TPU:1, one launch (start us, length us, event | category | flops | bytes accessed | tf_op | source)
XLA Modules:
  0.0 103.9 jit_solution(2050490467453012416)
XLA Ops:
  0.6 1.0 shard_map.59
  1.6 15.8 %all_to_all.15 = f32[8,40,128]{2,1,0:T(8,128)S(1)} all-to-all(f32[8,40,128]{2,1,0:T(8,128)S(1)} %bitcast.15), channel_id=1, replica_groups=mesh['gx'=8,'gy'=8,'gz'=8] {'gx'}, dimensions={0} | all-to-all | bytes 327680 | tf_op jit(solution)/shard_map/all_to_all | solution.py:447
  17.4 3.9 %collective-permute-start.1 = (f32[8,40,128]{2,1,0:T(8,128)S(1)}, f32[8,40,128]{2,1,0:T(8,128)S(1)}, u32[]{:S(2)}, u32[]{:S(2)}) collective-permute-start(f32[8,40,128]{2,1,0:T(8,128)S(1)} %all_to_all.15), channel_id=1, source_target_pairs={{0,8},{8,16},{16,24},{24,32},{32,40},{40,48},{48,56},{1,9},{9,17},... | collective-permute-start | bytes 491528 | tf_op jit(solution)/shard_map/ppermute | solution.py:451
  21.3 1.3 %collective-permute-start = (f32[8,40,128]{2,1,0:T(8,128)S(1)}, f32[8,40,128]{2,1,0:T(8,128)S(1)}, u32[]{:S(2)}, u32[]{:S(2)}) collective-permute-start(f32[8,40,128]{2,1,0:T(8,128)S(1)} %all_to_all.15), channel_id=1, source_target_pairs={{8,0},{16,8},{24,16},{32,24},{40,32},{48,40},{56,48},{9,1},{17,9},... | collective-permute-start | bytes 491528 | tf_op jit(solution)/shard_map/ppermute | solution.py:451
  22.6 6.4 %collective-permute-start.3 = (f32[8,24,128]{2,1,0:T(8,128)S(1)}, f32[8,24,128]{2,1,0:T(8,128)S(1)}, u32[]{:S(2)}, u32[]{:S(2)}) collective-permute-start(f32[8,24,128]{2,1,0:T(8,128)S(1)} %get-tuple-element.12), channel_id=1, source_target_pairs={{0,16},{8,24},{16,32},{24,40},{32,48},{40,56},{1,17},{9,25},{17,33... | collective-permute-start | bytes 294920 | tf_op jit(solution)/shard_map/ppermute | solution.py:451
  29.1 1.3 %collective-permute-start.2 = (f32[8,24,128]{2,1,0:T(8,128)S(1)}, f32[8,24,128]{2,1,0:T(8,128)S(1)}, u32[]{:S(2)}, u32[]{:S(2)}) collective-permute-start(f32[8,24,128]{2,1,0:T(8,128)S(1)} %get-tuple-element.13), channel_id=1, source_target_pairs={{16,0},{24,8},{32,16},{40,24},{48,32},{56,40},{17,1},{25,9},{33,17... | collective-permute-start | bytes 294920 | tf_op jit(solution)/shard_map/ppermute | solution.py:451
  30.4 0.3 collective-permute-done.3
  30.7 8.7 %collective-permute-done.2 = f32[8,24,128]{2,1,0:T(8,128)S(1)} collective-permute-done((f32[8,24,128]{2,1,0:T(8,128)S(1)}, f32[8,24,128]{2,1,0:T(8,128)S(1)}, u32[]{:S(2)}, u32[]{:S(2)}) %collective-permute-start.2) | collective-permute-done | bytes 98336 | tf_op jit(solution)/shard_map/ppermute | solution.py:451
  39.4 0.0 collective-permute-done.1
  39.4 0.0 collective-permute-done
  39.4 2.2 %shard_map.60 = (f32[9,16,8,128]{3,2,1,0:T(8,128)S(1)}, f32[9,7,8,128]{3,2,1,0:T(8,128)S(1)}, f32[9,7,8,128]{3,2,1,0:T(8,128)S(1)}) custom-call(f32[320,128]{1,0:T(8,128)S(1)} %bitcast.14, f32[320,128]{1,0:T(8,128)S(1)} %bitcast.17, f32[320,128]{1,0:T(8,128)S(1)} %bitcast.16, f32[192,128]{1,0:T(8,128)S(1)} %bitcast.20, f32[192,128]{1,0:T(8,128)S(1)} %bitcast.19), custom_call_target="tpu_custom_call" | custom-call | tf_op jit(solution)/shard_map/pallas_call | solution.py:455
  41.6 2.5 %collective-permute-start.4 = (f32[9,7,8,128]{3,2,1,0:T(8,128)S(1)}, f32[9,7,8,128]{3,2,1,0:T(8,128)S(1)}, u32[]{:S(2)}, u32[]{:S(2)}) collective-permute-start(f32[9,7,8,128]{3,2,1,0:T(8,128)S(1)} %get-tuple-element.8), channel_id=1, source_target_pairs={{0,64},{64,128},{128,192},{192,256},{256,320},{320,384},{384,448},... | collective-permute-start | bytes 774152 | tf_op jit(solution)/shard_map/ppermute | solution.py:468
  44.0 4.5 %collective-permute-start.5 = (f32[9,7,8,128]{3,2,1,0:T(8,128)S(1)}, f32[9,7,8,128]{3,2,1,0:T(8,128)S(1)}, u32[]{:S(2)}, u32[]{:S(2)}) collective-permute-start(f32[9,7,8,128]{3,2,1,0:T(8,128)S(1)} %get-tuple-element.9), channel_id=1, source_target_pairs={{64,0},{128,64},{192,128},{256,192},{320,256},{384,320},{448,384},... | collective-permute-start | bytes 774152 | tf_op jit(solution)/shard_map/ppermute | solution.py:469
  48.6 2.1 %collective-permute-done.4.low = f32[9,7,8,128]{3,2,1,0:T(8,128)S(1)} collective-permute-done((f32[9,7,8,128]{3,2,1,0:T(8,128)S(1)}, f32[9,7,8,128]{3,2,1,0:T(8,128)S(1)}, u32[]{:S(2)}, u32[]{:S(2)}) %collective-permute-start.4) | collective-permute-done | bytes 258080 | tf_op jit(solution)/shard_map/ppermute | solution.py:468
  50.7 1.2 %collective-permute-done.5.high = f32[9,7,8,128]{3,2,1,0:T(8,128)S(1)} collective-permute-done((f32[9,7,8,128]{3,2,1,0:T(8,128)S(1)}, f32[9,7,8,128]{3,2,1,0:T(8,128)S(1)}, u32[]{:S(2)}, u32[]{:S(2)}) %collective-permute-start.5) | collective-permute-done | bytes 258080 | tf_op jit(solution)/shard_map/ppermute | solution.py:469
  51.8 7.4 %shard_map.61 = (f32[64,128]{1,0:T(8,128)S(1)}, f32[832,128]{1,0:T(8,128)S(1)}) custom-call(f32[9,16,8,128]{3,2,1,0:T(8,128)S(1)} %get-tuple-element.7.main, f32[9,7,8,128]{3,2,1,0:T(8,128)S(1)} %collective-permute-done.4.low, f32[9,7,8,128]{3,2,1,0:T(8,128)S(1)} %collective-permute-done.5.high), custom_call_target="tpu_custom_call" | custom-call | tf_op jit(solution)/shard_map/pallas_call | solution.py:471
  59.2 23.4 %all_to_all.16 = f32[64,1,128]{2,1,0:T(1,128)S(1)} all-to-all(f32[64,1,128]{2,1,0:T(1,128)S(1)} %bitcast.21), channel_id=1, replica_groups=mesh['gx'=8,'gy'=8,'gz'=8] {'gy','gz'}, dimensions={0} | all-to-all | bytes 65536 | tf_op jit(solution)/shard_map/all_to_all | solution.py:486
  82.5 0.1 shard_map.62
  82.6 18.4 %all_to_all.17 = f32[8,104,128]{2,1,0:T(8,128)S(1)} all-to-all(f32[8,104,128]{2,1,0:T(8,128)S(1)} %bitcast.12), channel_id=1, replica_groups=mesh['gx'=8,'gy'=8,'gz'=8] {'gx'}, dimensions={0} | all-to-all | bytes 851968 | tf_op jit(solution)/shard_map/all_to_all | solution.py:490
  101.1 2.8 %shard_map.63 = (f32[2,4,8,128]{3,2,1,0:T(8,128)}, f32[2,4,8,128]{3,2,1,0:T(8,128)}) custom-call(f32[832,128]{1,0:T(8,128)S(1)} %bitcast.13), custom_call_target="tpu_custom_call" | custom-call | tf_op jit(solution)/shard_map/pallas_call | solution.py:491
  (1 shorter events, 0.0 us)
Async XLA Ops:
  17.4 22.0 %collective-permute-start.1 = (f32[8,40,128]{2,1,0:T(8,128)S(1)}, f32[8,40,128]{2,1,0:T(8,128)S(1)}, u32[]{:S(2)}, u32[]{:S(2)}) collective-permute-start(f32[8,40,128]{2,1,0:T(8,128)S(1)} %all_to_all.15), channel_id=1, source_target_pairs={{0,8},{8,16},{16,24},{24,32},{32,40},{40,48},{48,56},{1,9},{9,17},... | collective-permute-start | bytes 491528 | tf_op jit(solution)/shard_map/ppermute | solution.py:451
  21.3 18.1 %collective-permute-start = (f32[8,40,128]{2,1,0:T(8,128)S(1)}, f32[8,40,128]{2,1,0:T(8,128)S(1)}, u32[]{:S(2)}, u32[]{:S(2)}) collective-permute-start(f32[8,40,128]{2,1,0:T(8,128)S(1)} %all_to_all.15), channel_id=1, source_target_pairs={{8,0},{16,8},{24,16},{32,24},{40,32},{48,40},{56,48},{9,1},{17,9},... | collective-permute-start | bytes 491528 | tf_op jit(solution)/shard_map/ppermute | solution.py:451
  22.6 8.1 %collective-permute-start.3 = (f32[8,24,128]{2,1,0:T(8,128)S(1)}, f32[8,24,128]{2,1,0:T(8,128)S(1)}, u32[]{:S(2)}, u32[]{:S(2)}) collective-permute-start(f32[8,24,128]{2,1,0:T(8,128)S(1)} %get-tuple-element.12), channel_id=1, source_target_pairs={{0,16},{8,24},{16,32},{24,40},{32,48},{40,56},{1,17},{9,25},{17,33... | collective-permute-start | bytes 294920 | tf_op jit(solution)/shard_map/ppermute | solution.py:451
  29.1 10.3 %collective-permute-start.2 = (f32[8,24,128]{2,1,0:T(8,128)S(1)}, f32[8,24,128]{2,1,0:T(8,128)S(1)}, u32[]{:S(2)}, u32[]{:S(2)}) collective-permute-start(f32[8,24,128]{2,1,0:T(8,128)S(1)} %get-tuple-element.13), channel_id=1, source_target_pairs={{16,0},{24,8},{32,16},{40,24},{48,32},{56,40},{17,1},{25,9},{33,17... | collective-permute-start | bytes 294920 | tf_op jit(solution)/shard_map/ppermute | solution.py:451
  41.6 9.1 %collective-permute-start.4 = (f32[9,7,8,128]{3,2,1,0:T(8,128)S(1)}, f32[9,7,8,128]{3,2,1,0:T(8,128)S(1)}, u32[]{:S(2)}, u32[]{:S(2)}) collective-permute-start(f32[9,7,8,128]{3,2,1,0:T(8,128)S(1)} %get-tuple-element.8), channel_id=1, source_target_pairs={{0,64},{64,128},{128,192},{192,256},{256,320},{320,384},{384,448},... | collective-permute-start | bytes 774152 | tf_op jit(solution)/shard_map/ppermute | solution.py:468
  44.0 7.8 %collective-permute-start.5 = (f32[9,7,8,128]{3,2,1,0:T(8,128)S(1)}, f32[9,7,8,128]{3,2,1,0:T(8,128)S(1)}, u32[]{:S(2)}, u32[]{:S(2)}) collective-permute-start(f32[9,7,8,128]{3,2,1,0:T(8,128)S(1)} %get-tuple-element.9), channel_id=1, source_target_pairs={{64,0},{128,64},{192,128},{256,192},{320,256},{384,320},{448,384},... | collective-permute-start | bytes 774152 | tf_op jit(solution)/shard_map/ppermute | solution.py:469

commit v5 on v4

--- a/solution.py
+++ b/solution.py
@@ -11,8 +11,8 @@
 EXT = FINE + 2 * DEPTH
 SENT = 7
 FIELDS = 9
-ROWS = 40
-BACK = 104
+ROWS = 36
+BACK = 101
 SUMS = 4 * (2 * KRYLOV + 5)
 UNIQUE = KRYLOV * (KRYLOV + 1) // 2
 f32 = jnp.float32
@@ -93,6 +93,14 @@
     for by in (4, 2, 1):
         a = add_pairs(a, (sink(a[0], by), sink(a[1], by)))
     return quick_sum(*a)
+
+
+def merge(a, b, d):
+    low = (sublanes() & d) == 0
+    return add_pairs(
+        tuple(jnp.where(low, x, y) for x, y in zip(a, b)),
+        tuple(jnp.where(low, sink(x, -d), sink(y, d)) for x, y in zip(a, b)),
+    )
 
 
 def swap_blocks(v, width):
@@ -124,14 +132,16 @@
     for x in range(4):
         last += [membrane[x], empty]
     lower, upper, last = (jnp.concatenate(part, 0).T for part in (lower, upper, last))
-    near = (lanes() % 32) < 8
+    group = (lanes() % 32) // 8
     for j in range(8):
         at = j * ROWS
+        a, b = last[16 * j : 16 * j + 8], last[16 * j + 8 : 16 * j + 16]
+        m = jnp.where(group == 2, turn(b, 16), turn(sink(b, 4), 24))
+        m = jnp.where(group == 1, turn(sink(a, 4), 8), m)
+        m = jnp.where(group == 0, a, m)
         out[pl.ds(at, 16), :] = lower[16 * j : 16 * j + 16]
-        out[pl.ds(at + 16, 8), :] = jnp.where(
-            near, last[16 * j : 16 * j + 8], turn(last[16 * j + 8 : 16 * j + 16], 8)
-        )
-        out[pl.ds(at + 24, 16), :] = upper[16 * j : 16 * j + 16]
+        out[pl.ds(at + 16, 4), :] = m[:4]
+        out[pl.ds(at + 20, 16), :] = upper[16 * j : 16 * j + 16]
 
 
 def plane_kernel(main, above, below, above2, below2, out, first, final):
@@ -142,22 +152,22 @@
 
     def plane(z):
         v = [
-            take(below2, 8 + z, 24),
+            take(below2, 4 + z, 20),
             take(below, z, ROWS),
-            take(below, 24 + z, ROWS),
+            take(below, 20 + z, ROWS),
             take(main, z, ROWS),
-            take(main, 24 + z, ROWS),
+            take(main, 20 + z, ROWS),
             take(above, z, ROWS),
-            take(above, 24 + z, ROWS),
-            take(above2, z, 24),
+            take(above, 20 + z, ROWS),
+            take(above2, z, 20),
         ]
         v = swap_blocks(v, 4)
-        r, shift = z % 8, 8 * (z // 8)
-        m = turn(take(above2, 16 + r, 24), 28 - shift)
+        r, shift = z % 4, 8 * (z // 4)
+        m = turn(take(above2, 16 + r, 20), 28 - shift)
         m = jnp.where(y < 28, turn(take(above, 16 + r, ROWS), 20 - shift), m)
         m = jnp.where(y < 20, turn(take(main, 16 + r, ROWS), 12 - shift), m)
         m = jnp.where(y < 12, turn(take(below, 16 + r, ROWS), 4 - shift), m)
-        m = jnp.where(y < 4, turn(take(below2, r, 24), -4 - shift), m)
+        m = jnp.where(y < 4, turn(take(below2, r, 20), -4 - shift), m)
         return v + [m]
 
     for z in range(FINE):
@@ -197,7 +207,7 @@
     return r * (r + 1) // 2 + s
 
 
-def cycle_kernel(main, low, high, sums, back, face, inv, ta, tb, images, halves, parts, acc):
+def cycle_kernel(main, low, high, sums, back, face, inv, ta, tb, images, halves, acc):
     lane = lanes()
     ix = sublanes() * 4 + lane // 32
     last_x, first_x = ix == 31, ix == 0
@@ -314,28 +324,30 @@
                 kept = ([], [], [], [])
             before, here, t_here = here, after, t_after
 
-    parts[...] = jnp.zeros((2048, 128), f32)
-    for r in range(1, KRYLOV + 1):
-        for s in range(r + 1):
-            terms = []
-            for at in range(8):
-                a, b = images[r, at], images[s, at]
-                ah, al, bh, bl = halves[0, r, at], halves[1, r, at], halves[0, s, at], halves[1, s, at]
-                p = a * b
-                terms.append((p, ((ah * bh - p) + ah * bl + al * bh) + al * bl))
-            value = total_of(terms)
-            slot = slot_of(r - 1, s - 1) * 8
-            parts[pl.ds(slot, 8), :] = value[0]
-            parts[pl.ds(1024 + slot, 8), :] = value[1]
-
+    def product(r, s):
+        terms = []
+        for at in range(8):
+            a, b = images[r, at], images[s, at]
+            ah, al, bh, bl = halves[0, r, at], halves[1, r, at], halves[0, s, at], halves[1, s, at]
+            p = a * b
+            terms.append((p, ((ah * bh - p) + ah * bl + al * bh) + al * bl))
+        return total_of(terms)
+
+    pairs = {
+        slot_of(r - 1, s - 1): (r, s) for r in range(1, KRYLOV + 1) for s in range(r + 1)
+    }
     for group in range(16):
-        value = total_of(
-            (
-                parts[pl.ds(group * 64 + i, 8, stride=8), :],
-                parts[pl.ds(1024 + group * 64 + i, 8, stride=8), :],
-            )
-            for i in range(8)
-        )
+        found = [pairs.get(8 * group + i) for i in range(8)]
+        if None not in found:
+            values = [product(*pair) for pair in found]
+            for d in (4, 2, 1):
+                values = [merge(values[i], values[i + d], d) for i in range(d)]
+            value = values[0]
+        elif any(found):
+            (pair,) = (pair for pair in found if pair)
+            value = fold_sublanes(product(*pair))
+        else:
+            value = (jnp.zeros((8, 128), f32),) * 2
         acc[0, pl.ds(group * 8, 8), :] = value[0]
         acc[1, pl.ds(group * 8, 8), :] = value[1]
     turned = acc[0].T, acc[1].T
@@ -444,14 +456,14 @@
     packed = pl.pallas_call(pack_kernel, out_shape=held(8 * ROWS, 128))(
         source, sigma_intra, sigma_extra, membrane
     )
-    own = lax.all_to_all(packed.reshape(8, ROWS, 128), "gx", 0, 0, tiled=True)
+    own = lax.all_to_all(packed.reshape(8, ROWS, 1, 128), "gx", 0, 0, tiled=True)
 
     def from_y(value, by):
         pairs = [(i, i - by) for i in range(ny) if 0 <= i - by < ny]
         got = lax.ppermute(value, "gy", pairs)
         return got.reshape(-1, 128)
 
-    halo = (from_y(own, 1), from_y(own, -1), from_y(own[:, :24], 2), from_y(own[:, 16:], -2))
+    halo = (from_y(own, 1), from_y(own, -1), from_y(own[:, :20], 2), from_y(own[:, 16:], -2))
     planes, first, final = pl.pallas_call(
         plane_kernel,
         out_shape=(
@@ -478,7 +490,6 @@
             scratch(2, EXT, 8, 128),
             scratch(KRYLOV + 1, 8, 8, 128),
             scratch(2, KRYLOV + 1, 8, 8, 128),
-            scratch(2048, 128),
             scratch(2, 128, 128),
         ],
     )(*near(planes, low, high))
@@ -487,7 +498,7 @@
     back = pl.pallas_call(
         sum_kernel, out_shape=held(8 * BACK, 128), input_output_aliases={1: 0}
     )(*near(got.reshape(-1, 128), back))
-    got = lax.all_to_all(back.reshape(8, BACK, 128), "gx", 0, 0, tiled=True)
+    got = lax.all_to_all(back.reshape(8, BACK, 1, 128), "gx", 0, 0, tiled=True)
     return pl.pallas_call(
         solve_kernel,
         out_shape=(shape(2, 4, 8, 128), shape(2, 4, 8, 128)),

time: 104 us -> 103 us (level)
  no operation moved by 1% of the time
where the time goes in v5:
time: 103 us
  blocking collectives  56.9 us (55%)
  starting transfers between devices  20 us (19%)
  Pallas kernels  13.3 us (13%)
  waiting for transfers between devices  11.9 us (12%)
    all_to_all x1, blocking collectives, body(): lax.all_to_all(sums.reshape(-1, 1, 128), ('gy', 'gz'), 0, 0, tiled=True)  23.1 us
    all_to_all x1, blocking collectives, body(): got = lax.all_to_all(back.reshape(8, BACK, 1, 128), 'gx', 0, 0, tiled=True)  18.2 us
    all_to_all x1, blocking collectives, body(): lax.all_to_all(packed.reshape(8, ROWS, 1, 128), 'gx', 0, 0, tiled=True)  15.6 us
    ppermute x4, starting transfers between devices, from_y(): got = lax.ppermute(value, 'gy', pairs)  12.8 us
    ppermute x4, waiting for transfers between devices, from_y(): got = lax.ppermute(value, 'gy', pairs)  8.7 us
    pallas_call x1, Pallas kernels, body(): pl.pallas_call(cycle_kernel, out_shape=(held(ny * nz, 128), held(8 * BACK...  7.2 us
    ppermute x1, starting transfers between devices, body(): high = lax.ppermute(first, ('gx', 'gz'), [(b, a) for a, b in up])  4.57 us
    pallas_call x1, Pallas kernels, body(): pl.pallas_call(solve_kernel, out_shape=(shape(2, 4, 8, 128), shape(2, 4,...  2.81 us
  transfers between devices with their start and end apart: 6, of which 4 were waited for; matrix products, arithmetic and copies ran while one was open for 0% of the time, Pallas kernels for 0%

profile of v5, /device:TPU:1, one launch (start us, length us, event | category | flops | bytes accessed | tf_op | source)
XLA Modules:
  0.0 102.9 jit_solution(11824655502518066620)
XLA Ops:
  0.6 1.0 shard_map.59
  1.7 15.6 %all_to_all.15 = f32[8,36,1,128]{3,2,1,0:T(1,128)S(1)} all-to-all(f32[8,36,1,128]{3,2,1,0:T(1,128)S(1)} %bitcast.15), channel_id=1, replica_groups=mesh['gx'=8,'gy'=8,'gz'=8] {'gx'}, dimensions={0} | all-to-all | bytes 294912 | tf_op jit(solution)/shard_map/all_to_all | solution.py:459
  17.2 3.8 %collective-permute-start.1 = (f32[8,36,1,128]{3,2,1,0:T(1,128)S(1)}, f32[8,36,1,128]{3,2,1,0:T(1,128)S(1)}, u32[]{:S(2)}, u32[]{:S(2)}) collective-permute-start(f32[8,36,1,128]{3,2,1,0:T(1,128)S(1)} %all_to_all.15), channel_id=1, source_target_pairs={{0,8},{8,16},{16,24},{24,32},{32,40},{40,48},{48,56},{1,9},{9,17},... | collective-permute-start | bytes 442376 | tf_op jit(solution)/shard_map/ppermute | solution.py:463
  21.0 1.3 %collective-permute-start = (f32[8,36,1,128]{3,2,1,0:T(1,128)S(1)}, f32[8,36,1,128]{3,2,1,0:T(1,128)S(1)}, u32[]{:S(2)}, u32[]{:S(2)}) collective-permute-start(f32[8,36,1,128]{3,2,1,0:T(1,128)S(1)} %all_to_all.15), channel_id=1, source_target_pairs={{8,0},{16,8},{24,16},{32,24},{40,32},{48,40},{56,48},{9,1},{17,9},... | collective-permute-start | bytes 442376 | tf_op jit(solution)/shard_map/ppermute | solution.py:463
  22.3 6.4 %collective-permute-start.3 = (f32[8,20,1,128]{3,2,1,0:T(1,128)S(1)}, f32[8,20,1,128]{3,2,1,0:T(1,128)S(1)}, u32[]{:S(2)}, u32[]{:S(2)}) collective-permute-start(f32[8,20,1,128]{3,2,1,0:T(1,128)S(1)} %get-tuple-element.12), channel_id=1, source_target_pairs={{0,16},{8,24},{16,32},{24,40},{32,48},{40,56},{1,17},{9,25},{17,33... | collective-permute-start | bytes 245768 | tf_op jit(solution)/shard_map/ppermute | solution.py:463
  28.8 1.3 %collective-permute-start.2 = (f32[8,20,1,128]{3,2,1,0:T(1,128)S(1)}, f32[8,20,1,128]{3,2,1,0:T(1,128)S(1)}, u32[]{:S(2)}, u32[]{:S(2)}) collective-permute-start(f32[8,20,1,128]{3,2,1,0:T(1,128)S(1)} %get-tuple-element.13), channel_id=1, source_target_pairs={{16,0},{24,8},{32,16},{40,24},{48,32},{56,40},{17,1},{25,9},{33,17... | collective-permute-start | bytes 245768 | tf_op jit(solution)/shard_map/ppermute | solution.py:463
  30.1 0.2 collective-permute-done.3
  30.2 8.5 %collective-permute-done.2 = f32[8,20,1,128]{3,2,1,0:T(1,128)S(1)} collective-permute-done((f32[8,20,1,128]{3,2,1,0:T(1,128)S(1)}, f32[8,20,1,128]{3,2,1,0:T(1,128)S(1)}, u32[]{:S(2)}, u32[]{:S(2)}) %collective-permute-start.2) | collective-permute-done | bytes 81952 | tf_op jit(solution)/shard_map/ppermute | solution.py:463
  38.8 0.0 collective-permute-done.1
  38.8 0.0 collective-permute-done
  38.8 2.2 %shard_map.60 = (f32[9,16,8,128]{3,2,1,0:T(8,128)S(1)}, f32[9,7,8,128]{3,2,1,0:T(8,128)S(1)}, f32[9,7,8,128]{3,2,1,0:T(8,128)S(1)}) custom-call(f32[288,128]{1,0:T(8,128)S(1)} %bitcast.14, f32[288,128]{1,0:T(8,128)S(1)} %bitcast.17, f32[288,128]{1,0:T(8,128)S(1)} %bitcast.16, f32[160,128]{1,0:T(8,128)S(1)} %bitcast.20, f32[160,128]{1,0:T(8,128)S(1)} %bitcast.19), custom_call_target="tpu_custom_call" | custom-call | tf_op jit(solution)/shard_map/pallas_call | solution.py:467
  40.9 2.6 %collective-permute-start.4 = (f32[9,7,8,128]{3,2,1,0:T(8,128)S(1)}, f32[9,7,8,128]{3,2,1,0:T(8,128)S(1)}, u32[]{:S(2)}, u32[]{:S(2)}) collective-permute-start(f32[9,7,8,128]{3,2,1,0:T(8,128)S(1)} %get-tuple-element.8), channel_id=1, source_target_pairs={{0,64},{64,128},{128,192},{192,256},{256,320},{320,384},{384,448},... | collective-permute-start | bytes 774152 | tf_op jit(solution)/shard_map/ppermute | solution.py:480
  43.6 4.6 %collective-permute-start.5 = (f32[9,7,8,128]{3,2,1,0:T(8,128)S(1)}, f32[9,7,8,128]{3,2,1,0:T(8,128)S(1)}, u32[]{:S(2)}, u32[]{:S(2)}) collective-permute-start(f32[9,7,8,128]{3,2,1,0:T(8,128)S(1)} %get-tuple-element.9), channel_id=1, source_target_pairs={{64,0},{128,64},{192,128},{256,192},{320,256},{384,320},{448,384},... | collective-permute-start | bytes 774152 | tf_op jit(solution)/shard_map/ppermute | solution.py:481
  48.2 2.1 %collective-permute-done.4.low = f32[9,7,8,128]{3,2,1,0:T(8,128)S(1)} collective-permute-done((f32[9,7,8,128]{3,2,1,0:T(8,128)S(1)}, f32[9,7,8,128]{3,2,1,0:T(8,128)S(1)}, u32[]{:S(2)}, u32[]{:S(2)}) %collective-permute-start.4) | collective-permute-done | bytes 258080 | tf_op jit(solution)/shard_map/ppermute | solution.py:480
  50.2 1.2 %collective-permute-done.5.high = f32[9,7,8,128]{3,2,1,0:T(8,128)S(1)} collective-permute-done((f32[9,7,8,128]{3,2,1,0:T(8,128)S(1)}, f32[9,7,8,128]{3,2,1,0:T(8,128)S(1)}, u32[]{:S(2)}, u32[]{:S(2)}) %collective-permute-start.5) | collective-permute-done | bytes 258080 | tf_op jit(solution)/shard_map/ppermute | solution.py:481
  51.4 7.2 %shard_map.61 = (f32[64,128]{1,0:T(8,128)S(1)}, f32[808,128]{1,0:T(8,128)S(1)}) custom-call(f32[9,16,8,128]{3,2,1,0:T(8,128)S(1)} %get-tuple-element.7.main, f32[9,7,8,128]{3,2,1,0:T(8,128)S(1)} %collective-permute-done.4.low, f32[9,7,8,128]{3,2,1,0:T(8,128)S(1)} %collective-permute-done.5.high), custom_call_target="tpu_custom_call" | custom-call | tf_op jit(solution)/shard_map/pallas_call | solution.py:483
  58.6 23.1 %all_to_all.16 = f32[64,1,128]{2,1,0:T(1,128)S(1)} all-to-all(f32[64,1,128]{2,1,0:T(1,128)S(1)} %bitcast.21), channel_id=1, replica_groups=mesh['gx'=8,'gy'=8,'gz'=8] {'gy','gz'}, dimensions={0} | all-to-all | bytes 65536 | tf_op jit(solution)/shard_map/all_to_all | solution.py:497
  81.7 0.1 shard_map.62
  81.8 18.2 %all_to_all.17 = f32[8,101,1,128]{3,2,1,0:T(1,128)S(1)} all-to-all(f32[8,101,1,128]{3,2,1,0:T(1,128)S(1)} %bitcast.13), channel_id=1, replica_groups=mesh['gx'=8,'gy'=8,'gz'=8] {'gx'}, dimensions={0} | all-to-all | bytes 827392 | tf_op jit(solution)/shard_map/all_to_all | solution.py:501
  100.0 2.8 %shard_map.63 = (f32[2,4,8,128]{3,2,1,0:T(8,128)}, f32[2,4,8,128]{3,2,1,0:T(8,128)}) custom-call(f32[808,128]{1,0:T(8,128)S(1)} %bitcast.12), custom_call_target="tpu_custom_call" | custom-call | tf_op jit(solution)/shard_map/pallas_call | solution.py:502
  (1 shorter events, 0.0 us)
Async XLA Ops:
  17.2 21.5 %collective-permute-start.1 = (f32[8,36,1,128]{3,2,1,0:T(1,128)S(1)}, f32[8,36,1,128]{3,2,1,0:T(1,128)S(1)}, u32[]{:S(2)}, u32[]{:S(2)}) collective-permute-start(f32[8,36,1,128]{3,2,1,0:T(1,128)S(1)} %all_to_all.15), channel_id=1, source_target_pairs={{0,8},{8,16},{16,24},{24,32},{32,40},{40,48},{48,56},{1,9},{9,17},... | collective-permute-start | bytes 442376 | tf_op jit(solution)/shard_map/ppermute | solution.py:463
  21.0 17.8 %collective-permute-start = (f32[8,36,1,128]{3,2,1,0:T(1,128)S(1)}, f32[8,36,1,128]{3,2,1,0:T(1,128)S(1)}, u32[]{:S(2)}, u32[]{:S(2)}) collective-permute-start(f32[8,36,1,128]{3,2,1,0:T(1,128)S(1)} %all_to_all.15), channel_id=1, source_target_pairs={{8,0},{16,8},{24,16},{32,24},{40,32},{48,40},{56,48},{9,1},{17,9},... | collective-permute-start | bytes 442376 | tf_op jit(solution)/shard_map/ppermute | solution.py:463
  22.3 7.9 %collective-permute-start.3 = (f32[8,20,1,128]{3,2,1,0:T(1,128)S(1)}, f32[8,20,1,128]{3,2,1,0:T(1,128)S(1)}, u32[]{:S(2)}, u32[]{:S(2)}) collective-permute-start(f32[8,20,1,128]{3,2,1,0:T(1,128)S(1)} %get-tuple-element.12), channel_id=1, source_target_pairs={{0,16},{8,24},{16,32},{24,40},{32,48},{40,56},{1,17},{9,25},{17,33... | collective-permute-start | bytes 245768 | tf_op jit(solution)/shard_map/ppermute | solution.py:463
  28.8 10.0 %collective-permute-start.2 = (f32[8,20,1,128]{3,2,1,0:T(1,128)S(1)}, f32[8,20,1,128]{3,2,1,0:T(1,128)S(1)}, u32[]{:S(2)}, u32[]{:S(2)}) collective-permute-start(f32[8,20,1,128]{3,2,1,0:T(1,128)S(1)} %get-tuple-element.13), channel_id=1, source_target_pairs={{16,0},{24,8},{32,16},{40,24},{48,32},{56,40},{17,1},{25,9},{33,17... | collective-permute-start | bytes 245768 | tf_op jit(solution)/shard_map/ppermute | solution.py:463
  40.9 9.3 %collective-permute-start.4 = (f32[9,7,8,128]{3,2,1,0:T(8,128)S(1)}, f32[9,7,8,128]{3,2,1,0:T(8,128)S(1)}, u32[]{:S(2)}, u32[]{:S(2)}) collective-permute-start(f32[9,7,8,128]{3,2,1,0:T(8,128)S(1)} %get-tuple-element.8), channel_id=1, source_target_pairs={{0,64},{64,128},{128,192},{192,256},{256,320},{320,384},{384,448},... | collective-permute-start | bytes 774152 | tf_op jit(solution)/shard_map/ppermute | solution.py:480
  43.6 7.8 %collective-permute-start.5 = (f32[9,7,8,128]{3,2,1,0:T(8,128)S(1)}, f32[9,7,8,128]{3,2,1,0:T(8,128)S(1)}, u32[]{:S(2)}, u32[]{:S(2)}) collective-permute-start(f32[9,7,8,128]{3,2,1,0:T(8,128)S(1)} %get-tuple-element.9), channel_id=1, source_target_pairs={{64,0},{128,64},{192,128},{256,192},{320,256},{384,320},{448,384},... | collective-permute-start | bytes 774152 | tf_op jit(solution)/shard_map/ppermute | solution.py:481

commit v6 on v5

--- a/solution.py
+++ b/solution.py
@@ -3,6 +3,7 @@
 from jax import lax
 from jax.experimental import pallas as pl
 from jax.experimental.pallas import tpu as pltpu
+from jax.sharding import Mesh
 from jax.sharding import PartitionSpec as P
 
 KRYLOV = 10
@@ -12,10 +13,12 @@
 SENT = 7
 FIELDS = 9
 ROWS = 36
+WIDE, THIN = 56, 20
 BACK = 101
 SUMS = 4 * (2 * KRYLOV + 5)
 UNIQUE = KRYLOV * (KRYLOV + 1) // 2
 f32 = jnp.float32
+GY = ("gy_0", "gy_1")
 
 
 def lanes(rows=8):
@@ -134,40 +137,50 @@
     lower, upper, last = (jnp.concatenate(part, 0).T for part in (lower, upper, last))
     group = (lanes() % 32) // 8
     for j in range(8):
-        at = j * ROWS
         a, b = last[16 * j : 16 * j + 8], last[16 * j + 8 : 16 * j + 16]
         m = jnp.where(group == 2, turn(b, 16), turn(sink(b, 4), 24))
         m = jnp.where(group == 1, turn(sink(a, 4), 8), m)
         m = jnp.where(group == 0, a, m)
-        out[pl.ds(at, 16), :] = lower[16 * j : 16 * j + 16]
-        out[pl.ds(at + 16, 4), :] = m[:4]
-        out[pl.ds(at + 20, 16), :] = upper[16 * j : 16 * j + 16]
-
-
-def plane_kernel(main, above, below, above2, below2, out, first, final):
+        for at in (2 * j * ROWS, (2 * j + 1) * ROWS):
+            out[pl.ds(at, 16), :] = lower[16 * j : 16 * j + 16]
+            out[pl.ds(at + 16, 4), :] = m[:4]
+            out[pl.ds(at + 20, 16), :] = upper[16 * j : 16 * j + 16]
+
+
+def choose_kernel(pair, wide, thin):
+    odd = lax.axis_index("gy_1") == 1
+    for s in range(8):
+        at = 2 * ROWS * s
+        rows = pair[pl.ds(at + 16, WIDE), :], pair[pl.ds(at, WIDE), :]
+        wide[pl.ds(WIDE * s, WIDE), :] = jnp.where(odd, *rows)
+        rows = pair[pl.ds(at + 2 * ROWS - THIN, THIN), :], pair[pl.ds(at, THIN), :]
+        thin[pl.ds(THIN * s, THIN), :] = jnp.where(odd, *rows)
+
+
+def plane_kernel(pair, wide, thin, out, first, final):
     y = lanes() % 32
+    odd = lax.axis_index("gy_1")
+    is_even = jnp.full((8, 128), odd, jnp.int32) == 0
 
     def take(ref, row, height):
         return ref[pl.ds(row, 8, stride=height), :]
 
+    def ordered(own, far, last):
+        even = far + own + last
+        other = last + own + far
+        return [a if a is b else jnp.where(is_even, a, b) for a, b in zip(even, other)]
+
     def plane(z):
-        v = [
-            take(below2, 4 + z, 20),
-            take(below, z, ROWS),
-            take(below, 20 + z, ROWS),
-            take(main, z, ROWS),
-            take(main, 20 + z, ROWS),
-            take(above, z, ROWS),
-            take(above, 20 + z, ROWS),
-            take(above2, z, 20),
-        ]
-        v = swap_blocks(v, 4)
+        own = [take(pair, at + z, 2 * ROWS) for at in (0, 20, 36, 56)]
+        far = [take(wide, at + z, WIDE) for at in (4 - 4 * odd, 20, 40 - 4 * odd)]
+        v = swap_blocks(ordered(own, far, [take(thin, 4 * odd + z, THIN)]), 4)
         r, shift = z % 4, 8 * (z // 4)
-        m = turn(take(above2, 16 + r, 20), 28 - shift)
-        m = jnp.where(y < 28, turn(take(above, 16 + r, ROWS), 20 - shift), m)
-        m = jnp.where(y < 20, turn(take(main, 16 + r, ROWS), 12 - shift), m)
-        m = jnp.where(y < 12, turn(take(below, 16 + r, ROWS), 4 - shift), m)
-        m = jnp.where(y < 4, turn(take(below2, r, 20), -4 - shift), m)
+        own = [take(pair, at + r, 2 * ROWS) for at in (16, 52)]
+        far = [take(wide, at + 16 * odd + r, WIDE) for at in (0, 36)]
+        parts = ordered(own, far, [take(thin, 16 - 16 * odd + r, THIN)])
+        m = turn(parts[4], 28 - shift)
+        for n in (3, 2, 1, 0):
+            m = jnp.where(y < 8 * n + 4, turn(parts[n], 8 * n - 4 - shift), m)
         return v + [m]
 
     for z in range(FINE):
@@ -452,18 +465,24 @@
 
 
 def body(source, sigma_intra, sigma_extra, membrane):
-    nx, ny, nz = (lax.axis_size(a) for a in ("gx", "gy", "gz"))
-    packed = pl.pallas_call(pack_kernel, out_shape=held(8 * ROWS, 128))(
+    nx, nz = (lax.axis_size(a) for a in ("gx", "gz"))
+    ny = lax.axis_size(GY)
+    packed = pl.pallas_call(pack_kernel, out_shape=held(16 * ROWS, 128))(
         source, sigma_intra, sigma_extra, membrane
     )
-    own = lax.all_to_all(packed.reshape(8, ROWS, 1, 128), "gx", 0, 0, tiled=True)
-
-    def from_y(value, by):
-        pairs = [(i, i - by) for i in range(ny) if 0 <= i - by < ny]
-        got = lax.ppermute(value, "gy", pairs)
-        return got.reshape(-1, 128)
-
-    halo = (from_y(own, 1), from_y(own, -1), from_y(own[:, :20], 2), from_y(own[:, 16:], -2))
+    pair = lax.all_to_all(packed.reshape(16, ROWS, 1, 128), ("gx", "gy_1"), 0, 0, tiled=True)
+    (pair,) = near(pair.reshape(-1, 128))
+    wide, thin = pl.pallas_call(
+        choose_kernel, out_shape=(held(8 * WIDE, 128), held(8 * THIN, 128))
+    )(pair)
+    across = [(i, i + 1) for i in range(1, ny - 1, 2)]
+    wide = lax.ppermute(wide, GY, across + [(b, a) for a, b in across])
+    thin = lax.ppermute(
+        thin,
+        GY,
+        [(i, i - 2) for i in range(2, ny, 2)] + [(i, i + 2) for i in range(1, ny - 2, 2)],
+    )
+    halo = wide, thin
     planes, first, final = pl.pallas_call(
         plane_kernel,
         out_shape=(
@@ -471,7 +490,7 @@
             held(FIELDS, SENT, 8, 128),
             held(FIELDS, SENT, 8, 128),
         ),
-    )(*near(own.reshape(-1, 128), *halo))
+    )(*near(pair, *halo))
 
     def place(c):
         return (c % nx) * nz + c // nx
@@ -494,7 +513,7 @@
         ],
     )(*near(planes, low, high))
 
-    got = lax.all_to_all(sums.reshape(-1, 1, 128), ("gy", "gz"), 0, 0, tiled=True)
+    got = lax.all_to_all(sums.reshape(-1, 1, 128), GY + ("gz",), 0, 0, tiled=True)
     back = pl.pallas_call(
         sum_kernel, out_shape=held(8 * BACK, 128), input_output_aliases={1: 0}
     )(*near(got.reshape(-1, 128), back))
@@ -507,11 +526,13 @@
 
 
 def solution(mesh):
-    spread = P(None, "gx", "gy", "gz")
+    nx, ny, nz = (mesh.shape[a] for a in ("gx", "gy", "gz"))
+    pairs = Mesh(mesh.devices.reshape(nx, ny // 2, 2, nz), ("gx", *GY, "gz"))
+    spread = P(None, "gx", GY, "gz")
     return jax.shard_map(
         body,
-        mesh=mesh,
-        in_specs=(spread, spread, spread, P("gx", "gy", "gz")),
+        mesh=pairs,
+        in_specs=(spread, spread, spread, P("gx", GY, "gz")),
         out_specs=(spread, spread),
         check_vma=False,
     )

time: 103 us -> 100 us (0.971)
  starting transfers between devices: 20 us -> 8.74 us
  blocking collectives: 56.9 us -> 65 us
    ppermute x4 -> x2, starting transfers between devices: 12.8 us -> 1.97 us  [the longest x1 1.29 us: body(): lax.ppermute(thin, GY, [(i, i - 2) for i in range(2, ny, 2)] + [(i, i + 2...]
    all_to_all x2, blocking collectives: 38.7 us -> 46.8 us  [the longest x1 26.1 us: body(): lax.all_to_all(sums.reshape(-1, 1, 128), GY + ('gz',), 0, 0, tiled=True)]
    ppermute x4 -> x2, waiting for transfers between devices: 8.7 us -> 9.03 us  [the longest x1 9.02 us: body(): lax.ppermute(thin, GY, [(i, i - 2) for i in range(2, ny, 2)] + [(i, i + 2...]
  transfers between devices with their start and end apart: 6 -> 4, of which waited for: 4 -> 3; matrix products, arithmetic and copies ran while one was open for 0% -> 0% of each run, Pallas kernels for 0% -> 0%
where the time goes in v6:
time: 100 us
  blocking collectives  65 us (65%)
  Pallas kernels  13.3 us (13%)
  waiting for transfers between devices  12.3 us (12%)
  starting transfers between devices  8.74 us (9%)
    all_to_all x1, blocking collectives, body(): lax.all_to_all(sums.reshape(-1, 1, 128), GY + ('gz',), 0, 0, tiled=True)  26.1 us
    all_to_all x1, blocking collectives, body(): lax.all_to_all(packed.reshape(16, ROWS, 1, 128), ('gx', 'gy_1'), 0, 0, ti...  20.7 us
    all_to_all x1, blocking collectives, body(): got = lax.all_to_all(back.reshape(8, BACK, 1, 128), 'gx', 0, 0, tiled=True)  18.2 us
    ppermute x1, waiting for transfers between devices, body(): lax.ppermute(thin, GY, [(i, i - 2) for i in range(2, ny, 2)] + [(i, i + 2...  9.02 us
    pallas_call x1, Pallas kernels, body(): pl.pallas_call(cycle_kernel, out_shape=(held(ny * nz, 128), held(8 * BACK...  7.2 us
    ppermute x1, starting transfers between devices, body(): high = lax.ppermute(first, ('gx', 'gz'), [(b, a) for a, b in up])  3.78 us
    ppermute x1, starting transfers between devices, body(): low = lax.ppermute(final, ('gx', 'gz'), up)  2.99 us
    pallas_call x1, Pallas kernels, body(): pl.pallas_call(solve_kernel, out_shape=(shape(2, 4, 8, 128), shape(2, 4,...  2.81 us
  transfers between devices with their start and end apart: 4, of which 3 were waited for; matrix products, arithmetic and copies ran while one was open for 0% of the time, Pallas kernels for 0%

profile of v6, /device:TPU:1, one launch (start us, length us, event | category | flops | bytes accessed | tf_op | source)
XLA Modules:
  0.0 100.0 jit_solution(962438146773043093)
XLA Ops:
  0.6 1.0 %shard_map.59 = f32[576,128]{1,0:T(8,128)S(1)} custom-call(f32[2,4,8,128]{3,2,1,0:T(8,128)} %source.1, f32[3,4,8,128]{3,2,1,0:T(8,128)} %intra.1, f32[3,4,8,128]{3,2,1,0:T(8,128)} %extra.1, f32[4,8,128]{2,1,0:T(8,128)} %membrane.1), custom_call_target="tpu_custom_call" | custom-call | tf_op jit(solution)/shard_map/pallas_call | solution.py:470
  1.7 20.7 %all_to_all.15 = f32[16,36,1,128]{3,2,1,0:T(1,128)S(1)} all-to-all(f32[16,36,1,128]{3,2,1,0:T(1,128)S(1)} %bitcast.12), channel_id=1, replica_groups=mesh['gx'=8,'gy_0'=4,'gy_1'=2,'gz'=8] {'gx','gy_1'}, dimensions={0} | all-to-all | bytes 589824 | tf_op jit(solution)/shard_map/all_to_all | solution.py:473
  22.3 0.7 collective-permute-start
  23.0 1.3 %collective-permute-start.1 = (f32[160,128]{1,0:T(8,128)S(1)}, f32[160,128]{1,0:T(8,128)S(1)}, u32[]{:S(2)}, u32[]{:S(2)}) collective-permute-start(f32[160,128]{1,0:T(8,128)S(1)} %get-tuple-element.10), channel_id=1, source_target_pairs={{16,0},{32,16},{48,32},{8,24},{24,40},{40,56},{17,1},{33,17},{49,3... | collective-permute-start | bytes 245768 | tf_op jit(solution)/shard_map/ppermute | solution.py:480
  24.3 9.0 %collective-permute-done.1.thin = f32[160,128]{1,0:T(8,128)S(1)} collective-permute-done((f32[160,128]{1,0:T(8,128)S(1)}, f32[160,128]{1,0:T(8,128)S(1)}, u32[]{:S(2)}, u32[]{:S(2)}) %collective-permute-start.1) | collective-permute-done | bytes 81952 | tf_op jit(solution)/shard_map/ppermute | solution.py:480
  33.4 0.0 collective-permute-done.wide
  33.4 2.1 %shard_map.61 = (f32[9,16,8,128]{3,2,1,0:T(8,128)S(1)}, f32[9,7,8,128]{3,2,1,0:T(8,128)S(1)}, f32[9,7,8,128]{3,2,1,0:T(8,128)S(1)}) custom-call(f32[576,128]{1,0:T(8,128)S(1)} %bitcast.9, f32[448,128]{1,0:T(8,128)S(1)} %collective-permute-done.wide, f32[160,128]{1,0:T(8,128)S(1)} %collective-permute-done.1.thin), custom_call_target="tpu_custom_call" | custom-call | tf_op jit(solution)/shard_map/pallas_call | solution.py:486
  35.5 3.0 %collective-permute-start.2 = (f32[9,7,8,128]{3,2,1,0:T(8,128)S(1)}, f32[9,7,8,128]{3,2,1,0:T(8,128)S(1)}, u32[]{:S(2)}, u32[]{:S(2)}) collective-permute-start(f32[9,7,8,128]{3,2,1,0:T(8,128)S(1)} %get-tuple-element.12), channel_id=1, source_target_pairs={{0,64},{64,128},{128,192},{192,256},{256,320},{320,384},{384,448},... | collective-permute-start | bytes 774152 | tf_op jit(solution)/shard_map/ppermute | solution.py:499
  38.5 3.8 %collective-permute-start.3 = (f32[9,7,8,128]{3,2,1,0:T(8,128)S(1)}, f32[9,7,8,128]{3,2,1,0:T(8,128)S(1)}, u32[]{:S(2)}, u32[]{:S(2)}) collective-permute-start(f32[9,7,8,128]{3,2,1,0:T(8,128)S(1)} %get-tuple-element.13), channel_id=1, source_target_pairs={{64,0},{128,64},{192,128},{256,192},{320,256},{384,320},{448,384},... | collective-permute-start | bytes 774152 | tf_op jit(solution)/shard_map/ppermute | solution.py:500
  42.3 2.1 %collective-permute-done.2.low = f32[9,7,8,128]{3,2,1,0:T(8,128)S(1)} collective-permute-done((f32[9,7,8,128]{3,2,1,0:T(8,128)S(1)}, f32[9,7,8,128]{3,2,1,0:T(8,128)S(1)}, u32[]{:S(2)}, u32[]{:S(2)}) %collective-permute-start.2) | collective-permute-done | bytes 258080 | tf_op jit(solution)/shard_map/ppermute | solution.py:499
  44.4 1.2 %collective-permute-done.3.high = f32[9,7,8,128]{3,2,1,0:T(8,128)S(1)} collective-permute-done((f32[9,7,8,128]{3,2,1,0:T(8,128)S(1)}, f32[9,7,8,128]{3,2,1,0:T(8,128)S(1)}, u32[]{:S(2)}, u32[]{:S(2)}) %collective-permute-start.3) | collective-permute-done | bytes 258080 | tf_op jit(solution)/shard_map/ppermute | solution.py:500
  45.6 7.2 %shard_map.62 = (f32[64,128]{1,0:T(8,128)S(1)}, f32[808,128]{1,0:T(8,128)S(1)}) custom-call(f32[9,16,8,128]{3,2,1,0:T(8,128)S(1)} %get-tuple-element.11.main, f32[9,7,8,128]{3,2,1,0:T(8,128)S(1)} %collective-permute-done.2.low, f32[9,7,8,128]{3,2,1,0:T(8,128)S(1)} %collective-permute-done.3.high), custom_call_target="tpu_custom_call" | custom-call | tf_op jit(solution)/shard_map/pallas_call | solution.py:502
  52.8 26.1 %all_to_all.16 = f32[64,1,128]{2,1,0:T(1,128)S(1)} all-to-all(f32[64,1,128]{2,1,0:T(1,128)S(1)} %bitcast.14), channel_id=1, replica_groups=mesh['gx'=8,'gy_0'=4,'gy_1'=2,'gz'=8] {'gy_0','gy_1','gz'}, dimensions={0} | all-to-all | bytes 65536 | tf_op jit(solution)/shard_map/all_to_all | solution.py:516
  78.9 0.1 shard_map.63
  79.0 18.2 %all_to_all.17 = f32[8,101,1,128]{3,2,1,0:T(1,128)S(1)} all-to-all(f32[8,101,1,128]{3,2,1,0:T(1,128)S(1)} %bitcast.11), channel_id=1, replica_groups=mesh['gx'=8,'gy_0'=4,'gy_1'=2,'gz'=8] {'gx'}, dimensions={0} | all-to-all | bytes 827392 | tf_op jit(solution)/shard_map/all_to_all | solution.py:520
  97.2 2.8 %shard_map.64 = (f32[2,4,8,128]{3,2,1,0:T(8,128)}, f32[2,4,8,128]{3,2,1,0:T(8,128)}) custom-call(f32[808,128]{1,0:T(8,128)S(1)} %bitcast.10), custom_call_target="tpu_custom_call" | custom-call | tf_op jit(solution)/shard_map/pallas_call | solution.py:521
  (1 shorter events, 0.0 us)
Async XLA Ops:
  22.3 11.0 %collective-permute-start = (f32[448,128]{1,0:T(8,128)S(1)}, f32[448,128]{1,0:T(8,128)S(1)}, u32[]{:S(2)}, u32[]{:S(2)}) collective-permute-start(f32[448,128]{1,0:T(8,128)S(1)} %get-tuple-element.9), channel_id=1, source_target_pairs={{8,16},{24,32},{40,48},{16,8},{32,24},{48,40},{9,17},{25,33},{41,4... | collective-permute-start | bytes 688136 | tf_op jit(solution)/shard_map/ppermute | solution.py:479
  23.0 10.3 %collective-permute-start.1 = (f32[160,128]{1,0:T(8,128)S(1)}, f32[160,128]{1,0:T(8,128)S(1)}, u32[]{:S(2)}, u32[]{:S(2)}) collective-permute-start(f32[160,128]{1,0:T(8,128)S(1)} %get-tuple-element.10), channel_id=1, source_target_pairs={{16,0},{32,16},{48,32},{8,24},{24,40},{40,56},{17,1},{33,17},{49,3... | collective-permute-start | bytes 245768 | tf_op jit(solution)/shard_map/ppermute | solution.py:480
  35.5 8.9 %collective-permute-start.2 = (f32[9,7,8,128]{3,2,1,0:T(8,128)S(1)}, f32[9,7,8,128]{3,2,1,0:T(8,128)S(1)}, u32[]{:S(2)}, u32[]{:S(2)}) collective-permute-start(f32[9,7,8,128]{3,2,1,0:T(8,128)S(1)} %get-tuple-element.12), channel_id=1, source_target_pairs={{0,64},{64,128},{128,192},{192,256},{256,320},{320,384},{384,448},... | collective-permute-start | bytes 774152 | tf_op jit(solution)/shard_map/ppermute | solution.py:499
  38.5 7.1 %collective-permute-start.3 = (f32[9,7,8,128]{3,2,1,0:T(8,128)S(1)}, f32[9,7,8,128]{3,2,1,0:T(8,128)S(1)}, u32[]{:S(2)}, u32[]{:S(2)}) collective-permute-start(f32[9,7,8,128]{3,2,1,0:T(8,128)S(1)} %get-tuple-element.13), channel_id=1, source_target_pairs={{64,0},{128,64},{192,128},{256,192},{320,256},{384,320},{448,384},... | collective-permute-start | bytes 774152 | tf_op jit(solution)/shard_map/ppermute | solution.py:500

commit v7 on v6

--- a/solution.py
+++ b/solution.py
@@ -170,11 +170,11 @@
         other = last + own + far
         return [a if a is b else jnp.where(is_even, a, b) for a, b in zip(even, other)]
 
-    def plane(z):
+    def plane(r, n):
+        z, shift = 4 * n + r, 8 * n
         own = [take(pair, at + z, 2 * ROWS) for at in (0, 20, 36, 56)]
         far = [take(wide, at + z, WIDE) for at in (4 - 4 * odd, 20, 40 - 4 * odd)]
         v = swap_blocks(ordered(own, far, [take(thin, 4 * odd + z, THIN)]), 4)
-        r, shift = z % 4, 8 * (z // 4)
         own = [take(pair, at + r, 2 * ROWS) for at in (16, 52)]
         far = [take(wide, at + 16 * odd + r, WIDE) for at in (0, 36)]
         parts = ordered(own, far, [take(thin, 16 - 16 * odd + r, THIN)])
@@ -183,17 +183,25 @@
             m = jnp.where(y < 8 * n + 4, turn(parts[n], 8 * n - 4 - shift), m)
         return v + [m]
 
-    for z in range(FINE):
-        for f, value in enumerate(plane(z)):
-            out[f, z] = value
-    for ref, at in ((first, lambda d: d - 1), (final, lambda d: FINE - d)):
-        for d in range(1, SENT + 1):
-            near = (y > d) & (y < 31 - d)
-            for f in range(FIELDS):
+    def four(r, _):
+        for n in range(FINE // 4):
+            for f, value in enumerate(plane(r, n)):
+                out[f, 4 * n + r] = value
+        return _
+
+    lax.fori_loop(0, 4, four, 0)
+
+    def edges(f, _):
+        for ref, at in ((first, lambda d: d - 1), (final, lambda d: FINE - d)):
+            for d in range(1, SENT + 1):
                 value = out[f, at(d)]
                 if 2 < d < SENT:
-                    value = jnp.where(near, value, turn(out[f, at(14 - d)], 16))
+                    inner = (y > d) & (y < 31 - d)
+                    value = jnp.where(inner, value, turn(out[f, at(14 - d)], 16))
                 ref[f, d - 1] = value
+        return _
+
+    lax.fori_loop(0, FIELDS, edges, 0)
 
 
 def x_up(v):

time: 100 us -> 100 us (level)
  no operation moved by 1% of the time
where the time goes in v7:
time: 100 us; the launch traced here: 99.7 us
  blocking collectives  65 us (65%)
  Pallas kernels  12.9 us (13%)
  waiting for transfers between devices  12.3 us (12%)
  starting transfers between devices  8.74 us (9%)
    all_to_all x1, blocking collectives, body(): lax.all_to_all(sums.reshape(-1, 1, 128), GY + ('gz',), 0, 0, tiled=True)  26.1 us
    all_to_all x1, blocking collectives, body(): lax.all_to_all(packed.reshape(16, ROWS, 1, 128), ('gx', 'gy_1'), 0, 0, ti...  20.7 us
    all_to_all x1, blocking collectives, body(): got = lax.all_to_all(back.reshape(8, BACK, 1, 128), 'gx', 0, 0, tiled=True)  18.2 us
    ppermute x1, waiting for transfers between devices, body(): lax.ppermute(thin, GY, [(i, i - 2) for i in range(2, ny, 2)] + [(i, i + 2...  9.02 us
    pallas_call x1, Pallas kernels, body(): pl.pallas_call(cycle_kernel, out_shape=(held(ny * nz, 128), held(8 * BACK...  7.2 us
    ppermute x1, starting transfers between devices, body(): high = lax.ppermute(first, ('gx', 'gz'), [(b, a) for a, b in up])  3.78 us
    ppermute x1, starting transfers between devices, body(): low = lax.ppermute(final, ('gx', 'gz'), up)  2.99 us
    pallas_call x1, Pallas kernels, body(): pl.pallas_call(solve_kernel, out_shape=(shape(2, 4, 8, 128), shape(2, 4,...  2.81 us
  transfers between devices with their start and end apart: 4, of which 3 were waited for; matrix products, arithmetic and copies ran while one was open for 0% of the time, Pallas kernels for 0%

profile of v7, /device:TPU:1, one launch (start us, length us, event | category | flops | bytes accessed | tf_op | source)
XLA Modules:
  0.0 99.7 jit_solution(1152944417514542576)
XLA Ops:
  0.6 1.0 %shard_map.59 = f32[576,128]{1,0:T(8,128)S(1)} custom-call(f32[2,4,8,128]{3,2,1,0:T(8,128)} %source.1, f32[3,4,8,128]{3,2,1,0:T(8,128)} %intra.1, f32[3,4,8,128]{3,2,1,0:T(8,128)} %extra.1, f32[4,8,128]{2,1,0:T(8,128)} %membrane.1), custom_call_target="tpu_custom_call" | custom-call | tf_op jit(solution)/shard_map/pallas_call | solution.py:478
  1.7 20.7 %all_to_all.15 = f32[16,36,1,128]{3,2,1,0:T(1,128)S(1)} all-to-all(f32[16,36,1,128]{3,2,1,0:T(1,128)S(1)} %bitcast.12), channel_id=1, replica_groups=mesh['gx'=8,'gy_0'=4,'gy_1'=2,'gz'=8] {'gx','gy_1'}, dimensions={0} | all-to-all | bytes 589824 | tf_op jit(solution)/shard_map/all_to_all | solution.py:481
  22.3 0.7 collective-permute-start
  23.0 1.3 %collective-permute-start.1 = (f32[160,128]{1,0:T(8,128)S(1)}, f32[160,128]{1,0:T(8,128)S(1)}, u32[]{:S(2)}, u32[]{:S(2)}) collective-permute-start(f32[160,128]{1,0:T(8,128)S(1)} %get-tuple-element.10), channel_id=1, source_target_pairs={{16,0},{32,16},{48,32},{8,24},{24,40},{40,56},{17,1},{33,17},{49,3... | collective-permute-start | bytes 245768 | tf_op jit(solution)/shard_map/ppermute | solution.py:488
  24.3 9.0 %collective-permute-done.1.thin = f32[160,128]{1,0:T(8,128)S(1)} collective-permute-done((f32[160,128]{1,0:T(8,128)S(1)}, f32[160,128]{1,0:T(8,128)S(1)}, u32[]{:S(2)}, u32[]{:S(2)}) %collective-permute-start.1) | collective-permute-done | bytes 81952 | tf_op jit(solution)/shard_map/ppermute | solution.py:488
  33.4 0.0 collective-permute-done.wide
  33.4 1.8 %shard_map.61 = (f32[9,16,8,128]{3,2,1,0:T(8,128)S(1)}, f32[9,7,8,128]{3,2,1,0:T(8,128)S(1)}, f32[9,7,8,128]{3,2,1,0:T(8,128)S(1)}) custom-call(f32[576,128]{1,0:T(8,128)S(1)} %bitcast.9, f32[448,128]{1,0:T(8,128)S(1)} %collective-permute-done.wide, f32[160,128]{1,0:T(8,128)S(1)} %collective-permute-done.1.thin), custom_call_target="tpu_custom_call" | custom-call | tf_op jit(solution)/shard_map/pallas_call | solution.py:494
  35.1 3.0 %collective-permute-start.2 = (f32[9,7,8,128]{3,2,1,0:T(8,128)S(1)}, f32[9,7,8,128]{3,2,1,0:T(8,128)S(1)}, u32[]{:S(2)}, u32[]{:S(2)}) collective-permute-start(f32[9,7,8,128]{3,2,1,0:T(8,128)S(1)} %get-tuple-element.12), channel_id=1, source_target_pairs={{0,64},{64,128},{128,192},{192,256},{256,320},{320,384},{384,448},... | collective-permute-start | bytes 774152 | tf_op jit(solution)/shard_map/ppermute | solution.py:507
  38.1 3.8 %collective-permute-start.3 = (f32[9,7,8,128]{3,2,1,0:T(8,128)S(1)}, f32[9,7,8,128]{3,2,1,0:T(8,128)S(1)}, u32[]{:S(2)}, u32[]{:S(2)}) collective-permute-start(f32[9,7,8,128]{3,2,1,0:T(8,128)S(1)} %get-tuple-element.13), channel_id=1, source_target_pairs={{64,0},{128,64},{192,128},{256,192},{320,256},{384,320},{448,384},... | collective-permute-start | bytes 774152 | tf_op jit(solution)/shard_map/ppermute | solution.py:508
  41.9 2.1 %collective-permute-done.2.low = f32[9,7,8,128]{3,2,1,0:T(8,128)S(1)} collective-permute-done((f32[9,7,8,128]{3,2,1,0:T(8,128)S(1)}, f32[9,7,8,128]{3,2,1,0:T(8,128)S(1)}, u32[]{:S(2)}, u32[]{:S(2)}) %collective-permute-start.2) | collective-permute-done | bytes 258080 | tf_op jit(solution)/shard_map/ppermute | solution.py:507
  44.0 1.2 %collective-permute-done.3.high = f32[9,7,8,128]{3,2,1,0:T(8,128)S(1)} collective-permute-done((f32[9,7,8,128]{3,2,1,0:T(8,128)S(1)}, f32[9,7,8,128]{3,2,1,0:T(8,128)S(1)}, u32[]{:S(2)}, u32[]{:S(2)}) %collective-permute-start.3) | collective-permute-done | bytes 258080 | tf_op jit(solution)/shard_map/ppermute | solution.py:508
  45.2 7.2 %shard_map.62 = (f32[64,128]{1,0:T(8,128)S(1)}, f32[808,128]{1,0:T(8,128)S(1)}) custom-call(f32[9,16,8,128]{3,2,1,0:T(8,128)S(1)} %get-tuple-element.11.main, f32[9,7,8,128]{3,2,1,0:T(8,128)S(1)} %collective-permute-done.2.low, f32[9,7,8,128]{3,2,1,0:T(8,128)S(1)} %collective-permute-done.3.high), custom_call_target="tpu_custom_call" | custom-call | tf_op jit(solution)/shard_map/pallas_call | solution.py:510
  52.4 26.1 %all_to_all.16 = f32[64,1,128]{2,1,0:T(1,128)S(1)} all-to-all(f32[64,1,128]{2,1,0:T(1,128)S(1)} %bitcast.14), channel_id=1, replica_groups=mesh['gx'=8,'gy_0'=4,'gy_1'=2,'gz'=8] {'gy_0','gy_1','gz'}, dimensions={0} | all-to-all | bytes 65536 | tf_op jit(solution)/shard_map/all_to_all | solution.py:524
  78.5 0.1 shard_map.63
  78.6 18.2 %all_to_all.17 = f32[8,101,1,128]{3,2,1,0:T(1,128)S(1)} all-to-all(f32[8,101,1,128]{3,2,1,0:T(1,128)S(1)} %bitcast.11), channel_id=1, replica_groups=mesh['gx'=8,'gy_0'=4,'gy_1'=2,'gz'=8] {'gx'}, dimensions={0} | all-to-all | bytes 827392 | tf_op jit(solution)/shard_map/all_to_all | solution.py:528
  96.8 2.8 %shard_map.64 = (f32[2,4,8,128]{3,2,1,0:T(8,128)}, f32[2,4,8,128]{3,2,1,0:T(8,128)}) custom-call(f32[808,128]{1,0:T(8,128)S(1)} %bitcast.10), custom_call_target="tpu_custom_call" | custom-call | tf_op jit(solution)/shard_map/pallas_call | solution.py:529
  (1 shorter events, 0.0 us)
Async XLA Ops:
  22.3 11.0 %collective-permute-start = (f32[448,128]{1,0:T(8,128)S(1)}, f32[448,128]{1,0:T(8,128)S(1)}, u32[]{:S(2)}, u32[]{:S(2)}) collective-permute-start(f32[448,128]{1,0:T(8,128)S(1)} %get-tuple-element.9), channel_id=1, source_target_pairs={{8,16},{24,32},{40,48},{16,8},{32,24},{48,40},{9,17},{25,33},{41,4... | collective-permute-start | bytes 688136 | tf_op jit(solution)/shard_map/ppermute | solution.py:487
  23.0 10.3 %collective-permute-start.1 = (f32[160,128]{1,0:T(8,128)S(1)}, f32[160,128]{1,0:T(8,128)S(1)}, u32[]{:S(2)}, u32[]{:S(2)}) collective-permute-start(f32[160,128]{1,0:T(8,128)S(1)} %get-tuple-element.10), channel_id=1, source_target_pairs={{16,0},{32,16},{48,32},{8,24},{24,40},{40,56},{17,1},{33,17},{49,3... | collective-permute-start | bytes 245768 | tf_op jit(solution)/shard_map/ppermute | solution.py:488
  35.1 8.9 %collective-permute-start.2 = (f32[9,7,8,128]{3,2,1,0:T(8,128)S(1)}, f32[9,7,8,128]{3,2,1,0:T(8,128)S(1)}, u32[]{:S(2)}, u32[]{:S(2)}) collective-permute-start(f32[9,7,8,128]{3,2,1,0:T(8,128)S(1)} %get-tuple-element.12), channel_id=1, source_target_pairs={{0,64},{64,128},{128,192},{192,256},{256,320},{320,384},{384,448},... | collective-permute-start | bytes 774152 | tf_op jit(solution)/shard_map/ppermute | solution.py:507
  38.1 7.1 %collective-permute-start.3 = (f32[9,7,8,128]{3,2,1,0:T(8,128)S(1)}, f32[9,7,8,128]{3,2,1,0:T(8,128)S(1)}, u32[]{:S(2)}, u32[]{:S(2)}) collective-permute-start(f32[9,7,8,128]{3,2,1,0:T(8,128)S(1)} %get-tuple-element.13), channel_id=1, source_target_pairs={{64,0},{128,64},{192,128},{256,192},{320,256},{384,320},{448,384},... | collective-permute-start | bytes 774152 | tf_op jit(solution)/shard_map/ppermute | solution.py:508

commit v8 on v7

--- a/solution.py
+++ b/solution.py
@@ -35,6 +35,17 @@
 
 def sink(v, by):
     return pltpu.roll(v, by % 8, 0)
+
+
+def is_reversed():
+    return lax.axis_index("gz") % 2 == 1
+
+
+def backwards(v):
+    v = sink(v, 4)
+    for d in (2, 1):
+        v = jnp.where((sublanes() & d) == 0, sink(v, -d), sink(v, d))
+    return v
 
 
 def two_sum(a, b):
@@ -136,15 +147,19 @@
         last += [membrane[x], empty]
     lower, upper, last = (jnp.concatenate(part, 0).T for part in (lower, upper, last))
     group = (lanes() % 32) // 8
+    chunks = []
     for j in range(8):
         a, b = last[16 * j : 16 * j + 8], last[16 * j + 8 : 16 * j + 16]
         m = jnp.where(group == 2, turn(b, 16), turn(sink(b, 4), 24))
         m = jnp.where(group == 1, turn(sink(a, 4), 8), m)
         m = jnp.where(group == 0, a, m)
+        chunks.append((lower[16 * j : 16 * j + 16], m, upper[16 * j : 16 * j + 16]))
+    for j in range(8):
+        picked = [jnp.where(is_reversed(), a, b) for a, b in zip(chunks[7 - j], chunks[j])]
         for at in (2 * j * ROWS, (2 * j + 1) * ROWS):
-            out[pl.ds(at, 16), :] = lower[16 * j : 16 * j + 16]
-            out[pl.ds(at + 16, 4), :] = m[:4]
-            out[pl.ds(at + 20, 16), :] = upper[16 * j : 16 * j + 16]
+            out[pl.ds(at, 16), :] = picked[0]
+            out[pl.ds(at + 16, 4), :] = picked[1][:4]
+            out[pl.ds(at + 20, 16), :] = picked[2]
 
 
 def choose_kernel(pair, wide, thin):
@@ -448,6 +463,7 @@
             b[1] * combined[0] + b[2] * combined[1],
         ]
         for j, value in enumerate(swap_blocks(v + left, 8)):
+            value = jnp.where(is_reversed(), backwards(value), value)
             rows[pl.ds(4 * g + j, 8, stride=FINE), :] = value
     turned = rows[...].T
     for f in range(4):
@@ -501,7 +517,8 @@
     )(*near(pair, *halo))
 
     def place(c):
-        return (c % nx) * nz + c // nx
+        block, j = c // nx, c % nx
+        return (j if block % 2 == 0 else nx - 1 - j) * nz + block
 
     up = [(place(c), place(c + 1)) for c in range(nx * nz - 1)]
     low = lax.ppermute(final, ("gx", "gz"), up)

time: 100 us -> 98 us (0.980)
  blocking collectives: 65 us -> 59.3 us
  waiting for transfers between devices: 12.3 us -> 14.7 us
  starting transfers between devices: 8.74 us -> 10 us
    all_to_all x1, blocking collectives: 26.1 us -> 21.5 us  [body(): lax.all_to_all(sums.reshape(-1, 1, 128), GY + ('gz',), 0, 0, tiled=True)]
    ppermute x1, waiting for transfers between devices: 1.21 us -> 4.4 us  [body(): high = lax.ppermute(first, ('gx', 'gz'), [(b, a) for a, b in up])]
    ppermute x1, starting transfers between devices: 2.99 us -> 6.11 us  [body(): low = lax.ppermute(final, ('gx', 'gz'), up)]
    ppermute x1, starting transfers between devices: 3.78 us -> 1.92 us  [body(): high = lax.ppermute(first, ('gx', 'gz'), [(b, a) for a, b in up])]
    all_to_all x1, blocking collectives: 18.2 us -> 17.2 us  [body(): got = lax.all_to_all(back.reshape(8, BACK, 1, 128), 'gx', 0, 0, tiled=True)]
where the time goes in v8:
time: 98 us; the launch traced here: 97.7 us
  blocking collectives  59.3 us (61%)
  waiting for transfers between devices  14.7 us (15%)
  Pallas kernels  12.9 us (13%)
  starting transfers between devices  10 us (10%)
    all_to_all x1, blocking collectives, body(): lax.all_to_all(sums.reshape(-1, 1, 128), GY + ('gz',), 0, 0, tiled=True)  21.5 us
    all_to_all x1, blocking collectives, body(): lax.all_to_all(packed.reshape(16, ROWS, 1, 128), ('gx', 'gy_1'), 0, 0, ti...  20.7 us
    all_to_all x1, blocking collectives, body(): got = lax.all_to_all(back.reshape(8, BACK, 1, 128), 'gx', 0, 0, tiled=True)  17.2 us
    ppermute x1, waiting for transfers between devices, body(): lax.ppermute(thin, GY, [(i, i - 2) for i in range(2, ny, 2)] + [(i, i + 2...  9.02 us
    pallas_call x1, Pallas kernels, body(): pl.pallas_call(cycle_kernel, out_shape=(held(ny * nz, 128), held(8 * BACK...  7.2 us
    ppermute x1, starting transfers between devices, body(): low = lax.ppermute(final, ('gx', 'gz'), up)  6.11 us
    ppermute x1, waiting for transfers between devices, body(): high = lax.ppermute(first, ('gx', 'gz'), [(b, a) for a, b in up])  4.4 us
    pallas_call x1, Pallas kernels, body(): pl.pallas_call(solve_kernel, out_shape=(shape(2, 4, 8, 128), shape(2, 4,...  2.82 us
  transfers between devices with their start and end apart: 4, of which 3 were waited for; matrix products, arithmetic and copies ran while one was open for 0% of the time, Pallas kernels for 0%

profile of v8, /device:TPU:1, one launch (start us, length us, event | category | flops | bytes accessed | tf_op | source)
XLA Modules:
  0.0 97.7 jit_solution(12402050234595937456)
XLA Ops:
  0.6 1.0 %shard_map.59 = f32[576,128]{1,0:T(8,128)S(1)} custom-call(f32[2,4,8,128]{3,2,1,0:T(8,128)} %source.1, f32[3,4,8,128]{3,2,1,0:T(8,128)} %intra.1, f32[3,4,8,128]{3,2,1,0:T(8,128)} %extra.1, f32[4,8,128]{2,1,0:T(8,128)} %membrane.1), custom_call_target="tpu_custom_call" | custom-call | tf_op jit(solution)/shard_map/pallas_call | solution.py:494
  1.7 20.7 %all_to_all.15 = f32[16,36,1,128]{3,2,1,0:T(1,128)S(1)} all-to-all(f32[16,36,1,128]{3,2,1,0:T(1,128)S(1)} %bitcast.12), channel_id=1, replica_groups=mesh['gx'=8,'gy_0'=4,'gy_1'=2,'gz'=8] {'gx','gy_1'}, dimensions={0} | all-to-all | bytes 589824 | tf_op jit(solution)/shard_map/all_to_all | solution.py:497
  22.3 0.7 collective-permute-start
  23.0 1.3 %collective-permute-start.1 = (f32[160,128]{1,0:T(8,128)S(1)}, f32[160,128]{1,0:T(8,128)S(1)}, u32[]{:S(2)}, u32[]{:S(2)}) collective-permute-start(f32[160,128]{1,0:T(8,128)S(1)} %get-tuple-element.10), channel_id=1, source_target_pairs={{16,0},{32,16},{48,32},{8,24},{24,40},{40,56},{17,1},{33,17},{49,3... | collective-permute-start | bytes 245768 | tf_op jit(solution)/shard_map/ppermute | solution.py:504
  24.3 9.0 %collective-permute-done.1.thin = f32[160,128]{1,0:T(8,128)S(1)} collective-permute-done((f32[160,128]{1,0:T(8,128)S(1)}, f32[160,128]{1,0:T(8,128)S(1)}, u32[]{:S(2)}, u32[]{:S(2)}) %collective-permute-start.1) | collective-permute-done | bytes 81952 | tf_op jit(solution)/shard_map/ppermute | solution.py:504
  33.4 0.0 collective-permute-done.wide
  33.4 1.8 %shard_map.61 = (f32[9,16,8,128]{3,2,1,0:T(8,128)S(1)}, f32[9,7,8,128]{3,2,1,0:T(8,128)S(1)}, f32[9,7,8,128]{3,2,1,0:T(8,128)S(1)}) custom-call(f32[576,128]{1,0:T(8,128)S(1)} %bitcast.9, f32[448,128]{1,0:T(8,128)S(1)} %collective-permute-done.wide, f32[160,128]{1,0:T(8,128)S(1)} %collective-permute-done.1.thin), custom_call_target="tpu_custom_call" | custom-call | tf_op jit(solution)/shard_map/pallas_call | solution.py:510
  35.1 6.1 %collective-permute-start.2 = (f32[9,7,8,128]{3,2,1,0:T(8,128)S(1)}, f32[9,7,8,128]{3,2,1,0:T(8,128)S(1)}, u32[]{:S(2)}, u32[]{:S(2)}) collective-permute-start(f32[9,7,8,128]{3,2,1,0:T(8,128)S(1)} %get-tuple-element.12), channel_id=1, source_target_pairs={{0,64},{64,128},{128,192},{192,256},{256,320},{320,384},{384,448},... | collective-permute-start | bytes 774152 | tf_op jit(solution)/shard_map/ppermute | solution.py:524
  41.2 1.9 %collective-permute-start.3 = (f32[9,7,8,128]{3,2,1,0:T(8,128)S(1)}, f32[9,7,8,128]{3,2,1,0:T(8,128)S(1)}, u32[]{:S(2)}, u32[]{:S(2)}) collective-permute-start(f32[9,7,8,128]{3,2,1,0:T(8,128)S(1)} %get-tuple-element.13), channel_id=1, source_target_pairs={{64,0},{128,64},{192,128},{256,192},{320,256},{384,320},{448,384},... | collective-permute-start | bytes 774152 | tf_op jit(solution)/shard_map/ppermute | solution.py:525
  43.2 1.3 %collective-permute-done.2.low = f32[9,7,8,128]{3,2,1,0:T(8,128)S(1)} collective-permute-done((f32[9,7,8,128]{3,2,1,0:T(8,128)S(1)}, f32[9,7,8,128]{3,2,1,0:T(8,128)S(1)}, u32[]{:S(2)}, u32[]{:S(2)}) %collective-permute-start.2) | collective-permute-done | bytes 258080 | tf_op jit(solution)/shard_map/ppermute | solution.py:524
  44.5 4.4 %collective-permute-done.3.high = f32[9,7,8,128]{3,2,1,0:T(8,128)S(1)} collective-permute-done((f32[9,7,8,128]{3,2,1,0:T(8,128)S(1)}, f32[9,7,8,128]{3,2,1,0:T(8,128)S(1)}, u32[]{:S(2)}, u32[]{:S(2)}) %collective-permute-start.3) | collective-permute-done | bytes 258080 | tf_op jit(solution)/shard_map/ppermute | solution.py:525
  48.9 7.2 %shard_map.62 = (f32[64,128]{1,0:T(8,128)S(1)}, f32[808,128]{1,0:T(8,128)S(1)}) custom-call(f32[9,16,8,128]{3,2,1,0:T(8,128)S(1)} %get-tuple-element.11.main, f32[9,7,8,128]{3,2,1,0:T(8,128)S(1)} %collective-permute-done.2.low, f32[9,7,8,128]{3,2,1,0:T(8,128)S(1)} %collective-permute-done.3.high), custom_call_target="tpu_custom_call" | custom-call | tf_op jit(solution)/shard_map/pallas_call | solution.py:527
  56.1 21.5 %all_to_all.16 = f32[64,1,128]{2,1,0:T(1,128)S(1)} all-to-all(f32[64,1,128]{2,1,0:T(1,128)S(1)} %bitcast.14), channel_id=1, replica_groups=mesh['gx'=8,'gy_0'=4,'gy_1'=2,'gz'=8] {'gy_0','gy_1','gz'}, dimensions={0} | all-to-all | bytes 65536 | tf_op jit(solution)/shard_map/all_to_all | solution.py:541
  77.5 0.1 shard_map.63
  77.6 17.2 %all_to_all.17 = f32[8,101,1,128]{3,2,1,0:T(1,128)S(1)} all-to-all(f32[8,101,1,128]{3,2,1,0:T(1,128)S(1)} %bitcast.11), channel_id=1, replica_groups=mesh['gx'=8,'gy_0'=4,'gy_1'=2,'gz'=8] {'gx'}, dimensions={0} | all-to-all | bytes 827392 | tf_op jit(solution)/shard_map/all_to_all | solution.py:545
  94.9 2.8 %shard_map.64 = (f32[2,4,8,128]{3,2,1,0:T(8,128)}, f32[2,4,8,128]{3,2,1,0:T(8,128)}) custom-call(f32[808,128]{1,0:T(8,128)S(1)} %bitcast.10), custom_call_target="tpu_custom_call" | custom-call | tf_op jit(solution)/shard_map/pallas_call | solution.py:546
  (1 shorter events, 0.0 us)
Async XLA Ops:
  22.3 11.0 %collective-permute-start = (f32[448,128]{1,0:T(8,128)S(1)}, f32[448,128]{1,0:T(8,128)S(1)}, u32[]{:S(2)}, u32[]{:S(2)}) collective-permute-start(f32[448,128]{1,0:T(8,128)S(1)} %get-tuple-element.9), channel_id=1, source_target_pairs={{8,16},{24,32},{40,48},{16,8},{32,24},{48,40},{9,17},{25,33},{41,4... | collective-permute-start | bytes 688136 | tf_op jit(solution)/shard_map/ppermute | solution.py:503
  23.0 10.3 %collective-permute-start.1 = (f32[160,128]{1,0:T(8,128)S(1)}, f32[160,128]{1,0:T(8,128)S(1)}, u32[]{:S(2)}, u32[]{:S(2)}) collective-permute-start(f32[160,128]{1,0:T(8,128)S(1)} %get-tuple-element.10), channel_id=1, source_target_pairs={{16,0},{32,16},{48,32},{8,24},{24,40},{40,56},{17,1},{33,17},{49,3... | collective-permute-start | bytes 245768 | tf_op jit(solution)/shard_map/ppermute | solution.py:504
  35.1 9.4 %collective-permute-start.2 = (f32[9,7,8,128]{3,2,1,0:T(8,128)S(1)}, f32[9,7,8,128]{3,2,1,0:T(8,128)S(1)}, u32[]{:S(2)}, u32[]{:S(2)}) collective-permute-start(f32[9,7,8,128]{3,2,1,0:T(8,128)S(1)} %get-tuple-element.12), channel_id=1, source_target_pairs={{0,64},{64,128},{128,192},{192,256},{256,320},{320,384},{384,448},... | collective-permute-start | bytes 774152 | tf_op jit(solution)/shard_map/ppermute | solution.py:524
  41.2 7.6 %collective-permute-start.3 = (f32[9,7,8,128]{3,2,1,0:T(8,128)S(1)}, f32[9,7,8,128]{3,2,1,0:T(8,128)S(1)}, u32[]{:S(2)}, u32[]{:S(2)}) collective-permute-start(f32[9,7,8,128]{3,2,1,0:T(8,128)S(1)} %get-tuple-element.13), channel_id=1, source_target_pairs={{64,0},{128,64},{192,128},{256,192},{320,256},{384,320},{448,384},... | collective-permute-start | bytes 774152 | tf_op jit(solution)/shard_map/ppermute | solution.py:525

commit v9 on v8

--- a/solution.py
+++ b/solution.py
@@ -276,17 +276,17 @@
         diagonals = []
         for s in range(2):
             above = field(s * 3 + 2, i + 1)
-            up_z = 0.5 * (sz[s] + above)
+            up_z = sz[s] + above
             face[s * 3 + 2, i] = up_z
             if i > 0:
                 sx, sy = field(s * 3, i), field(s * 3 + 1, i)
-                up_x = 0.5 * (sx + jnp.where(last_x, 0.0, x_up(sx)))
-                low_x = 0.5 * (sx + jnp.where(first_x, 0.0, x_down(sx)))
-                up_y = 0.5 * (sy + y_up(sy))
-                low_y = 0.5 * (sy + y_down(sy))
+                up_x = sx + jnp.where(last_x, 0.0, x_up(sx))
+                low_x = sx + jnp.where(first_x, 0.0, x_down(sx))
+                up_y = sy + y_up(sy)
+                low_y = sy + y_down(sy)
                 face[s * 3, i] = jnp.where(last_x, 0.0, up_x)
                 face[s * 3 + 1, i] = up_y
-                diagonals.append(up_x + low_x + up_y + low_y + up_z + low_z[s])
+                diagonals.append(0.5 * (up_x + low_x + up_y + low_y + up_z + low_z[s]))
             sz[s], low_z[s] = above, up_z
         if i > 0:
             di, de = diagonals
@@ -294,27 +294,33 @@
             det = m * di + m * de + di * de
             inside = m > 0.0
             scale = jnp.where(inside, 1.0 / jnp.where(inside, det, 1.0), 0.0)
-            inv[0, i] = de * scale
-            inv[1, i] = m * scale
-            inv[2, i] = -di * scale
-            inv[3, i] = (m + di) * scale
+            values = (-de * scale, -m * scale, di * scale, -(m + di) * scale)
+            for n in range(4):
+                inv[n, i] = values[n]
             if DEPTH <= i < DEPTH + FINE:
-                for n, value in enumerate(((di + de) * scale, -di * scale, (m + di) * scale)):
+                for n, value in enumerate(((di + de) * scale, values[2], values[3])):
                     blocks_kept[n].append(value)
                 if len(blocks_kept[0]) == 4:
                     for n in range(3):
                         send_back(2 * KRYLOV + 2 + n, (i - DEPTH) // 4, blocks_kept[n])
                     blocks_kept = ([], [], [])
 
-    def remember(r, at, value):
-        images[r, at] = value
-        halves[0, r, at], halves[1, r, at] = split(value)
-
+    def remember(r, value):
+        size = None
+        for v in value:
+            size = jnp.abs(v) if size is None else jnp.maximum(size, jnp.abs(v))
+        grid = size * 12288.0
+        for at, v in enumerate(value):
+            high_part = (v + grid) - grid
+            images[r, at], halves[0, r, at], halves[1, r, at] = v, high_part, v - high_part
+
+    image = []
     for part in range(2):
         for g in range(FINE // 4):
             planes = [main[6 + part, 4 * g + j] for j in range(4)]
-            remember(0, part * 4 + g, compact(planes))
+            image.append(compact(planes))
             send_back(part, g, planes)
+    remember(0, image)
 
     buffers = (ta, tb)
 
@@ -337,37 +343,39 @@
         start, end = 2 + k, EXT - 2 - k
         (before, _), (here, t_here) = blocks(start - 1), blocks(start)
         kept = ([], [], [], [])
+        image = ([], [])
         for i in range(start, end):
             after, t_after = blocks(i + 1)
             shared = spread(0, i, (before, here, after))
-            b = (-shared, -(shared + spread(1, i, (before, here, after))))
-            if DEPTH <= i < DEPTH + FINE:
-                for part in range(2):
-                    kept[part].append(t_here[part] + b[part])
+            twice = (shared, shared + spread(1, i, (before, here, after)))
             for part in range(2):
-                value = b[part]
-                if k > 0:
-                    value = 2.0 * value - vector(k - 1, part, i)
+                value = 0.5 * twice[part] if k == 0 else twice[part] - vector(k - 1, part, i)
                 if k + 1 < KRYLOV:
                     buffers[(k + 1) % 2][part, i] = value
                 if DEPTH <= i < DEPTH + FINE:
+                    kept[part].append(t_here[part] + 0.5 * twice[part])
                     kept[2 + part].append(value)
             if len(kept[0]) == 4:
                 g = (i - DEPTH) // 4
                 for part in range(2):
-                    remember(k + 1, part * 4 + g, compact(kept[part]))
+                    image[part].append(compact(kept[part]))
                     send_back(2 * k + 2 + part, g, kept[2 + part])
                 kept = ([], [], [], [])
             before, here, t_here = here, after, t_after
+        remember(k + 1, image[0] + image[1])
 
     def product(r, s):
-        terms = []
+        exact, rest = [], []
         for at in range(8):
-            a, b = images[r, at], images[s, at]
-            ah, al, bh, bl = halves[0, r, at], halves[1, r, at], halves[0, s, at], halves[1, s, at]
-            p = a * b
-            terms.append((p, ((ah * bh - p) + ah * bl + al * bh) + al * bl))
-        return total_of(terms)
+            high_a, low_a, high_b, low_b = (
+                halves[n, image, at] for image in (r, s) for n in range(2)
+            )
+            exact.append(high_a * high_b)
+            rest.append(high_a * low_b + low_a * images[s, at])
+        while len(exact) > 1:
+            exact = [a + b for a, b in zip(exact[::2], exact[1::2])]
+            rest = [a + b for a, b in zip(rest[::2], rest[1::2])]
+        return exact[0], rest[0]
 
     pairs = {
         slot_of(r - 1, s - 1): (r, s) for r in range(1, KRYLOV + 1) for s in range(r + 1)
@@ -459,8 +467,8 @@
             left.append(-sum(image[m] * vectors[m] for m in range(KRYLOV + 1)))
         b = [take(2 * KRYLOV + 2 + n, g) for n in range(3)]
         v = [
-            b[0] * combined[0] + b[1] * combined[1],
-            b[1] * combined[0] + b[2] * combined[1],
+            b[0] * combined[0] - b[1] * combined[1],
+            -(b[1] * combined[0] + b[2] * combined[1]),
         ]
         for j, value in enumerate(swap_blocks(v + left, 8)):
             value = jnp.where(is_reversed(), backwards(value), value)

time: 98 us -> 97.8 us (level)
  no operation moved by 1% of the time
where the time goes in v9:
time: 97.8 us; the launch traced here: 97.5 us
  blocking collectives  59.3 us (61%)
  waiting for transfers between devices  14.7 us (15%)
  Pallas kernels  12.7 us (13%)
  starting transfers between devices  10 us (10%)
    all_to_all x1, blocking collectives, body(): lax.all_to_all(sums.reshape(-1, 1, 128), GY + ('gz',), 0, 0, tiled=True)  21.5 us
    all_to_all x1, blocking collectives, body(): lax.all_to_all(packed.reshape(16, ROWS, 1, 128), ('gx', 'gy_1'), 0, 0, ti...  20.7 us
    all_to_all x1, blocking collectives, body(): got = lax.all_to_all(back.reshape(8, BACK, 1, 128), 'gx', 0, 0, tiled=True)  17.2 us
    ppermute x1, waiting for transfers between devices, body(): lax.ppermute(thin, GY, [(i, i - 2) for i in range(2, ny, 2)] + [(i, i + 2...  9.02 us
    pallas_call x1, Pallas kernels, body(): pl.pallas_call(cycle_kernel, out_shape=(held(ny * nz, 128), held(8 * BACK...  7.01 us
    ppermute x1, starting transfers between devices, body(): low = lax.ppermute(final, ('gx', 'gz'), up)  6.11 us
    ppermute x1, waiting for transfers between devices, body(): high = lax.ppermute(first, ('gx', 'gz'), [(b, a) for a, b in up])  4.4 us
    pallas_call x1, Pallas kernels, body(): pl.pallas_call(solve_kernel, out_shape=(shape(2, 4, 8, 128), shape(2, 4,...  2.82 us
  transfers between devices with their start and end apart: 4, of which 3 were waited for; matrix products, arithmetic and copies ran while one was open for 0% of the time, Pallas kernels for 0%

profile of v9, /device:TPU:1, one launch (start us, length us, event | category | flops | bytes accessed | tf_op | source)
XLA Modules:
  0.0 97.5 jit_solution(14299170003216598134)
XLA Ops:
  0.6 1.0 %shard_map.59 = f32[576,128]{1,0:T(8,128)S(1)} custom-call(f32[2,4,8,128]{3,2,1,0:T(8,128)} %source.1, f32[3,4,8,128]{3,2,1,0:T(8,128)} %intra.1, f32[3,4,8,128]{3,2,1,0:T(8,128)} %extra.1, f32[4,8,128]{2,1,0:T(8,128)} %membrane.1), custom_call_target="tpu_custom_call" | custom-call | tf_op jit(solution)/shard_map/pallas_call | solution.py:502
  1.7 20.7 %all_to_all.15 = f32[16,36,1,128]{3,2,1,0:T(1,128)S(1)} all-to-all(f32[16,36,1,128]{3,2,1,0:T(1,128)S(1)} %bitcast.12), channel_id=1, replica_groups=mesh['gx'=8,'gy_0'=4,'gy_1'=2,'gz'=8] {'gx','gy_1'}, dimensions={0} | all-to-all | bytes 589824 | tf_op jit(solution)/shard_map/all_to_all | solution.py:505
  22.3 0.7 collective-permute-start
  23.0 1.3 %collective-permute-start.1 = (f32[160,128]{1,0:T(8,128)S(1)}, f32[160,128]{1,0:T(8,128)S(1)}, u32[]{:S(2)}, u32[]{:S(2)}) collective-permute-start(f32[160,128]{1,0:T(8,128)S(1)} %get-tuple-element.10), channel_id=1, source_target_pairs={{16,0},{32,16},{48,32},{8,24},{24,40},{40,56},{17,1},{33,17},{49,3... | collective-permute-start | bytes 245768 | tf_op jit(solution)/shard_map/ppermute | solution.py:512
  24.3 9.0 %collective-permute-done.1.thin = f32[160,128]{1,0:T(8,128)S(1)} collective-permute-done((f32[160,128]{1,0:T(8,128)S(1)}, f32[160,128]{1,0:T(8,128)S(1)}, u32[]{:S(2)}, u32[]{:S(2)}) %collective-permute-start.1) | collective-permute-done | bytes 81952 | tf_op jit(solution)/shard_map/ppermute | solution.py:512
  33.4 0.0 collective-permute-done.wide
  33.4 1.8 %shard_map.61 = (f32[9,16,8,128]{3,2,1,0:T(8,128)S(1)}, f32[9,7,8,128]{3,2,1,0:T(8,128)S(1)}, f32[9,7,8,128]{3,2,1,0:T(8,128)S(1)}) custom-call(f32[576,128]{1,0:T(8,128)S(1)} %bitcast.9, f32[448,128]{1,0:T(8,128)S(1)} %collective-permute-done.wide, f32[160,128]{1,0:T(8,128)S(1)} %collective-permute-done.1.thin), custom_call_target="tpu_custom_call" | custom-call | tf_op jit(solution)/shard_map/pallas_call | solution.py:518
  35.1 6.1 %collective-permute-start.2 = (f32[9,7,8,128]{3,2,1,0:T(8,128)S(1)}, f32[9,7,8,128]{3,2,1,0:T(8,128)S(1)}, u32[]{:S(2)}, u32[]{:S(2)}) collective-permute-start(f32[9,7,8,128]{3,2,1,0:T(8,128)S(1)} %get-tuple-element.12), channel_id=1, source_target_pairs={{0,64},{64,128},{128,192},{192,256},{256,320},{320,384},{384,448},... | collective-permute-start | bytes 774152 | tf_op jit(solution)/shard_map/ppermute | solution.py:532
  41.2 1.9 %collective-permute-start.3 = (f32[9,7,8,128]{3,2,1,0:T(8,128)S(1)}, f32[9,7,8,128]{3,2,1,0:T(8,128)S(1)}, u32[]{:S(2)}, u32[]{:S(2)}) collective-permute-start(f32[9,7,8,128]{3,2,1,0:T(8,128)S(1)} %get-tuple-element.13), channel_id=1, source_target_pairs={{64,0},{128,64},{192,128},{256,192},{320,256},{384,320},{448,384},... | collective-permute-start | bytes 774152 | tf_op jit(solution)/shard_map/ppermute | solution.py:533
  43.2 1.3 %collective-permute-done.2.low = f32[9,7,8,128]{3,2,1,0:T(8,128)S(1)} collective-permute-done((f32[9,7,8,128]{3,2,1,0:T(8,128)S(1)}, f32[9,7,8,128]{3,2,1,0:T(8,128)S(1)}, u32[]{:S(2)}, u32[]{:S(2)}) %collective-permute-start.2) | collective-permute-done | bytes 258080 | tf_op jit(solution)/shard_map/ppermute | solution.py:532
  44.5 4.4 %collective-permute-done.3.high = f32[9,7,8,128]{3,2,1,0:T(8,128)S(1)} collective-permute-done((f32[9,7,8,128]{3,2,1,0:T(8,128)S(1)}, f32[9,7,8,128]{3,2,1,0:T(8,128)S(1)}, u32[]{:S(2)}, u32[]{:S(2)}) %collective-permute-start.3) | collective-permute-done | bytes 258080 | tf_op jit(solution)/shard_map/ppermute | solution.py:533
  48.9 7.0 %shard_map.62 = (f32[64,128]{1,0:T(8,128)S(1)}, f32[808,128]{1,0:T(8,128)S(1)}) custom-call(f32[9,16,8,128]{3,2,1,0:T(8,128)S(1)} %get-tuple-element.11.main, f32[9,7,8,128]{3,2,1,0:T(8,128)S(1)} %collective-permute-done.2.low, f32[9,7,8,128]{3,2,1,0:T(8,128)S(1)} %collective-permute-done.3.high), custom_call_target="tpu_custom_call" | custom-call | tf_op jit(solution)/shard_map/pallas_call | solution.py:535
  55.9 21.5 %all_to_all.16 = f32[64,1,128]{2,1,0:T(1,128)S(1)} all-to-all(f32[64,1,128]{2,1,0:T(1,128)S(1)} %bitcast.14), channel_id=1, replica_groups=mesh['gx'=8,'gy_0'=4,'gy_1'=2,'gz'=8] {'gy_0','gy_1','gz'}, dimensions={0} | all-to-all | bytes 65536 | tf_op jit(solution)/shard_map/all_to_all | solution.py:549
  77.4 0.1 shard_map.63
  77.4 17.2 %all_to_all.17 = f32[8,101,1,128]{3,2,1,0:T(1,128)S(1)} all-to-all(f32[8,101,1,128]{3,2,1,0:T(1,128)S(1)} %bitcast.11), channel_id=1, replica_groups=mesh['gx'=8,'gy_0'=4,'gy_1'=2,'gz'=8] {'gx'}, dimensions={0} | all-to-all | bytes 827392 | tf_op jit(solution)/shard_map/all_to_all | solution.py:553
  94.7 2.8 %shard_map.64 = (f32[2,4,8,128]{3,2,1,0:T(8,128)}, f32[2,4,8,128]{3,2,1,0:T(8,128)}) custom-call(f32[808,128]{1,0:T(8,128)S(1)} %bitcast.10), custom_call_target="tpu_custom_call" | custom-call | tf_op jit(solution)/shard_map/pallas_call | solution.py:554
  (1 shorter events, 0.0 us)
Async XLA Ops:
  22.3 11.0 %collective-permute-start = (f32[448,128]{1,0:T(8,128)S(1)}, f32[448,128]{1,0:T(8,128)S(1)}, u32[]{:S(2)}, u32[]{:S(2)}) collective-permute-start(f32[448,128]{1,0:T(8,128)S(1)} %get-tuple-element.9), channel_id=1, source_target_pairs={{8,16},{24,32},{40,48},{16,8},{32,24},{48,40},{9,17},{25,33},{41,4... | collective-permute-start | bytes 688136 | tf_op jit(solution)/shard_map/ppermute | solution.py:511
  23.0 10.3 %collective-permute-start.1 = (f32[160,128]{1,0:T(8,128)S(1)}, f32[160,128]{1,0:T(8,128)S(1)}, u32[]{:S(2)}, u32[]{:S(2)}) collective-permute-start(f32[160,128]{1,0:T(8,128)S(1)} %get-tuple-element.10), channel_id=1, source_target_pairs={{16,0},{32,16},{48,32},{8,24},{24,40},{40,56},{17,1},{33,17},{49,3... | collective-permute-start | bytes 245768 | tf_op jit(solution)/shard_map/ppermute | solution.py:512
  35.1 9.4 %collective-permute-start.2 = (f32[9,7,8,128]{3,2,1,0:T(8,128)S(1)}, f32[9,7,8,128]{3,2,1,0:T(8,128)S(1)}, u32[]{:S(2)}, u32[]{:S(2)}) collective-permute-start(f32[9,7,8,128]{3,2,1,0:T(8,128)S(1)} %get-tuple-element.12), channel_id=1, source_target_pairs={{0,64},{64,128},{128,192},{192,256},{256,320},{320,384},{384,448},... | collective-permute-start | bytes 774152 | tf_op jit(solution)/shard_map/ppermute | solution.py:532
  41.2 7.6 %collective-permute-start.3 = (f32[9,7,8,128]{3,2,1,0:T(8,128)S(1)}, f32[9,7,8,128]{3,2,1,0:T(8,128)S(1)}, u32[]{:S(2)}, u32[]{:S(2)}) collective-permute-start(f32[9,7,8,128]{3,2,1,0:T(8,128)S(1)} %get-tuple-element.13), channel_id=1, source_target_pairs={{64,0},{128,64},{192,128},{256,192},{320,256},{384,320},{448,384},... | collective-permute-start | bytes 774152 | tf_op jit(solution)/shard_map/ppermute | solution.py:533

commit v10 on v9

--- a/solution.py
+++ b/solution.py
@@ -14,7 +14,7 @@
 FIELDS = 9
 ROWS = 36
 WIDE, THIN = 56, 20
-BACK = 101
+BACK = 102
 SUMS = 4 * (2 * KRYLOV + 5)
 UNIQUE = KRYLOV * (KRYLOV + 1) // 2
 f32 = jnp.float32
@@ -239,7 +239,7 @@
 
 def slot_of(r, s):
     if s < 0:
-        return UNIQUE + r if r < KRYLOV - 1 else 64 + UNIQUE
+        return UNIQUE + r
     return r * (r + 1) // 2 + s
 
 
@@ -398,34 +398,31 @@
     value = fold_sublanes(
         total_of((turned[0][8 * i : 8 * i + 8], turned[1][8 * i : 8 * i + 8]) for i in range(16))
     )
-    row = jnp.where(is_high(), value[0], turn(value[1], 64))
+    rows = jnp.where(sublanes() % 2 == 0, *value)
     for i in range(sums.shape[0] // 8):
-        sums[pl.ds(8 * i, 8), :] = row
-
-
-def is_high():
-    return (lanes() < 64) | (lanes() == 64 + UNIQUE)
-
-
-def low_words(error):
-    return turn(jnp.where(lanes() < UNIQUE, error, 0.0), 64)
+        sums[pl.ds(8 * i, 8), :] = rows
 
 
 def sum_kernel(received, _, back):
     zero = jnp.zeros((8, 128), f32)
     groups = range(received.shape[0] // 8)
-    high, error = fold_sublanes(total_of((received[pl.ds(8 * i, 8), :], zero) for i in groups))
-    row = jnp.where(is_high(), high, high + low_words(error))
-    back[pl.ds(SUMS, 8, stride=BACK), :] = row
+    value = total_of((received[pl.ds(8 * i, 8), :], zero) for i in groups)
+    for by in (4, 2):
+        value = add_pairs(value, (sink(value[0], by), sink(value[1], by)))
+    high, error = value
+    value = quick_sum(high, error + sink(high, -1))
+    even = sublanes() % 2 == 0
+    for n in range(2):
+        back[pl.ds(SUMS + n, 8, stride=BACK), :] = jnp.where(even, value[n], sink(value[n], 1))
 
 
 def solve_kernel(received, solution, residual, rows):
     def take(array, g):
         return received[pl.ds(array * 4 + g, 8, stride=BACK), :]
 
-    zero = jnp.zeros((8, 128), f32)
-    high, error = fold_sublanes((received[pl.ds(SUMS, 8, stride=BACK), :], zero))
-    error = jnp.where(lanes() < UNIQUE, error + turn(high, 64), error)
+    high, error = fold_sublanes(
+        tuple(received[pl.ds(SUMS + n, 8, stride=BACK), :] for n in range(2))
+    )
     row, lane = sublanes(16), lanes(16)
     matrix = []
     for n, part in enumerate((high, error)):
@@ -534,7 +531,7 @@
 
     sums, back = pl.pallas_call(
         cycle_kernel,
-        out_shape=(held(ny * nz, 128), held(8 * BACK, 128)),
+        out_shape=(held(2 * ny * nz, 128), held(8 * BACK, 128)),
         scratch_shapes=[
             scratch(6, EXT, 8, 128),
             scratch(4, EXT, 8, 128),
@@ -546,7 +543,7 @@
         ],
     )(*near(planes, low, high))
 
-    got = lax.all_to_all(sums.reshape(-1, 1, 128), GY + ("gz",), 0, 0, tiled=True)
+    got = lax.all_to_all(sums.reshape(-1, 2, 128), GY + ("gz",), 0, 0, tiled=True)
     back = pl.pallas_call(
         sum_kernel, out_shape=held(8 * BACK, 128), input_output_aliases={1: 0}
     )(*near(got.reshape(-1, 128), back))

time: 97.8 us -> 99.1 us (1.013)
  blocking collectives: 59.3 us -> 60.7 us
where the time goes in v10:
time: 99.1 us; the launch traced here: 98.7 us
  blocking collectives  60.7 us (61%)
  waiting for transfers between devices  14.7 us (15%)
  Pallas kernels  12.6 us (13%)
  starting transfers between devices  10 us (10%)
    all_to_all x1, blocking collectives, body(): lax.all_to_all(sums.reshape(-1, 2, 128), GY + ('gz',), 0, 0, tiled=True)  22.1 us
    all_to_all x1, blocking collectives, body(): lax.all_to_all(packed.reshape(16, ROWS, 1, 128), ('gx', 'gy_1'), 0, 0, ti...  20.7 us
    all_to_all x1, blocking collectives, body(): got = lax.all_to_all(back.reshape(8, BACK, 1, 128), 'gx', 0, 0, tiled=True)  17.9 us
    ppermute x1, waiting for transfers between devices, body(): lax.ppermute(thin, GY, [(i, i - 2) for i in range(2, ny, 2)] + [(i, i + 2...  9.02 us
    pallas_call x1, Pallas kernels, body(): pl.pallas_call(cycle_kernel, out_shape=(held(2 * ny * nz, 128), held(8 *...  6.96 us
    ppermute x1, starting transfers between devices, body(): low = lax.ppermute(final, ('gx', 'gz'), up)  6.11 us
    ppermute x1, waiting for transfers between devices, body(): high = lax.ppermute(first, ('gx', 'gz'), [(b, a) for a, b in up])  4.4 us
    pallas_call x1, Pallas kernels, body(): pl.pallas_call(solve_kernel, out_shape=(shape(2, 4, 8, 128), shape(2, 4,...  2.78 us
  transfers between devices with their start and end apart: 4, of which 3 were waited for; matrix products, arithmetic and copies ran while one was open for 0% of the time, Pallas kernels for 0%

profile of v10, /device:TPU:1, one launch (start us, length us, event | category | flops | bytes accessed | tf_op | source)
XLA Modules:
  0.0 98.7 jit_solution(8003180586000625839)
XLA Ops:
  0.6 1.0 %shard_map.59 = f32[576,128]{1,0:T(8,128)S(1)} custom-call(f32[2,4,8,128]{3,2,1,0:T(8,128)} %source.1, f32[3,4,8,128]{3,2,1,0:T(8,128)} %intra.1, f32[3,4,8,128]{3,2,1,0:T(8,128)} %extra.1, f32[4,8,128]{2,1,0:T(8,128)} %membrane.1), custom_call_target="tpu_custom_call" | custom-call | tf_op jit(solution)/shard_map/pallas_call | solution.py:499
  1.7 20.7 %all_to_all.15 = f32[16,36,1,128]{3,2,1,0:T(1,128)S(1)} all-to-all(f32[16,36,1,128]{3,2,1,0:T(1,128)S(1)} %bitcast.10), channel_id=1, replica_groups=mesh['gx'=8,'gy_0'=4,'gy_1'=2,'gz'=8] {'gx','gy_1'}, dimensions={0} | all-to-all | bytes 589824 | tf_op jit(solution)/shard_map/all_to_all | solution.py:502
  22.3 0.7 collective-permute-start
  23.0 1.3 %collective-permute-start.1 = (f32[160,128]{1,0:T(8,128)S(1)}, f32[160,128]{1,0:T(8,128)S(1)}, u32[]{:S(2)}, u32[]{:S(2)}) collective-permute-start(f32[160,128]{1,0:T(8,128)S(1)} %get-tuple-element.10), channel_id=1, source_target_pairs={{16,0},{32,16},{48,32},{8,24},{24,40},{40,56},{17,1},{33,17},{49,3... | collective-permute-start | bytes 245768 | tf_op jit(solution)/shard_map/ppermute | solution.py:509
  24.3 9.0 %collective-permute-done.1.thin = f32[160,128]{1,0:T(8,128)S(1)} collective-permute-done((f32[160,128]{1,0:T(8,128)S(1)}, f32[160,128]{1,0:T(8,128)S(1)}, u32[]{:S(2)}, u32[]{:S(2)}) %collective-permute-start.1) | collective-permute-done | bytes 81952 | tf_op jit(solution)/shard_map/ppermute | solution.py:509
  33.4 0.0 collective-permute-done.wide
  33.4 1.8 %shard_map.61 = (f32[9,16,8,128]{3,2,1,0:T(8,128)S(1)}, f32[9,7,8,128]{3,2,1,0:T(8,128)S(1)}, f32[9,7,8,128]{3,2,1,0:T(8,128)S(1)}) custom-call(f32[576,128]{1,0:T(8,128)S(1)} %bitcast.7, f32[448,128]{1,0:T(8,128)S(1)} %collective-permute-done.wide, f32[160,128]{1,0:T(8,128)S(1)} %collective-permute-done.1.thin), custom_call_target="tpu_custom_call" | custom-call | tf_op jit(solution)/shard_map/pallas_call | solution.py:515
  35.1 6.1 %collective-permute-start.2 = (f32[9,7,8,128]{3,2,1,0:T(8,128)S(1)}, f32[9,7,8,128]{3,2,1,0:T(8,128)S(1)}, u32[]{:S(2)}, u32[]{:S(2)}) collective-permute-start(f32[9,7,8,128]{3,2,1,0:T(8,128)S(1)} %get-tuple-element.12), channel_id=1, source_target_pairs={{0,64},{64,128},{128,192},{192,256},{256,320},{320,384},{384,448},... | collective-permute-start | bytes 774152 | tf_op jit(solution)/shard_map/ppermute | solution.py:529
  41.2 1.9 %collective-permute-start.3 = (f32[9,7,8,128]{3,2,1,0:T(8,128)S(1)}, f32[9,7,8,128]{3,2,1,0:T(8,128)S(1)}, u32[]{:S(2)}, u32[]{:S(2)}) collective-permute-start(f32[9,7,8,128]{3,2,1,0:T(8,128)S(1)} %get-tuple-element.13), channel_id=1, source_target_pairs={{64,0},{128,64},{192,128},{256,192},{320,256},{384,320},{448,384},... | collective-permute-start | bytes 774152 | tf_op jit(solution)/shard_map/ppermute | solution.py:530
  43.2 1.3 %collective-permute-done.2.low = f32[9,7,8,128]{3,2,1,0:T(8,128)S(1)} collective-permute-done((f32[9,7,8,128]{3,2,1,0:T(8,128)S(1)}, f32[9,7,8,128]{3,2,1,0:T(8,128)S(1)}, u32[]{:S(2)}, u32[]{:S(2)}) %collective-permute-start.2) | collective-permute-done | bytes 258080 | tf_op jit(solution)/shard_map/ppermute | solution.py:529
  44.5 4.4 %collective-permute-done.3.high = f32[9,7,8,128]{3,2,1,0:T(8,128)S(1)} collective-permute-done((f32[9,7,8,128]{3,2,1,0:T(8,128)S(1)}, f32[9,7,8,128]{3,2,1,0:T(8,128)S(1)}, u32[]{:S(2)}, u32[]{:S(2)}) %collective-permute-start.3) | collective-permute-done | bytes 258080 | tf_op jit(solution)/shard_map/ppermute | solution.py:530
  48.9 7.0 %shard_map.62 = (f32[128,128]{1,0:T(8,128)S(1)}, f32[816,128]{1,0:T(8,128)S(1)}) custom-call(f32[9,16,8,128]{3,2,1,0:T(8,128)S(1)} %get-tuple-element.11.main, f32[9,7,8,128]{3,2,1,0:T(8,128)S(1)} %collective-permute-done.2.low, f32[9,7,8,128]{3,2,1,0:T(8,128)S(1)} %collective-permute-done.3.high), custom_call_target="tpu_custom_call" | custom-call | tf_op jit(solution)/shard_map/pallas_call | solution.py:532
  55.8 22.1 %all_to_all.16 = f32[64,2,128]{2,1,0:T(2,128)S(1)} all-to-all(f32[64,2,128]{2,1,0:T(2,128)S(1)} %bitcast.12), channel_id=1, replica_groups=mesh['gx'=8,'gy_0'=4,'gy_1'=2,'gz'=8] {'gy_0','gy_1','gz'}, dimensions={0} | all-to-all | bytes 131072 | tf_op jit(solution)/shard_map/all_to_all | solution.py:546
  78.0 17.9 %all_to_all.17 = f32[8,102,1,128]{3,2,1,0:T(1,128)S(1)} all-to-all(f32[8,102,1,128]{3,2,1,0:T(1,128)S(1)} %bitcast.8), channel_id=1, replica_groups=mesh['gx'=8,'gy_0'=4,'gy_1'=2,'gz'=8] {'gx'}, dimensions={0} | all-to-all | bytes 835584 | tf_op jit(solution)/shard_map/all_to_all | solution.py:550
  96.0 2.8 %shard_map.64 = (f32[2,4,8,128]{3,2,1,0:T(8,128)}, f32[2,4,8,128]{3,2,1,0:T(8,128)}) custom-call(f32[816,128]{1,0:T(8,128)S(1)} %bitcast.9), custom_call_target="tpu_custom_call" | custom-call | tf_op jit(solution)/shard_map/pallas_call | solution.py:551
  (2 shorter events, 0.1 us)
Async XLA Ops:
  22.3 11.0 %collective-permute-start = (f32[448,128]{1,0:T(8,128)S(1)}, f32[448,128]{1,0:T(8,128)S(1)}, u32[]{:S(2)}, u32[]{:S(2)}) collective-permute-start(f32[448,128]{1,0:T(8,128)S(1)} %get-tuple-element.9), channel_id=1, source_target_pairs={{8,16},{24,32},{40,48},{16,8},{32,24},{48,40},{9,17},{25,33},{41,4... | collective-permute-start | bytes 688136 | tf_op jit(solution)/shard_map/ppermute | solution.py:508
  23.0 10.3 %collective-permute-start.1 = (f32[160,128]{1,0:T(8,128)S(1)}, f32[160,128]{1,0:T(8,128)S(1)}, u32[]{:S(2)}, u32[]{:S(2)}) collective-permute-start(f32[160,128]{1,0:T(8,128)S(1)} %get-tuple-element.10), channel_id=1, source_target_pairs={{16,0},{32,16},{48,32},{8,24},{24,40},{40,56},{17,1},{33,17},{49,3... | collective-permute-start | bytes 245768 | tf_op jit(solution)/shard_map/ppermute | solution.py:509
  35.1 9.4 %collective-permute-start.2 = (f32[9,7,8,128]{3,2,1,0:T(8,128)S(1)}, f32[9,7,8,128]{3,2,1,0:T(8,128)S(1)}, u32[]{:S(2)}, u32[]{:S(2)}) collective-permute-start(f32[9,7,8,128]{3,2,1,0:T(8,128)S(1)} %get-tuple-element.12), channel_id=1, source_target_pairs={{0,64},{64,128},{128,192},{192,256},{256,320},{320,384},{384,448},... | collective-permute-start | bytes 774152 | tf_op jit(solution)/shard_map/ppermute | solution.py:529
  41.2 7.6 %collective-permute-start.3 = (f32[9,7,8,128]{3,2,1,0:T(8,128)S(1)}, f32[9,7,8,128]{3,2,1,0:T(8,128)S(1)}, u32[]{:S(2)}, u32[]{:S(2)}) collective-permute-start(f32[9,7,8,128]{3,2,1,0:T(8,128)S(1)} %get-tuple-element.13), channel_id=1, source_target_pairs={{64,0},{128,64},{192,128},{256,192},{320,256},{384,320},{448,384},... | collective-permute-start | bytes 774152 | tf_op jit(solution)/shard_map/ppermute | solution.py:530
